TPU v7x, 256 devices: a whole 4x4x8 slice. The times are simulated.
256 devices in a mesh: gx: 16 (over x, z_lo, core), gy: 16 (over z_hi, y).
Axes of the slice: x: 4, y: 4, z: 8 (z_hi: 4, z_lo: 2; z = z_hi * 2 + z_lo), core: 2. Of those that a mesh axis runs over, the one named last changes fastest.
Arguments:
- fine_source: bfloat16 [16, 16, 4, 8000], P('gx', 'gy'), may hold values from -6 to 6
- fine_blocks: bfloat16 [3, 12, 20, 20], replicated, may hold values from -0.5 to 0.5
- coarse_blocks: bfloat16 [3, 12, 20, 20], replicated, may hold values from -0.5 to 0.5
- child_filter_matrices: bfloat16 [2, 20, 20], replicated, may hold values from -1 to 1
Outputs:
- fine_result: float32 [16, 16, 4, 8000], P('gx', 'gy')
All inputs are finite; a program needn't handle non-finite values.
Results may differ from a plain program's by a relative error of at most 0.013.
Values may be sent and summed in bfloat16 or wider, within the bound.
No kernel may reach another device: no remote copies, remote signals or barrier semaphores. Data moves between devices by JAX's collectives and lax.ppermute only.
A program may use at most 64 MiB of HBM per device.

v0:
```python
import functools

import jax
import jax.numpy as jnp
from jax import lax
from jax.experimental import pallas as pl
from jax.experimental.pallas import tpu as pltpu
from jax.sharding import PartitionSpec as P

K2 = 20
TERMS = 12
BF = jnp.bfloat16
F32 = jnp.float32
ORDER = (1, 2, 0)
FINE_ROWS = 80
COARSE_ROWS = 48


def iota(shape, dim):
    return lax.broadcasted_iota(jnp.int32, shape, dim)


def dot(a, b):
    return jnp.dot(a, b, preferred_element_type=F32)


def place(n):
    block, t = n >> 7, n & 127
    first = (t * 205) >> 11
    return block, first, t - 10 * first, t < 100


def lane_constants(which):
    b, f, s, ok = place(iota((256, K2), 0))
    index = b * 10 + (f if which == 0 else s)
    spread_rows = jnp.where(ok & (index == iota((256, K2), 1)), 1.0, 0.0).astype(BF)
    b, f, s, ok = place(iota((K2, 256), 1))
    index = b * 10 + (f if which == 0 else s)
    spread_lanes = jnp.where(ok & (index == iota((K2, 256), 0)), 1.0, 0.0).astype(BF)
    _, f0, s0, ok0 = place(iota((256, 256), 0))
    _, f1, s1, ok1 = place(iota((256, 256), 1))
    same = (s0 == s1) if which == 0 else (f0 == f1)
    mask = jnp.where(same & ok0 & ok1, 1.0, 0.0)
    return spread_rows, spread_lanes, mask


def lane_matrix(transposed, constants):
    spread_rows, spread_lanes, mask = constants
    wide = dot(transposed, spread_lanes).astype(BF)
    return (dot(spread_rows, wide) * mask).astype(BF)


def row_constants(rows, nz, copies):
    shift = nz.bit_length() - 1
    r = iota((rows, K2), 0)
    spread_rows = jnp.where((r >> shift) == iota((rows, K2), 1), 1.0, 0.0).astype(BF)
    spreads = []
    for c in range(copies):
        col = iota((K2, copies * rows), 1) - c * rows
        here = (col >= 0) & (col < rows) & ((col >> shift) == iota((K2, copies * rows), 0))
        spreads.append(jnp.where(here, 1.0, 0.0).astype(BF))
    shape = (rows, copies * rows)
    col = iota(shape, 1)
    for c in range(1, copies):
        col = jnp.where(iota(shape, 1) >= c * rows, iota(shape, 1) - c * rows, col)
    mask = jnp.where((iota(shape, 0) & (nz - 1)) == (col & (nz - 1)), 1.0, 0.0)
    return spread_rows, spreads, mask


def flipped(matrix):
    return matrix.astype(F32).T.astype(BF)


def build_kernel(fine_ref, coarse_ref, child_ref, *outs):
    (fine_rows, fine_y, fine_z, coarse_rows, coarse_y, coarse_z,
     down_rows, down_y, down_z, up_rows, up_y, up_z) = outs
    on_first, on_second = lane_constants(0), lane_constants(1)
    levels = (
        (fine_ref, fine_rows, fine_y, fine_z, FINE_ROWS, 4),
        (coarse_ref, coarse_rows, coarse_y, coarse_z, COARSE_ROWS, 2),
    )
    for blocks, rows_out, y_out, z_out, rows, nz in levels:
        spread_rows, spreads, mask = row_constants(rows, nz, 3)

        def term(m, carry, blocks=blocks, rows_out=rows_out, y_out=y_out, z_out=z_out, rows=rows,
                 spread_rows=spread_rows, spreads=spreads, mask=mask):
            wide = jnp.zeros((K2, 3 * rows), F32)
            for n, d in enumerate(ORDER):
                matrix = blocks[d, m]
                wide = wide + dot(matrix, spreads[n])
                transposed = flipped(matrix)
                y_out[m, pl.ds(n * 256, 256), :] = lane_matrix(transposed, on_first)
                z_out[n, m] = lane_matrix(transposed, on_second)
            rows_out[m] = (dot(spread_rows, wide.astype(BF)) * mask).astype(BF)
            return carry

        lax.fori_loop(0, TERMS, term, 0, unroll=2)

    px, py = lax.axis_index("gx") & 1, lax.axis_index("gy") & 1
    own_x, other_x, own_y, other_y = child_ref[px], child_ref[1 - px], child_ref[py], child_ref[1 - py]
    down_y[0] = lane_matrix(flipped(own_y), on_first)
    down_y[1] = lane_matrix(flipped(other_y), on_first)
    up_y[...] = lane_matrix(own_y, on_first)
    for c in range(2):
        down_z[c] = lane_matrix(flipped(child_ref[c]), on_second)
        up_z[c] = lane_matrix(child_ref[c], on_second)
    _, spreads, _ = row_constants(FINE_ROWS, 4, 2)
    wide = (dot(own_x, spreads[0]) + dot(other_x, spreads[1])).astype(BF)
    r = iota((2 * COARSE_ROWS, K2), 0)
    r = jnp.where(r >= COARSE_ROWS, r - COARSE_ROWS, r)
    spread_rows = jnp.where((r >> 1) == iota((2 * COARSE_ROWS, K2), 1), 1.0, 0.0).astype(BF)
    shape = (2 * COARSE_ROWS, 2 * FINE_ROWS)
    r = iota(shape, 0)
    cz = jnp.where(r >= COARSE_ROWS, 1, 0)
    keep = (2 * (r & 1) + cz) == (iota(shape, 1) & 3)
    down_rows[...] = (dot(spread_rows, wide) * jnp.where(keep, 1.0, 0.0)).astype(BF)
    shape = (K2, COARSE_ROWS)
    spread = jnp.where((iota(shape, 1) >> 1) == iota(shape, 0), 1.0, 0.0).astype(BF)
    wide = dot(flipped(own_x), spread).astype(BF)
    shape = (FINE_ROWS, K2)
    spread_rows = jnp.where((iota(shape, 0) >> 2) == iota(shape, 1), 1.0, 0.0).astype(BF)
    shape = (FINE_ROWS, COARSE_ROWS)
    keep = ((iota(shape, 0) & 3) >> 1) == (iota(shape, 1) & 1)
    up_rows[...] = (dot(spread_rows, wide) * jnp.where(keep, 1.0, 0.0)).astype(BF)


def build(fine_blocks, coarse_blocks, child):
    def s(*shape):
        return jax.ShapeDtypeStruct(shape, BF)

    out_shape = (
        s(TERMS, FINE_ROWS, 3 * FINE_ROWS), s(TERMS, 768, 256), s(3, TERMS, 256, 256),
        s(TERMS, COARSE_ROWS, 3 * COARSE_ROWS), s(TERMS, 768, 256), s(3, TERMS, 256, 256),
        s(2 * COARSE_ROWS, 2 * FINE_ROWS), s(2, 256, 256), s(2, 256, 256),
        s(FINE_ROWS, COARSE_ROWS), s(256, 256), s(2, 256, 256),
    )
    return pl.pallas_call(
        build_kernel, out_shape=out_shape, name="build",
        compiler_params=pltpu.CompilerParams(vmem_limit_bytes=32 << 20),
        cost_estimate=pl.CostEstimate(flops=8 * 10**9, bytes_accessed=20 * 10**6, transcendentals=0),
    )(fine_blocks, coarse_blocks, child)


def source_kernel(own, xup, xlow, yup, ylow, corner, down_rows, down_y, down_z,
                  along_x, along_y, parent, natural, pair_low, pair_high, mixed, turned):
    shape = (400, 512)
    n, lane = iota(shape, 0), iota(shape, 1)
    j = (n * 205) >> 12
    k = n - 20 * j
    g, rest = lane >> 8, lane & 255
    h, jj, kk, ok = place(rest)
    select = jnp.where(ok & (j == 10 * h + jj) & (k == 10 * g + kk), 1.0, 0.0).astype(BF)

    def converted(ref, slot):
        values = ref[0, 0].astype(F32)
        for i in range(K2):
            natural[slot, 4 * i:4 * i + 4, :] = values[:, 400 * i:400 * i + 400]
        return dot(natural[slot].astype(BF), select)

    centre = converted(own, 0).astype(BF)
    x_up, x_low = converted(xup, 1), converted(xlow, 2)
    y_up, y_low = converted(yup, 3), converted(ylow, 4)
    diagonal = converted(corner, 5).astype(BF)
    along_x[0:80, :] = centre
    along_x[80:160, :] = x_up.astype(BF)
    along_x[160:240, :] = x_low.astype(BF)
    along_y[:, 0:512] = centre
    along_y[:, 512:1024] = y_up.astype(BF)
    along_y[:, 1024:1536] = y_low.astype(BF)
    px, py = lax.axis_index("gx") & 1, lax.axis_index("gy") & 1
    pair_low[0:80, :] = centre
    pair_low[80:160, :] = jnp.where(px == 0, x_up, x_low).astype(BF)
    pair_high[0:80, :] = jnp.where(py == 0, y_up, y_low).astype(BF)
    pair_high[80:160, :] = diagonal
    for c, pair in enumerate((pair_low, pair_high)):
        rows = dot(down_rows[...], pair[...]).astype(BF)
        for g in range(2):
            mixed[c, 96 * g:96 * g + 96, :] = rows[:, 256 * g:256 * g + 256]
    summed = dot(mixed[0], down_y[0]) + dot(mixed[1], down_y[1])
    summed = summed.astype(BF)
    for c in range(2):
        for g in range(2):
            for h in range(2):
                turned[c, 48 * h:48 * h + 48, 128 * g:128 * g + 128] = (
                    summed[96 * g + 48 * c:96 * g + 48 * c + 48, 128 * h:128 * h + 128]
                )
    total = (dot(turned[0], down_z[0]) + dot(turned[1], down_z[1])).astype(BF)
    for g in range(2):
        for h in range(2):
            parent[:, 256 * g + 128 * h:256 * g + 128 * h + 128] = (
                total[48 * h:48 * h + 48, 128 * g:128 * g + 128]
            )


def source(columns, down_rows, down_y, down_z):
    out_shape = (
        jax.ShapeDtypeStruct((3 * FINE_ROWS, 512), BF),
        jax.ShapeDtypeStruct((FINE_ROWS, 1536), BF),
        jax.ShapeDtypeStruct((COARSE_ROWS, 512), BF),
    )
    scratch = [
        pltpu.VMEM((6, FINE_ROWS, 400), F32),
        pltpu.VMEM((2 * FINE_ROWS, 512), BF),
        pltpu.VMEM((2 * FINE_ROWS, 512), BF),
        pltpu.VMEM((2, 4 * COARSE_ROWS, 256), BF),
        pltpu.VMEM((2, 2 * COARSE_ROWS, 256), BF),
    ]
    return pl.pallas_call(
        source_kernel, out_shape=out_shape, scratch_shapes=scratch, name="source",
        compiler_params=pltpu.CompilerParams(vmem_limit_bytes=16 << 20),
        cost_estimate=pl.CostEstimate(flops=10**9, bytes_accessed=10**6, transcendentals=0),
    )(*columns, down_rows, down_y, down_z)


def level(rows, nz, along_x, along_y, row_mats, y_mats, z_mats, first, plain, sums, centres):
    for m in range(TERMS):
        both = dot(row_mats[m], along_x)
        sides = dot(row_mats[m][:, 0:rows], along_y)
        for g in range(2):
            here = pl.ds(g * rows, rows)
            first[m, here, 0:256] = both[:, 256 * g:256 * g + 256].astype(BF)
            first[m, here, 256:512] = sides[:, 512 + 256 * g:768 + 256 * g].astype(BF)
            first[m, here, 512:768] = sides[:, 1024 + 256 * g:1280 + 256 * g].astype(BF)
            plain[m, here, :] = sides[:, 256 * g:256 * g + 256].astype(BF)
    for m in range(TERMS):
        summed = dot(first[m], y_mats[m]).astype(BF)
        centre = dot(plain[m], y_mats[m, 0:256, :]).astype(BF)
        for g in range(2):
            for h in range(2):
                here = pl.ds(h * rows, rows)
                lanes = pl.ds(m * 256 + g * 128, 128)
                sums[here, lanes] = summed[g * rows:(g + 1) * rows, 128 * h:128 * h + 128]
                centres[here, lanes] = centre[g * rows:(g + 1) * rows, 128 * h:128 * h + 128]
    total = dot(sums[...], z_mats[0].reshape(TERMS * 256, 256))
    upper = dot(centres[...], z_mats[1].reshape(TERMS * 256, 256))
    lower = dot(centres[...], z_mats[2].reshape(TERMS * 256, 256))
    z = iota((2 * rows, 256), 0) & (nz - 1)
    total = total + jnp.where(z == nz - 1, 0.0, pltpu.roll(upper, 2 * rows - 1, 0))
    return total + jnp.where(z == 0, 0.0, pltpu.roll(lower, 1, 0))


def level_scratch(rows):
    return [
        pltpu.VMEM((TERMS, 2 * rows, 768), BF),
        pltpu.VMEM((TERMS, 2 * rows, 256), BF),
        pltpu.VMEM((2 * rows, TERMS * 256), BF),
        pltpu.VMEM((2 * rows, TERMS * 256), BF),
    ]


def fine_kernel(along_x, along_y, row_mats, y_mats, z_mats, out, *scratch):
    out[...] = level(FINE_ROWS, 4, along_x[...], along_y[...], row_mats, y_mats, z_mats, *scratch)


def fine(along_x, along_y, row_mats, y_mats, z_mats):
    return pl.pallas_call(
        fine_kernel, out_shape=jax.ShapeDtypeStruct((2 * FINE_ROWS, 256), F32),
        scratch_shapes=level_scratch(FINE_ROWS), name="fine",
        compiler_params=pltpu.CompilerParams(vmem_limit_bytes=32 << 20),
        cost_estimate=pl.CostEstimate(flops=6 * 10**9, bytes_accessed=10 * 10**6, transcendentals=0),
    )(along_x, along_y, row_mats, y_mats, z_mats)


def coarse_kernel(own, xup, xlow, yup, ylow, row_mats, y_mats, z_mats, up_rows, up_y, up_z, fine_term,
                  out, along_x, along_y, grown, turned, *scratch):
    along_x[0:48, :] = own[...]
    along_x[48:96, :] = xup[...]
    along_x[96:144, :] = xlow[...]
    along_y[:, 0:512] = own[...]
    along_y[:, 512:1024] = yup[...]
    along_y[:, 1024:1536] = ylow[...]
    result = level(COARSE_ROWS, 2, along_x[...], along_y[...], row_mats, y_mats, z_mats, *scratch).astype(BF)
    for h in range(2):
        part = dot(up_rows[...], result[48 * h:48 * h + 48, :]).astype(BF)
        for g in range(2):
            grown[80 * g:80 * g + 80, 128 * h:128 * h + 128] = part[:, 128 * g:128 * g + 128]
    part = dot(grown[...], up_y[...]).astype(BF)
    for h in range(2):
        for g in range(2):
            turned[80 * h:80 * h + 80, 128 * g:128 * g + 128] = part[80 * g:80 * g + 80, 128 * h:128 * h + 128]
    even = dot(turned[...], up_z[0])
    odd = dot(turned[...], up_z[1])
    expanded = jnp.where((iota((160, 256), 0) & 1) == 0, even, odd)
    total = fine_term[...] + expanded
    high = total.astype(BF)
    low = (total - high.astype(F32)).astype(BF)
    natural = jnp.zeros((80, 400), F32)
    for h in range(2):
        shape = (256, 400)
        g, jj, kk, ok = place(iota(shape, 0))
        n = iota(shape, 1)
        select = jnp.where(ok & (n == (10 * h + jj) * 20 + 10 * g + kk), 1.0, 0.0).astype(BF)
        natural = natural + dot(high[80 * h:80 * h + 80, :], select) + dot(low[80 * h:80 * h + 80, :], select)
    for i in range(K2):
        out[0, 0, :, 400 * i:400 * i + 400] = natural[4 * i:4 * i + 4, :]


def coarse(parents, row_mats, y_mats, z_mats, up_rows, up_y, up_z, fine_term):
    scratch = [
        pltpu.VMEM((3 * COARSE_ROWS, 512), BF),
        pltpu.VMEM((COARSE_ROWS, 1536), BF),
        pltpu.VMEM((160, 256), BF),
        pltpu.VMEM((160, 256), BF),
    ] + level_scratch(COARSE_ROWS)
    return pl.pallas_call(
        coarse_kernel, out_shape=jax.ShapeDtypeStruct((1, 1, 4, 8000), F32),
        scratch_shapes=scratch, name="coarse",
        compiler_params=pltpu.CompilerParams(vmem_limit_bytes=32 << 20),
        cost_estimate=pl.CostEstimate(flops=4 * 10**9, bytes_accessed=10 * 10**6, transcendentals=0),
    )(*parents, row_mats, y_mats, z_mats, up_rows, up_y, up_z, fine_term)


def moved(block, axis, distance):
    count = lax.axis_size(axis)
    route = [(i + distance, i) for i in range(count) if 0 <= i + distance < count]
    return lax.ppermute(block, axis, route)


def corner(block):
    nx, ny = lax.axis_size("gx"), lax.axis_size("gy")
    route = [(x * ny + y, (x ^ 1) * ny + (y ^ 1)) for x in range(nx) for y in range(ny)]
    return lax.ppermute(block, ("gx", "gy"), route)


def shards(fine_source, fine_blocks, coarse_blocks, child_filter_matrices):
    columns = [fine_source, moved(fine_source, "gx", 1), moved(fine_source, "gx", -1),
               moved(fine_source, "gy", 1), moved(fine_source, "gy", -1), corner(fine_source)]
    built = build(fine_blocks, coarse_blocks, child_filter_matrices)
    along_x, along_y, parent = source(columns, *built[6:9])
    parents = [parent, moved(parent, "gx", 2), moved(parent, "gx", -2),
               moved(parent, "gy", 2), moved(parent, "gy", -2)]
    fine_term = fine(along_x, along_y, *built[0:3])
    return coarse(parents, *built[3:6], *built[9:12], fine_term)


def solution(mesh):
    in_specs = (P("gx", "gy", None, None), P(), P(), P())
    out_specs = P("gx", "gy", None, None)
    return jax.shard_map(shards, mesh=mesh, in_specs=in_specs, out_specs=out_specs, check_vma=False)
```

profile of v0, /device:TPU:130, one launch (start us, length us, event | category | flops | bytes accessed | tf_op | source)
XLA Modules:
  0.0 64.4 jit_solution(9383929722464934223)
XLA Ops:
  0.0 3.5 %collective-permute-start.3 = (bf16[1,1,4,8000]{3,2,1,0:T(4,128)(2,1)}, bf16[1,1,4,8000]{3,2,1,0:T(4,128)(2,1)S(1)}, u32[]{:S(2)}, u32[]{:S(2)}) collective-permute-start(bf16[1,1,4,8000]{3,2,1,0:T(4,128)(2,1)} %own.1), channel_id=1, source_target_pairs={{0,1},{1,2},{2,3},{3,4},{4,5},{5,6},{6,7},{7,8},{8,9},{9,10},{10,1... | collective-permute-start | bytes 192008 | tf_op jit(solution)/shard_map/ppermute | solution.py:316
  3.5 6.6 %collective-permute-start.2 = (bf16[1,1,4,8000]{3,2,1,0:T(4,128)(2,1)}, bf16[1,1,4,8000]{3,2,1,0:T(4,128)(2,1)S(1)}, u32[]{:S(2)}, u32[]{:S(2)}) collective-permute-start(bf16[1,1,4,8000]{3,2,1,0:T(4,128)(2,1)} %own.1), channel_id=1, source_target_pairs={{1,0},{2,1},{3,2},{4,3},{5,4},{6,5},{7,6},{8,7},{9,8},{10,9},{11,1... | collective-permute-start | bytes 192008 | tf_op jit(solution)/shard_map/ppermute | solution.py:316
  10.1 1.9 %collective-permute-start.1 = (bf16[1,1,4,8000]{3,2,1,0:T(4,128)(2,1)}, bf16[1,1,4,8000]{3,2,1,0:T(4,128)(2,1)S(1)}, u32[]{:S(2)}, u32[]{:S(2)}) collective-permute-start(bf16[1,1,4,8000]{3,2,1,0:T(4,128)(2,1)} %own.1), channel_id=1, source_target_pairs={{0,16},{16,32},{32,48},{48,64},{64,80},{80,96},{96,112},{112,128},... | collective-permute-start | bytes 192008 | tf_op jit(solution)/shard_map/ppermute | solution.py:316
  12.0 4.5 %collective-permute-start = (bf16[1,1,4,8000]{3,2,1,0:T(4,128)(2,1)}, bf16[1,1,4,8000]{3,2,1,0:T(4,128)(2,1)S(1)}, u32[]{:S(2)}, u32[]{:S(2)}) collective-permute-start(bf16[1,1,4,8000]{3,2,1,0:T(4,128)(2,1)} %own.1), channel_id=1, source_target_pairs={{16,0},{32,16},{48,32},{64,48},{80,64},{96,80},{112,96},{128,112},... | collective-permute-start | bytes 192008 | tf_op jit(solution)/shard_map/ppermute | solution.py:316
  16.6 0.1 collective-permute-start.4
  16.7 0.7 %copy.5.child_ref = bf16[2,20,20]{2,1,0:T(8,128)(2,1)S(1)} copy(bf16[2,20,20]{2,0,1:T(2,128)(2,1)} %param.7) | data formatting | bytes 3200 | tf_op args[3]
  17.4 0.9 %copy-done = bf16[3,12,20,20]{3,2,1,0:T(8,128)(2,1)S(1)} copy-done((bf16[3,12,20,20]{3,2,1,0:T(8,128)(2,1)S(1)}, bf16[3,12,20,20]{3,2,1,0:T(8,128)(2,1)}, u32[]{:S(2)}) %copy-start) | copy-done | bytes 28824
  18.3 0.9 %copy-done.1 = bf16[3,12,20,20]{3,2,1,0:T(8,128)(2,1)S(1)} copy-done((bf16[3,12,20,20]{3,2,1,0:T(8,128)(2,1)S(1)}, bf16[3,12,20,20]{3,2,1,0:T(8,128)(2,1)}, u32[]{:S(2)}) %copy-start.1) | copy-done | bytes 28824
  19.2 18.9 %build.1 = (bf16[12,80,240]{2,1,0:T(8,128)(2,1)S(1)}, bf16[12,768,256]{2,1,0:T(8,128)(2,1)S(1)}, bf16[3,12,256,256]{3,2,1,0:T(8,128)(2,1)S(1)}, bf16[12,48,144]{...) custom-call(bf16[3,12,20,20]{3,2,1,0:T(8,128)(2,1)S(1)} %copy-done, ...), custom_call_target="tpu_custom_call" | custom-call | flops 8000000000 | bytes 20000000 | tf_op jit(solution)/shard_map/build/pallas_call | solution.py:137
  38.1 0.0 collective-permute-done.3.ylow
  38.2 0.0 collective-permute-done.2.yup
  38.2 0.0 collective-permute-done.1.xlow
  38.2 0.0 collective-permute-done.xup
  38.2 0.0 collective-permute-done.4.corner
  38.2 1.3 %source.1 = (bf16[240,512]{1,0:T(8,128)(2,1)S(1)}, bf16[80,1536]{1,0:T(8,128)(2,1)S(1)}, bf16[48,512]{1,0:T(8,128)(2,1)S(1)}) custom-call(bf16[1,1,4,8000]{3,2,1,0:T(4,128)(2,1)S(1)} %copy-done.2, bf16[1,1,4,8000]{3,2,1,0:T(4,128)(2,1)S(1)} %collective-permute-done.xup, bf16[1,1,4,8000]{3,2,1,0:T(4,128)(2,1)S(1)} %collective-permute-done.1.xlow, ...), custom_call_target="tpu_custom_call" | custom-call | flops 1000000000 | bytes 1000000 | tf_op jit(solution)/shard_map/source/pallas_call | solution.py:208
  39.5 1.9 %collective-permute-start.8 = (bf16[48,512]{1,0:T(8,128)(2,1)S(1)}, bf16[48,512]{1,0:T(8,128)(2,1)S(1)}, u32[]{:S(2)}, u32[]{:S(2)}) collective-permute-start(bf16[48,512]{1,0:T(8,128)(2,1)S(1)} %get-tuple-element.23.own), channel_id=1, source_target_pairs={{0,2},{1,3},{2,4},{3,5},{4,6},{5,7},{6,8},{7,9},{8,10},{9,11},{10,... | collective-permute-start | bytes 147464 | tf_op jit(solution)/shard_map/ppermute | solution.py:316
  41.4 8.4 %collective-permute-start.7 = (bf16[48,512]{1,0:T(8,128)(2,1)S(1)}, bf16[48,512]{1,0:T(8,128)(2,1)S(1)}, u32[]{:S(2)}, u32[]{:S(2)}) collective-permute-start(bf16[48,512]{1,0:T(8,128)(2,1)S(1)} %get-tuple-element.23.own), channel_id=1, source_target_pairs={{2,0},{3,1},{4,2},{5,3},{6,4},{7,5},{8,6},{9,7},{10,8},{11,9},{12,... | collective-permute-start | bytes 147464 | tf_op jit(solution)/shard_map/ppermute | solution.py:316
  49.9 2.0 %collective-permute-start.6 = (bf16[48,512]{1,0:T(8,128)(2,1)S(1)}, bf16[48,512]{1,0:T(8,128)(2,1)S(1)}, u32[]{:S(2)}, u32[]{:S(2)}) collective-permute-start(bf16[48,512]{1,0:T(8,128)(2,1)S(1)} %get-tuple-element.23.own), channel_id=1, source_target_pairs={{0,32},{16,48},{32,64},{48,80},{64,96},{80,112},{96,128},{112,144}... | collective-permute-start | bytes 147464 | tf_op jit(solution)/shard_map/ppermute | solution.py:316
  51.9 4.7 %collective-permute-start.5 = (bf16[48,512]{1,0:T(8,128)(2,1)S(1)}, bf16[48,512]{1,0:T(8,128)(2,1)S(1)}, u32[]{:S(2)}, u32[]{:S(2)}) collective-permute-start(bf16[48,512]{1,0:T(8,128)(2,1)S(1)} %get-tuple-element.23.own), channel_id=1, source_target_pairs={{32,0},{48,16},{64,32},{80,48},{96,64},{112,80},{128,96},{144,112}... | collective-permute-start | bytes 147464 | tf_op jit(solution)/shard_map/ppermute | solution.py:316
  56.6 3.3 %fine.1.fine_term = f32[160,256]{1,0:T(8,128)S(1)} custom-call(bf16[240,512]{1,0:T(8,128)(2,1)S(1)} %get-tuple-element.30.along_x, bf16[80,1536]{1,0:T(8,128)(2,1)S(1)} %get-tuple-element.31.along_y, bf16[12,80,240]{2,1,0:T(8,128)(2,1)S(1)} %get-tuple-element.32.row_mats, bf16[12,768,256]{2,1,0:T(8,128)(2,1)S(1)} %get-tuple-element.33.y_mats, ...), custom_call_target="tpu_custom_call" | custom-call | flops 6000000000 | bytes 10000000 | tf_op jit(solution)/shard_map/fine/pallas_call | solution.py:256
  59.9 0.0 collective-permute-done.8.ylow
  59.9 0.0 collective-permute-done.7.yup
  59.9 0.0 collective-permute-done.5.xup
  59.9 4.4 %coarse.1 = f32[1,1,4,8000]{3,2,1,0:T(4,128)} custom-call(bf16[48,512]{1,0:T(8,128)(2,1)S(1)} %get-tuple-element.23.own, bf16[48,512]{1,0:T(8,128)(2,1)S(1)} %collective-permute-done.5.xup, bf16[48,512]{1,0:T(8,128)(2,1)S(1)} %collective-permute-done.6.xlow, bf16[48,512]{1,0:T(8,128)(2,1)S(1)} %collective-permute-done.7.yup, ...), custom_call_target="tpu_custom_call" | custom-call | flops 4000000000 | bytes 10000000 | tf_op jit(solution)/shard_map/coarse/pallas_call | solution.py:305
  (5 shorter events, 0.0 us)
Async XLA Ops:
  0.0 38.1 %collective-permute-start.3 = (bf16[1,1,4,8000]{3,2,1,0:T(4,128)(2,1)}, bf16[1,1,4,8000]{3,2,1,0:T(4,128)(2,1)S(1)}, u32[]{:S(2)}, u32[]{:S(2)}) collective-permute-start(bf16[1,1,4,8000]{3,2,1,0:T(4,128)(2,1)} %own.1), channel_id=1, source_target_pairs={{0,1},{1,2},{2,3},{3,4},{4,5},{5,6},{6,7},{7,8},{8,9},{9,10},{10,1... | collective-permute-start | bytes 192008 | tf_op jit(solution)/shard_map/ppermute | solution.py:316
  3.5 34.7 %collective-permute-start.2 = (bf16[1,1,4,8000]{3,2,1,0:T(4,128)(2,1)}, bf16[1,1,4,8000]{3,2,1,0:T(4,128)(2,1)S(1)}, u32[]{:S(2)}, u32[]{:S(2)}) collective-permute-start(bf16[1,1,4,8000]{3,2,1,0:T(4,128)(2,1)} %own.1), channel_id=1, source_target_pairs={{1,0},{2,1},{3,2},{4,3},{5,4},{6,5},{7,6},{8,7},{9,8},{10,9},{11,1... | collective-permute-start | bytes 192008 | tf_op jit(solution)/shard_map/ppermute | solution.py:316
  10.1 28.1 %collective-permute-start.1 = (bf16[1,1,4,8000]{3,2,1,0:T(4,128)(2,1)}, bf16[1,1,4,8000]{3,2,1,0:T(4,128)(2,1)S(1)}, u32[]{:S(2)}, u32[]{:S(2)}) collective-permute-start(bf16[1,1,4,8000]{3,2,1,0:T(4,128)(2,1)} %own.1), channel_id=1, source_target_pairs={{0,16},{16,32},{32,48},{48,64},{64,80},{80,96},{96,112},{112,128},... | collective-permute-start | bytes 192008 | tf_op jit(solution)/shard_map/ppermute | solution.py:316
  12.0 26.2 %collective-permute-start = (bf16[1,1,4,8000]{3,2,1,0:T(4,128)(2,1)}, bf16[1,1,4,8000]{3,2,1,0:T(4,128)(2,1)S(1)}, u32[]{:S(2)}, u32[]{:S(2)}) collective-permute-start(bf16[1,1,4,8000]{3,2,1,0:T(4,128)(2,1)} %own.1), channel_id=1, source_target_pairs={{16,0},{32,16},{48,32},{64,48},{80,64},{96,80},{112,96},{128,112},... | collective-permute-start | bytes 192008 | tf_op jit(solution)/shard_map/ppermute | solution.py:316
  16.6 21.6 %collective-permute-start.4 = (bf16[1,1,4,8000]{3,2,1,0:T(4,128)(2,1)}, bf16[1,1,4,8000]{3,2,1,0:T(4,128)(2,1)S(1)}, u32[]{:S(2)}, u32[]{:S(2)}) collective-permute-start(bf16[1,1,4,8000]{3,2,1,0:T(4,128)(2,1)} %own.1), channel_id=1, source_target_pairs={{0,17},{1,16},{2,19},{3,18},{4,21},{5,20},{6,23},{7,22},{8,25},{9,... | collective-permute-start | bytes 192008 | tf_op jit(solution)/shard_map/ppermute | solution.py:322
  17.4 0.9 %copy-start = (bf16[3,12,20,20]{3,2,1,0:T(8,128)(2,1)S(1)}, bf16[3,12,20,20]{3,2,1,0:T(8,128)(2,1)}, u32[]{:S(2)}) copy-start(bf16[3,12,20,20]{3,2,1,0:T(8,128)(2,1)} %fine_ref.1) | copy-start | bytes 86404
  18.3 0.9 %copy-start.1 = (bf16[3,12,20,20]{3,2,1,0:T(8,128)(2,1)S(1)}, bf16[3,12,20,20]{3,2,1,0:T(8,128)(2,1)}, u32[]{:S(2)}) copy-start(bf16[3,12,20,20]{3,2,1,0:T(8,128)(2,1)} %coarse_ref.1) | copy-start | bytes 86404
  19.2 19.0 %copy-start.2 = (bf16[1,1,4,8000]{3,2,1,0:T(4,128)(2,1)S(1)}, bf16[1,1,4,8000]{3,2,1,0:T(4,128)(2,1)}, u32[]{:S(2)}) copy-start(bf16[1,1,4,8000]{3,2,1,0:T(4,128)(2,1)} %own.1) | copy-start | bytes 192004
  39.5 20.4 %collective-permute-start.8 = (bf16[48,512]{1,0:T(8,128)(2,1)S(1)}, bf16[48,512]{1,0:T(8,128)(2,1)S(1)}, u32[]{:S(2)}, u32[]{:S(2)}) collective-permute-start(bf16[48,512]{1,0:T(8,128)(2,1)S(1)} %get-tuple-element.23.own), channel_id=1, source_target_pairs={{0,2},{1,3},{2,4},{3,5},{4,6},{5,7},{6,8},{7,9},{8,10},{9,11},{10,... | collective-permute-start | bytes 147464 | tf_op jit(solution)/shard_map/ppermute | solution.py:316
  41.4 18.5 %collective-permute-start.7 = (bf16[48,512]{1,0:T(8,128)(2,1)S(1)}, bf16[48,512]{1,0:T(8,128)(2,1)S(1)}, u32[]{:S(2)}, u32[]{:S(2)}) collective-permute-start(bf16[48,512]{1,0:T(8,128)(2,1)S(1)} %get-tuple-element.23.own), channel_id=1, source_target_pairs={{2,0},{3,1},{4,2},{5,3},{6,4},{7,5},{8,6},{9,7},{10,8},{11,9},{12,... | collective-permute-start | bytes 147464 | tf_op jit(solution)/shard_map/ppermute | solution.py:316
  49.9 10.0 %collective-permute-start.6 = (bf16[48,512]{1,0:T(8,128)(2,1)S(1)}, bf16[48,512]{1,0:T(8,128)(2,1)S(1)}, u32[]{:S(2)}, u32[]{:S(2)}) collective-permute-start(bf16[48,512]{1,0:T(8,128)(2,1)S(1)} %get-tuple-element.23.own), channel_id=1, source_target_pairs={{0,32},{16,48},{32,64},{48,80},{64,96},{80,112},{96,128},{112,144}... | collective-permute-start | bytes 147464 | tf_op jit(solution)/shard_map/ppermute | solution.py:316
  51.9 8.0 %collective-permute-start.5 = (bf16[48,512]{1,0:T(8,128)(2,1)S(1)}, bf16[48,512]{1,0:T(8,128)(2,1)S(1)}, u32[]{:S(2)}, u32[]{:S(2)}) collective-permute-start(bf16[48,512]{1,0:T(8,128)(2,1)S(1)} %get-tuple-element.23.own), channel_id=1, source_target_pairs={{32,0},{48,16},{64,32},{80,48},{96,64},{112,80},{128,96},{144,112}... | collective-permute-start | bytes 147464 | tf_op jit(solution)/shard_map/ppermute | solution.py:316
where the time goes:
time: 65.5 us; the launch traced here: 64.4 us
  starting transfers between devices  33.7 us (51%)
  Pallas kernels  27.9 us (43%)
  local copies, waits for them, and re-layouts  2.58 us (4%)
    ppermute x8, starting transfers between devices, moved(): return lax.ppermute(block, axis, route)  33.6 us
    pallas_call x1, Pallas kernels, build(): pl.pallas_call(build_kernel, out_shape=out_shape, name='build', compiler_...  18.9 us
    pallas_call x1, Pallas kernels, coarse(): pl.pallas_call(coarse_kernel, out_shape=jax.ShapeDtypeStruct((1, 1, 4, 80...  4.45 us
    pallas_call x1, Pallas kernels, fine(): pl.pallas_call(fine_kernel, out_shape=jax.ShapeDtypeStruct((2 * FINE_ROWS...  3.26 us
    unnamed x7, local copies, waits for them, and re-layouts  2.58 us
  transfers between devices with their start and end apart: 9, of which 0 were waited for; matrix products, arithmetic and copies ran while one was open for 1% of the time, Pallas kernels for 34%

commit v1 on v0

v1 whole, which is shorter than its diff:
```python
import jax
import jax.numpy as jnp
from jax import lax
from jax.experimental import pallas as pl
from jax.experimental.pallas import tpu as pltpu
from jax.sharding import PartitionSpec as P

K2 = 20
TERMS = 12
BF = jnp.bfloat16
F32 = jnp.float32
FINE_ROWS = 80
COARSE_ROWS = 48


def iota(shape, dim):
    return lax.broadcasted_iota(jnp.int32, shape, dim)


def dot(a, b):
    return jnp.dot(a, b, preferred_element_type=F32)


def place(n):
    piece, t = n >> 5, n & 31
    jj = (t * 13) >> 6
    return piece, jj, t - 5 * jj, t < 25


def natural_place(n, y_order):
    block = n >> 7
    piece, jj, kk, ok = place(n & 127)
    j, k = (piece, block) if y_order else (block, piece)
    return jnp.where(ok, (5 * j + jj) * 20 + 5 * k + kk, -1)


def onehot(condition, dtype=BF):
    return jnp.where(condition, 1.0, 0.0).astype(dtype)


def lane_constants(on_j):
    def index(n):
        piece, jj, kk, ok = place(n)
        return jnp.where(ok, piece * 5 + (jj if on_j else kk), -1)

    def fixed(n, none):
        _, jj, kk, ok = place(n)
        return jnp.where(ok, kk if on_j else jj, none)

    spread_rows = onehot(index(iota((128, 1), 0)) == iota((128, K2), 1))
    spread_lanes = onehot(index(iota((1, 128), 1)) == iota((K2, 128), 0))
    mask = onehot(fixed(iota((128, 1), 0), -1) == fixed(iota((1, 128), 1), -2), F32)
    return spread_rows, spread_lanes, mask


def row_constants(rows, nz):
    shift = nz.bit_length() - 1
    spread_rows = onehot((iota((rows, 1), 0) >> shift) == iota((rows, K2), 1))
    lane = iota((1, 3 * rows), 1)
    which = jnp.where(lane >= rows, 1, 0) + jnp.where(lane >= 2 * rows, 1, 0)
    lane = lane - which * rows
    spreads = [
        onehot(jnp.where(which == c, lane >> shift, -1) == iota((K2, 3 * rows), 0)) for c in range(3)
    ]
    mask = onehot((iota((rows, 1), 0) & (nz - 1)) == (lane & (nz - 1)), F32)
    return spread_rows, spreads, mask


def flipped(matrix):
    return matrix.astype(F32).T.astype(BF)


def exchange(tiles):
    lane = iota((1, 128), 1)
    low = (lane & 64) == 0
    a, b, c, d = tiles
    a, c = jnp.where(low, a, pltpu.roll(c, 64, 1)), jnp.where(low, pltpu.roll(a, 64, 1), c)
    b, d = jnp.where(low, b, pltpu.roll(d, 64, 1)), jnp.where(low, pltpu.roll(b, 64, 1), d)
    low = (lane & 32) == 0
    a, b = jnp.where(low, a, pltpu.roll(b, 32, 1)), jnp.where(low, pltpu.roll(a, 96, 1), b)
    c, d = jnp.where(low, c, pltpu.roll(d, 32, 1)), jnp.where(low, pltpu.roll(c, 96, 1), d)
    return a, b, c, d


def build_kernel(fine_hbm, coarse_hbm, child_hbm, *refs):
    (fine_rows, fine_y, fine_z, fine_sides, coarse_rows, coarse_y, coarse_z, coarse_sides,
     down_rows, down_y, down_z, up_rows, up_y, up_z, fine_ref, coarse_ref, child_ref, sems) = refs
    copies = [
        pltpu.make_async_copy(src, dst, sems.at[n])
        for n, (src, dst) in enumerate(((fine_hbm, fine_ref), (coarse_hbm, coarse_ref), (child_hbm, child_ref)))
    ]
    for copy in copies:
        copy.start()
    px, py = lax.axis_index("gx") & 1, lax.axis_index("gy") & 1
    rows_y, lanes_y, mask_y = lane_constants(True)
    rows_z, lanes_z, mask_z = lane_constants(False)
    mask3_y = jnp.concatenate([mask_y] * 3, axis=1)
    mask3_z = jnp.concatenate([mask_z] * 3, axis=1)
    near_x, near_y = 2 - 2 * px, 2 - 2 * py
    levels = (
        (fine_ref, fine_rows, fine_y, fine_z, fine_sides, FINE_ROWS, 4, (1, near_x, 2 - near_x), (1, near_y, 2 - near_y)),
        (coarse_ref, coarse_rows, coarse_y, coarse_z, coarse_sides, COARSE_ROWS, 2, (1, 2 - near_x, near_x), (1, 2 - near_y, near_y)),
    )
    for copy in copies:
        copy.wait()
    for blocks, rows_out, y_out, z_out, sides_out, rows, nz, order_x, order_y in levels:
        spread_rows, spreads, mask = row_constants(rows, nz)

        def term(m, carry, blocks=blocks, rows_out=rows_out, y_out=y_out, z_out=z_out, sides_out=sides_out,
                 order_x=order_x, order_y=order_y, rows=rows,
                 spread_rows=spread_rows, spreads=spreads, mask=mask):
            wide = sum(dot(blocks[d, m], spreads[n]) for n, d in enumerate(order_x))
            rows_out[m] = (dot(spread_rows, wide.astype(BF)) * mask).astype(BF)
            wide_y = [dot(flipped(blocks[d, m]), lanes_y).astype(BF) for d in order_y]
            wide_z = [dot(flipped(blocks[d, m]), lanes_z).astype(BF) for d in (1, 2, 0)]
            mats = (dot(rows_y, jnp.concatenate(wide_y, axis=1)) * mask3_y).astype(BF)
            zero = jnp.zeros((128, 128), BF)
            for n in range(3):
                y_out[m, 128 * n:128 * n + 128, 0:128] = mats[:, 128 * n:128 * n + 128]
                y_out[m, 128 * n:128 * n + 128, 128:256] = zero
            y_out[m, 384:512, 0:128] = zero
            y_out[m, 384:512, 128:256] = mats[:, 0:128]
            mats = (dot(rows_z, jnp.concatenate(wide_z, axis=1)) * mask3_z).astype(BF)
            z_out[m] = mats[:, 0:128]
            sides_out[m] = mats[:, 128:384]
            return carry

        lax.fori_loop(0, TERMS, term, 0, unroll=6)

    first_child, second_child = child_ref[:, 0, :], child_ref[:, 1, :]

    def chosen(condition, a, b):
        return jnp.where(condition, a.astype(F32), b.astype(F32)).astype(BF)

    own_x, other_x = chosen(px == 0, first_child, second_child), chosen(px == 0, second_child, first_child)
    own_y, other_y = chosen(py == 0, first_child, second_child), chosen(py == 0, second_child, first_child)

    def lane_matrix(transposed, spread_rows, spread_lanes, mask):
        return (dot(spread_rows, dot(transposed, spread_lanes).astype(BF)) * mask).astype(BF)

    down_y[0:128, :] = lane_matrix(flipped(own_y), rows_y, lanes_y, mask_y)
    down_y[128:256, :] = lane_matrix(flipped(other_y), rows_y, lanes_y, mask_y)
    up_y[...] = lane_matrix(own_y, rows_y, lanes_y, mask_y)
    for c, child in enumerate((first_child, second_child)):
        down_z[128 * c:128 * c + 128, :] = lane_matrix(flipped(child), rows_z, lanes_z, mask_z)
        up_z[:, 128 * c:128 * c + 128] = lane_matrix(child, rows_z, lanes_z, mask_z)
    lane = iota((1, 160), 1)
    far = lane >= 80
    lane = jnp.where(far, lane - 80, lane)
    wide = dot(own_x, onehot(jnp.where(far, -1, lane >> 2) == iota((K2, 160), 0)))
    wide = wide + dot(other_x, onehot(jnp.where(far, lane >> 2, -1) == iota((K2, 160), 0)))
    r = iota((96, 1), 0)
    cz = jnp.where(r >= 48, 1, 0)
    r = r - 48 * cz
    mixed = dot(onehot((r >> 1) == iota((96, K2), 1)), wide.astype(BF))
    down_rows[...] = (mixed * onehot((2 * (r & 1) + cz) == (lane & 3), F32)).astype(BF)
    wide = dot(flipped(own_x), onehot((iota((1, 48), 1) >> 1) == iota((K2, 48), 0)))
    mixed = dot(onehot((iota((80, 1), 0) >> 2) == iota((80, K2), 1)), wide.astype(BF))
    keep = ((iota((80, 1), 0) & 3) >> 1) == (iota((1, 48), 1) & 1)
    up_rows[...] = (mixed * onehot(keep, F32)).astype(BF)


def build(fine_blocks, coarse_blocks, child):
    def s(*shape):
        return jax.ShapeDtypeStruct(shape, BF)

    out_shape = ()
    for rows in (FINE_ROWS, COARSE_ROWS):
        out_shape += (s(TERMS, rows, 3 * rows), s(TERMS, 512, 256), s(TERMS, 128, 128), s(TERMS, 128, 256))
    out_shape += (s(96, 160), s(256, 128), s(256, 128), s(80, 48), s(128, 128), s(128, 256))
    return pl.pallas_call(
        build_kernel, out_shape=out_shape, name="build",
        in_specs=[pl.BlockSpec(memory_space=pltpu.HBM)] * 3,
        scratch_shapes=[
            pltpu.VMEM((3, TERMS, K2, K2), BF), pltpu.VMEM((3, TERMS, K2, K2), BF),
            pltpu.VMEM((K2, 2, K2), BF), pltpu.SemaphoreType.DMA((3,)),
        ],
        compiler_params=pltpu.CompilerParams(vmem_limit_bytes=32 << 20),
        cost_estimate=pl.CostEstimate(flops=4 * 10**9, bytes_accessed=10 * 10**6, transcendentals=0),
    )(*(
        pltpu.with_memory_space_constraint(x, pltpu.HBM)
        for x in (fine_blocks, coarse_blocks, jnp.transpose(child, (1, 0, 2)))
    ))


def source_kernel(own, xnear, xfar, ynear, yfar, corner, down_rows, down_y, down_z,
                  along_x, along_y, parent, natural, pair, mixed, turned):
    select = onehot(iota((400, 512), 0) == natural_place(iota((1, 512), 1), True))

    def converted(ref, slot):
        values = ref[0, 0].astype(F32)
        for i in range(K2):
            natural[slot, 4 * i:4 * i + 4, :] = values[:, 400 * i:400 * i + 400]
        return dot(natural[slot].astype(BF), select).astype(BF)

    centre = converted(own, 0)
    x_near, y_near = converted(xnear, 1), converted(ynear, 2)
    diagonal = converted(corner, 3)
    along_x[0:80, :] = centre
    along_x[80:160, :] = x_near
    along_x[160:240, :] = converted(xfar, 4)
    along_y[:, 0:512] = centre
    along_y[:, 512:1024] = y_near
    along_y[:, 1024:1536] = converted(yfar, 5)
    pair[0:80, 0:512] = centre
    pair[80:160, 0:512] = x_near
    pair[0:80, 512:1024] = y_near
    pair[80:160, 512:1024] = diagonal
    rows = dot(down_rows[...], pair[...]).astype(BF)
    for b in range(4):
        for c in range(2):
            mixed[96 * b:96 * b + 96, 128 * c:128 * c + 128] = rows[:, 512 * c + 128 * b:512 * c + 128 * b + 128]
    summed = dot(mixed[...], down_y[...])
    blocks = exchange([summed[96 * b:96 * b + 96, :] for b in range(4)])
    for b in range(4):
        for c in range(2):
            turned[48 * b:48 * b + 48, 128 * c:128 * c + 128] = blocks[b][48 * c:48 * c + 48, :].astype(BF)
    total = dot(turned[...], down_z[...])
    blocks = exchange([total[48 * b:48 * b + 48, :] for b in range(4)])
    for b in range(4):
        parent[:, 128 * b:128 * b + 128] = blocks[b].astype(BF)


def source(columns, down_rows, down_y, down_z):
    out_shape = (
        jax.ShapeDtypeStruct((3 * FINE_ROWS, 512), BF),
        jax.ShapeDtypeStruct((FINE_ROWS, 1536), BF),
        jax.ShapeDtypeStruct((COARSE_ROWS, 512), BF),
    )
    scratch = [
        pltpu.VMEM((6, FINE_ROWS, 400), F32),
        pltpu.VMEM((2 * FINE_ROWS, 1024), BF),
        pltpu.VMEM((8 * COARSE_ROWS, 256), BF),
        pltpu.VMEM((4 * COARSE_ROWS, 256), BF),
    ]
    return pl.pallas_call(
        source_kernel, out_shape=out_shape, scratch_shapes=scratch, name="source",
        compiler_params=pltpu.CompilerParams(vmem_limit_bytes=16 << 20),
        cost_estimate=pl.CostEstimate(flops=10**9, bytes_accessed=10**6, transcendentals=0),
    )(*columns, down_rows, down_y, down_z)


def level_first(rows, along_x, along_y, row_mats, first):
    for m in range(TERMS):
        both = dot(row_mats[m], along_x)
        sides = dot(row_mats[m][:, 0:rows], along_y)
        for b in range(4):
            here = pl.ds(b * rows, rows)
            first[m, here, 0:128] = both[:, 128 * b:128 * b + 128].astype(BF)
            first[m, here, 128:256] = sides[:, 512 + 128 * b:640 + 128 * b].astype(BF)
            first[m, here, 256:384] = sides[:, 1024 + 128 * b:1152 + 128 * b].astype(BF)
            first[m, here, 384:512] = sides[:, 128 * b:128 * b + 128].astype(BF)


def level_rest(rows, nz, first, y_mats, z_mats, side_mats, sums, centres):
    for m in range(TERMS):
        result = dot(first[m], y_mats[m])
        for n, target in enumerate((sums, centres)):
            blocks = exchange([result[b * rows:(b + 1) * rows, 128 * n:128 * n + 128] for b in range(4)])
            for b in range(4):
                target[b * rows:(b + 1) * rows, 128 * m:128 * m + 128] = blocks[b].astype(BF)
    total = dot(sums[...], z_mats[...].reshape(TERMS * 128, 128))
    sides = dot(centres[...], side_mats[...].reshape(TERMS * 128, 256))
    z = iota((4 * rows, 128), 0) & (nz - 1)
    total = total + jnp.where(z == nz - 1, 0.0, pltpu.roll(sides[:, 0:128], 4 * rows - 1, 0))
    return total + jnp.where(z == 0, 0.0, pltpu.roll(sides[:, 128:256], 1, 0))


def level_scratch(rows):
    return [
        pltpu.VMEM((4 * rows, TERMS * 128), BF),
        pltpu.VMEM((4 * rows, TERMS * 128), BF),
    ]


def fine_first_kernel(along_x, along_y, row_mats, first):
    level_first(FINE_ROWS, along_x[...], along_y[...], row_mats, first)


def fine_first(along_x, along_y, row_mats):
    return pl.pallas_call(
        fine_first_kernel, out_shape=jax.ShapeDtypeStruct((TERMS, 4 * FINE_ROWS, 512), BF), name="fine_first",
        compiler_params=pltpu.CompilerParams(vmem_limit_bytes=16 << 20),
        cost_estimate=pl.CostEstimate(flops=2 * 10**9, bytes_accessed=10 * 10**6, transcendentals=0),
    )(along_x, along_y, row_mats)


def fine_rest_kernel(first, y_mats, z_mats, side_mats, out, sums, centres):
    out[...] = level_rest(FINE_ROWS, 4, first, y_mats, z_mats, side_mats, sums, centres)


def fine_rest(first, mats):
    return pl.pallas_call(
        fine_rest_kernel, out_shape=jax.ShapeDtypeStruct((4 * FINE_ROWS, 128), F32),
        scratch_shapes=level_scratch(FINE_ROWS), name="fine_rest",
        compiler_params=pltpu.CompilerParams(vmem_limit_bytes=16 << 20),
        cost_estimate=pl.CostEstimate(flops=4 * 10**9, bytes_accessed=10 * 10**6, transcendentals=0),
    )(first, *mats)


def coarse_kernel(own, xfar, xother, yfar, yother, row_mats, y_mats, z_mats, side_mats,
                  up_rows, up_y, up_z, fine_term, out, along_x, along_y, wide, grown, turned, split, first, *scratch):
    along_x[0:48, :] = own[...]
    along_x[48:96, :] = xfar[...]
    along_x[96:144, :] = xother[...]
    along_y[:, 0:512] = own[...]
    along_y[:, 512:1024] = yfar[...]
    along_y[:, 1024:1536] = yother[...]
    level_first(COARSE_ROWS, along_x[...], along_y[...], row_mats, first)
    result = level_rest(COARSE_ROWS, 2, first, y_mats, z_mats, side_mats, *scratch)
    blocks = exchange([result[48 * b:48 * b + 48, :] for b in range(4)])
    for b in range(4):
        wide[:, 128 * b:128 * b + 128] = blocks[b].astype(BF)
    part = dot(up_rows[...], wide[...]).astype(BF)
    for b in range(4):
        grown[80 * b:80 * b + 80, :] = part[:, 128 * b:128 * b + 128]
    part = dot(grown[...], up_y[...])
    blocks = exchange([part[80 * b:80 * b + 80, :] for b in range(4)])
    for b in range(4):
        turned[80 * b:80 * b + 80, :] = blocks[b].astype(BF)
    both = dot(turned[...], up_z[...])
    expanded = jnp.where((iota((320, 128), 0) & 1) == 0, both[:, 0:128], both[:, 128:256])
    total = fine_term[...] + expanded
    high = total.astype(BF)
    low = (total - high.astype(F32)).astype(BF)
    for b in range(4):
        split[0:80, 128 * b:128 * b + 128] = high[80 * b:80 * b + 80, :]
        split[80:160, 128 * b:128 * b + 128] = low[80 * b:80 * b + 80, :]
    select = onehot(natural_place(iota((512, 1), 0), False) == iota((512, 400), 1))
    natural = dot(split[...], select)
    natural = natural[0:80, :] + natural[80:160, :]
    for i in range(K2):
        out[0, 0, :, 400 * i:400 * i + 400] = natural[4 * i:4 * i + 4, :]


def coarse(parents, mats, up_rows, up_y, up_z, fine_term):
    scratch = [
        pltpu.VMEM((3 * COARSE_ROWS, 512), BF),
        pltpu.VMEM((COARSE_ROWS, 1536), BF),
        pltpu.VMEM((COARSE_ROWS, 512), BF),
        pltpu.VMEM((320, 128), BF),
        pltpu.VMEM((320, 128), BF),
        pltpu.VMEM((160, 512), BF),
        pltpu.VMEM((TERMS, 4 * COARSE_ROWS, 512), BF),
    ] + level_scratch(COARSE_ROWS)
    return pl.pallas_call(
        coarse_kernel, out_shape=jax.ShapeDtypeStruct((1, 1, 4, 8000), F32),
        scratch_shapes=scratch, name="coarse",
        compiler_params=pltpu.CompilerParams(vmem_limit_bytes=32 << 20),
        cost_estimate=pl.CostEstimate(flops=4 * 10**9, bytes_accessed=10 * 10**6, transcendentals=0),
    )(*parents, *mats, up_rows, up_y, up_z, fine_term)


def near(block, axis):
    return lax.ppermute(block, axis, [(i, i ^ 1) for i in range(lax.axis_size(axis))])


def far(block, axis):
    count = lax.axis_size(axis)
    return lax.ppermute(block, axis, [(i, ((i + 1) ^ 1) - 1) for i in range(1, count - 1)])


def corner(block):
    nx, ny = lax.axis_size("gx"), lax.axis_size("gy")
    route = [(x * ny + y, (x ^ 1) * ny + (y ^ 1)) for x in range(nx) for y in range(ny)]
    return lax.ppermute(block, ("gx", "gy"), route)


def shards(fine_source, fine_blocks, coarse_blocks, child_filter_matrices):
    columns = [fine_source, near(fine_source, "gx"), far(fine_source, "gx"),
               near(fine_source, "gy"), far(fine_source, "gy"), corner(fine_source)]
    built = build(fine_blocks, coarse_blocks, child_filter_matrices)
    along_x, along_y, parent = source(columns, *built[8:11])
    x_far, y_far = far(parent, "gx"), far(parent, "gy")
    first = fine_first(along_x, along_y, built[0])
    x_far, y_far, first = lax.optimization_barrier((x_far, y_far, first))
    fine_term = fine_rest(first, built[1:4])
    parents = [parent, x_far, near(x_far, "gx"), y_far, near(y_far, "gy")]
    return coarse(parents, built[4:8], *built[11:14], fine_term)


def solution(mesh):
    in_specs = (P("gx", "gy", None, None), P(), P(), P())
    out_specs = P("gx", "gy", None, None)
    return jax.shard_map(shards, mesh=mesh, in_specs=in_specs, out_specs=out_specs, check_vma=False)
```

time: 65.5 us -> 44.8 us (0.68)
  the two profiles are of different devices: /device:TPU:130 before, /device:TPU:92 now
where the time goes in v1:
time: 44.8 us; the launch traced here: 44.6 us
  Pallas kernels  19 us (42%)
  starting transfers between devices  18.2 us (41%)
  waiting for transfers between devices  7.3 us (16%)
    ppermute x4, starting transfers between devices, far(): lax.ppermute(block, axis, [(i, (i + 1 ^ 1) - 1) for i in range(1, count -...  17.2 us
    pallas_call x1, Pallas kernels, build(): pl.pallas_call(build_kernel, out_shape=out_shape, name='build', in_specs=...  10.4 us
    ppermute x4, waiting for transfers between devices, far(): lax.ppermute(block, axis, [(i, (i + 1 ^ 1) - 1) for i in range(1, count -...  4.94 us
    pallas_call x1, Pallas kernels, coarse(): pl.pallas_call(coarse_kernel, out_shape=jax.ShapeDtypeStruct((1, 1, 4, 80...  3.78 us
    ppermute x4, waiting for transfers between devices, near(): lax.ppermute(block, axis, [(i, i ^ 1) for i in range(lax.axis_size(axis))])  2.36 us
    pallas_call x1, Pallas kernels, fine_rest(): pl.pallas_call(fine_rest_kernel, out_shape=jax.ShapeDtypeStruct((4 * FINE...  1.79 us
    pallas_call x1, Pallas kernels, fine_first(): pl.pallas_call(fine_first_kernel, out_shape=jax.ShapeDtypeStruct((TERMS,...  1.54 us
    pallas_call x1, Pallas kernels, source(): pl.pallas_call(source_kernel, out_shape=out_shape, scratch_shapes=scratch...  1.48 us
  transfers between devices with their start and end apart: 9, of which 2 were waited for; matrix products, arithmetic and copies ran while one was open for 0% of the time, Pallas kernels for 31%

profile of v1, /device:TPU:92, one launch (start us, length us, event | category | flops | bytes accessed | tf_op | source)
XLA Modules:
  0.0 44.6 jit_solution(11870636395419464994)
XLA Ops:
  0.0 0.0 collective-permute-start
  0.0 3.9 %collective-permute-start.1 = (bf16[1,1,4,8000]{3,2,1,0:T(4,128)(2,1)}, bf16[1,1,4,8000]{3,2,1,0:T(4,128)(2,1)S(1)}, u32[]{:S(2)}, u32[]{:S(2)}) collective-permute-start(bf16[1,1,4,8000]{3,2,1,0:T(4,128)(2,1)} %own.1), channel_id=1, source_target_pairs={{16,32},{32,16},{48,64},{64,48},{80,96},{96,80},{112,128},{128,112... | collective-permute-start | bytes 192008 | tf_op jit(solution)/shard_map/ppermute | solution.py:360
  3.9 0.8 %collective-permute-start.2 = (bf16[1,1,4,8000]{3,2,1,0:T(4,128)(2,1)}, bf16[1,1,4,8000]{3,2,1,0:T(4,128)(2,1)S(1)}, u32[]{:S(2)}, u32[]{:S(2)}) collective-permute-start(bf16[1,1,4,8000]{3,2,1,0:T(4,128)(2,1)} %own.1), channel_id=1, source_target_pairs={{0,1},{1,0},{2,3},{3,2},{4,5},{5,4},{6,7},{7,6},{8,9},{9,8},{10,11... | collective-permute-start | bytes 192008 | tf_op jit(solution)/shard_map/ppermute | solution.py:355
  4.7 6.0 %collective-permute-start.3 = (bf16[1,1,4,8000]{3,2,1,0:T(4,128)(2,1)}, bf16[1,1,4,8000]{3,2,1,0:T(4,128)(2,1)S(1)}, u32[]{:S(2)}, u32[]{:S(2)}) collective-permute-start(bf16[1,1,4,8000]{3,2,1,0:T(4,128)(2,1)} %own.1), channel_id=1, source_target_pairs={{1,2},{2,1},{3,4},{4,3},{5,6},{6,5},{7,8},{8,7},{9,10},{10,9},{11,... | collective-permute-start | bytes 192008 | tf_op jit(solution)/shard_map/ppermute | solution.py:360
  10.7 0.1 collective-permute-start.4
  10.8 0.0 copy-start
  10.8 10.4 %build.1 = (bf16[12,80,240]{2,1,0:T(8,128)(2,1)S(1)}, bf16[12,512,256]{2,1,0:T(8,128)(2,1)S(1)}, bf16[12,128,128]{2,1,0:T(8,128)(2,1)S(1)}, bf16[12,128,256]{2,1...) custom-call(bf16[3,12,20,20]{3,2,1,0:T(8,128)(2,1)} %fine_hbm.1, ...), custom_call_target="tpu_custom_call" | custom-call | flops 4000000000 | bytes 10000000 | tf_op jit(solution)/shard_map/build/pallas_call | solution.py:171
  21.2 0.0 collective-permute-done.xnear
  21.2 0.0 collective-permute-done.1.xfar
  21.3 0.0 collective-permute-done.2.ynear
  21.3 0.0 collective-permute-done.3.yfar
  21.3 0.0 collective-permute-done.4.corner
  21.3 1.5 %source.1 = (bf16[240,512]{1,0:T(8,128)(2,1)S(1)}, bf16[80,1536]{1,0:T(8,128)(2,1)S(1)}, bf16[48,512]{1,0:T(8,128)(2,1)S(1)}) custom-call(bf16[1,1,4,8000]{3,2,1,0:T(4,128)(2,1)S(1)} %copy-done, bf16[1,1,4,8000]{3,2,1,0:T(4,128)(2,1)S(1)} %collective-permute-done.xnear, bf16[1,1,4,8000]{3,2,1,0:T(4,128)(2,1)S(1)} %collective-permute-done.1.xfar, ...), custom_call_target="tpu_custom_call" | custom-call | flops 1000000000 | bytes 1000000 | tf_op jit(solution)/shard_map/source/pallas_call | solution.py:236
  22.8 2.9 %collective-permute-start.5 = (bf16[48,512]{1,0:T(8,128)(2,1)S(1)}, bf16[48,512]{1,0:T(8,128)(2,1)S(1)}, u32[]{:S(2)}, u32[]{:S(2)}) collective-permute-start(bf16[48,512]{1,0:T(8,128)(2,1)S(1)} %get-tuple-element.28.own), channel_id=1, source_target_pairs={{16,32},{32,16},{48,64},{64,48},{80,96},{96,80},{112,128},{128,112... | collective-permute-start | bytes 147464 | tf_op jit(solution)/shard_map/ppermute | solution.py:360
  25.7 4.5 %collective-permute-start.6 = (bf16[48,512]{1,0:T(8,128)(2,1)S(1)}, bf16[48,512]{1,0:T(8,128)(2,1)S(1)}, u32[]{:S(2)}, u32[]{:S(2)}) collective-permute-start(bf16[48,512]{1,0:T(8,128)(2,1)S(1)} %get-tuple-element.28.own), channel_id=1, source_target_pairs={{1,2},{2,1},{3,4},{4,3},{5,6},{6,5},{7,8},{8,7},{9,10},{10,9},{11,... | collective-permute-start | bytes 147464 | tf_op jit(solution)/shard_map/ppermute | solution.py:360
  30.2 1.5 %fine_first.1.first = bf16[12,320,512]{2,1,0:T(8,128)(2,1)S(1)} custom-call(bf16[240,512]{1,0:T(8,128)(2,1)S(1)} %get-tuple-element.29.along_x, bf16[80,1536]{1,0:T(8,128)(2,1)S(1)} %get-tuple-element.30.along_y, bf16[12,80,240]{2,1,0:T(8,128)(2,1)S(1)} %get-tuple-element.31.row_mats), custom_call_target="tpu_custom_call" | custom-call | flops 2000000000 | bytes 10000000 | tf_op jit(solution)/shard_map/fine_first/pallas_call | solution.py:281
  31.7 0.0 collective-permute-done.5.xfar
  31.7 4.9 %collective-permute-done.6.yfar = bf16[48,512]{1,0:T(8,128)(2,1)S(1)} collective-permute-done((bf16[48,512]{1,0:T(8,128)(2,1)S(1)}, bf16[48,512]{1,0:T(8,128)(2,1)S(1)}, u32[]{:S(2)}, u32[]{:S(2)}) %collective-permute-start.6) | collective-permute-done | bytes 49184 | tf_op jit(solution)/shard_map/ppermute | solution.py:360
  36.7 0.0 collective-permute-start.7
  36.7 0.0 collective-permute-start.8
  36.7 1.8 %fine_rest.1.fine_term = f32[320,128]{1,0:T(8,128)S(1)} custom-call(bf16[12,320,512]{2,1,0:T(8,128)(2,1)S(1)} %fine_first.1.first, bf16[12,512,256]{2,1,0:T(8,128)(2,1)S(1)} %get-tuple-element.42.y_mats, bf16[12,128,128]{2,1,0:T(8,128)(2,1)S(1)} %get-tuple-element.43.z_mats, bf16[12,128,256]{2,1,0:T(8,128)(2,1)S(1)} %get-tuple-element.44.side_mats), custom_call_target="tpu_custom_call" | custom-call | flops 4000000000 | bytes 10000000 | tf_op jit(solution)/shard_map/fine_rest/pallas_call | solution.py:293
  38.5 0.0 collective-permute-done.7.xother
  38.5 2.3 %collective-permute-done.8.yother = bf16[48,512]{1,0:T(8,128)(2,1)S(1)} collective-permute-done((bf16[48,512]{1,0:T(8,128)(2,1)S(1)}, bf16[48,512]{1,0:T(8,128)(2,1)S(1)}, u32[]{:S(2)}, u32[]{:S(2)}) %collective-permute-start.8) | collective-permute-done | bytes 49184 | tf_op jit(solution)/shard_map/ppermute | solution.py:355
  40.8 3.8 %coarse.1 = f32[1,1,4,8000]{3,2,1,0:T(4,128)} custom-call(bf16[48,512]{1,0:T(8,128)(2,1)S(1)} %get-tuple-element.28.own, bf16[48,512]{1,0:T(8,128)(2,1)S(1)} %collective-permute-done.5.xfar, bf16[48,512]{1,0:T(8,128)(2,1)S(1)} %collective-permute-done.7.xother, bf16[48,512]{1,0:T(8,128)(2,1)S(1)} %collective-permute-done.6.yfar, ...), custom_call_target="tpu_custom_call" | custom-call | flops 4000000000 | bytes 10000000 | tf_op jit(solution)/shard_map/coarse/pallas_call | solution.py:346
  (1 shorter events, 0.0 us)
Async XLA Ops:
  0.0 21.2 %collective-permute-start = (bf16[1,1,4,8000]{3,2,1,0:T(4,128)(2,1)}, bf16[1,1,4,8000]{3,2,1,0:T(4,128)(2,1)S(1)}, u32[]{:S(2)}, u32[]{:S(2)}) collective-permute-start(bf16[1,1,4,8000]{3,2,1,0:T(4,128)(2,1)} %own.1), channel_id=1, source_target_pairs={{0,16},{16,0},{32,48},{48,32},{64,80},{80,64},{96,112},{112,96},{1... | collective-permute-start | bytes 192008 | tf_op jit(solution)/shard_map/ppermute | solution.py:355
  0.0 21.2 %collective-permute-start.1 = (bf16[1,1,4,8000]{3,2,1,0:T(4,128)(2,1)}, bf16[1,1,4,8000]{3,2,1,0:T(4,128)(2,1)S(1)}, u32[]{:S(2)}, u32[]{:S(2)}) collective-permute-start(bf16[1,1,4,8000]{3,2,1,0:T(4,128)(2,1)} %own.1), channel_id=1, source_target_pairs={{16,32},{32,16},{48,64},{64,48},{80,96},{96,80},{112,128},{128,112... | collective-permute-start | bytes 192008 | tf_op jit(solution)/shard_map/ppermute | solution.py:360
  3.9 17.4 %collective-permute-start.2 = (bf16[1,1,4,8000]{3,2,1,0:T(4,128)(2,1)}, bf16[1,1,4,8000]{3,2,1,0:T(4,128)(2,1)S(1)}, u32[]{:S(2)}, u32[]{:S(2)}) collective-permute-start(bf16[1,1,4,8000]{3,2,1,0:T(4,128)(2,1)} %own.1), channel_id=1, source_target_pairs={{0,1},{1,0},{2,3},{3,2},{4,5},{5,4},{6,7},{7,6},{8,9},{9,8},{10,11... | collective-permute-start | bytes 192008 | tf_op jit(solution)/shard_map/ppermute | solution.py:355
  4.7 16.5 %collective-permute-start.3 = (bf16[1,1,4,8000]{3,2,1,0:T(4,128)(2,1)}, bf16[1,1,4,8000]{3,2,1,0:T(4,128)(2,1)S(1)}, u32[]{:S(2)}, u32[]{:S(2)}) collective-permute-start(bf16[1,1,4,8000]{3,2,1,0:T(4,128)(2,1)} %own.1), channel_id=1, source_target_pairs={{1,2},{2,1},{3,4},{4,3},{5,6},{6,5},{7,8},{8,7},{9,10},{10,9},{11,... | collective-permute-start | bytes 192008 | tf_op jit(solution)/shard_map/ppermute | solution.py:360
  10.7 10.6 %collective-permute-start.4 = (bf16[1,1,4,8000]{3,2,1,0:T(4,128)(2,1)}, bf16[1,1,4,8000]{3,2,1,0:T(4,128)(2,1)S(1)}, u32[]{:S(2)}, u32[]{:S(2)}) collective-permute-start(bf16[1,1,4,8000]{3,2,1,0:T(4,128)(2,1)} %own.1), channel_id=1, source_target_pairs={{0,17},{1,16},{2,19},{3,18},{4,21},{5,20},{6,23},{7,22},{8,25},{9,... | collective-permute-start | bytes 192008 | tf_op jit(solution)/shard_map/ppermute | solution.py:366
  10.8 10.5 %copy-start = (bf16[1,1,4,8000]{3,2,1,0:T(4,128)(2,1)S(1)}, bf16[1,1,4,8000]{3,2,1,0:T(4,128)(2,1)}, u32[]{:S(2)}) copy-start(bf16[1,1,4,8000]{3,2,1,0:T(4,128)(2,1)} %own.1) | copy-start | bytes 192004
  22.8 8.9 %collective-permute-start.5 = (bf16[48,512]{1,0:T(8,128)(2,1)S(1)}, bf16[48,512]{1,0:T(8,128)(2,1)S(1)}, u32[]{:S(2)}, u32[]{:S(2)}) collective-permute-start(bf16[48,512]{1,0:T(8,128)(2,1)S(1)} %get-tuple-element.28.own), channel_id=1, source_target_pairs={{16,32},{32,16},{48,64},{64,48},{80,96},{96,80},{112,128},{128,112... | collective-permute-start | bytes 147464 | tf_op jit(solution)/shard_map/ppermute | solution.py:360
  25.7 11.0 %collective-permute-start.6 = (bf16[48,512]{1,0:T(8,128)(2,1)S(1)}, bf16[48,512]{1,0:T(8,128)(2,1)S(1)}, u32[]{:S(2)}, u32[]{:S(2)}) collective-permute-start(bf16[48,512]{1,0:T(8,128)(2,1)S(1)} %get-tuple-element.28.own), channel_id=1, source_target_pairs={{1,2},{2,1},{3,4},{4,3},{5,6},{6,5},{7,8},{8,7},{9,10},{10,9},{11,... | collective-permute-start | bytes 147464 | tf_op jit(solution)/shard_map/ppermute | solution.py:360
  36.7 1.8 %collective-permute-start.7 = (bf16[48,512]{1,0:T(8,128)(2,1)S(1)}, bf16[48,512]{1,0:T(8,128)(2,1)S(1)}, u32[]{:S(2)}, u32[]{:S(2)}) collective-permute-start(bf16[48,512]{1,0:T(8,128)(2,1)S(1)} %collective-permute-done.5.xfar), channel_id=1, source_target_pairs={{0,16},{16,0},{32,48},{48,32},{64,80},{80,64},{96,112},{112,96},{1... | collective-permute-start | bytes 147464 | tf_op jit(solution)/shard_map/ppermute | solution.py:355
  36.7 4.2 %collective-permute-start.8 = (bf16[48,512]{1,0:T(8,128)(2,1)S(1)}, bf16[48,512]{1,0:T(8,128)(2,1)S(1)}, u32[]{:S(2)}, u32[]{:S(2)}) collective-permute-start(bf16[48,512]{1,0:T(8,128)(2,1)S(1)} %collective-permute-done.6.yfar), channel_id=1, source_target_pairs={{0,1},{1,0},{2,3},{3,2},{4,5},{5,4},{6,7},{7,6},{8,9},{9,8},{10,11... | collective-permute-start | bytes 147464 | tf_op jit(solution)/shard_map/ppermute | solution.py:355

commit v2 on v1

--- a/solution.py
+++ b/solution.py
@@ -47,7 +47,7 @@
         _, jj, kk, ok = place(n)
         return jnp.where(ok, kk if on_j else jj, none)
 
-    spread_rows = onehot(index(iota((128, 1), 0)) == iota((128, K2), 1))
+    spread_rows = onehot(index(iota((128, 1), 0)) == iota((128, 32), 1))
     spread_lanes = onehot(index(iota((1, 128), 1)) == iota((K2, 128), 0))
     mask = onehot(fixed(iota((128, 1), 0), -1) == fixed(iota((1, 128), 1), -2), F32)
     return spread_rows, spread_lanes, mask
@@ -55,12 +55,13 @@
 
 def row_constants(rows, nz):
     shift = nz.bit_length() - 1
-    spread_rows = onehot((iota((rows, 1), 0) >> shift) == iota((rows, K2), 1))
-    lane = iota((1, 3 * rows), 1)
-    which = jnp.where(lane >= rows, 1, 0) + jnp.where(lane >= 2 * rows, 1, 0)
+    spread_rows = onehot((iota((rows, 1), 0) >> shift) == iota((rows, 32), 1))
+    wide = 256
+    lane = iota((1, wide), 1)
+    which = sum(jnp.where(lane >= c * rows, 1, 0) for c in range(1, 4))
     lane = lane - which * rows
     spreads = [
-        onehot(jnp.where(which == c, lane >> shift, -1) == iota((K2, 3 * rows), 0)) for c in range(3)
+        onehot(jnp.where(which == c, lane >> shift, -1) == iota((K2, wide), 0)) for c in range(3)
     ]
     mask = onehot((iota((rows, 1), 0) & (nz - 1)) == (lane & (nz - 1)), F32)
     return spread_rows, spreads, mask
@@ -83,49 +84,60 @@
 
 
 def build_kernel(fine_hbm, coarse_hbm, child_hbm, *refs):
-    (fine_rows, fine_y, fine_z, fine_sides, coarse_rows, coarse_y, coarse_z, coarse_sides,
-     down_rows, down_y, down_z, up_rows, up_y, up_z, fine_ref, coarse_ref, child_ref, sems) = refs
+    (fine_rows, fine_y, fine_z, coarse_rows, coarse_y, coarse_z,
+     down_rows, down_y, down_z, up_rows, up_y, up_z,
+     fine_ref, coarse_ref, child_ref, plain, turned, wide_y, wide_z, wide_rows, sems) = refs
     copies = [
         pltpu.make_async_copy(src, dst, sems.at[n])
         for n, (src, dst) in enumerate(((fine_hbm, fine_ref), (coarse_hbm, coarse_ref), (child_hbm, child_ref)))
     ]
     for copy in copies:
         copy.start()
+    plain[...] = jnp.zeros(plain.shape, F32)
+    turned[...] = jnp.zeros(turned.shape, F32)
     px, py = lax.axis_index("gx") & 1, lax.axis_index("gy") & 1
     rows_y, lanes_y, mask_y = lane_constants(True)
     rows_z, lanes_z, mask_z = lane_constants(False)
-    mask3_y = jnp.concatenate([mask_y] * 3, axis=1)
-    mask3_z = jnp.concatenate([mask_z] * 3, axis=1)
+    both = jnp.concatenate([lanes_y, lanes_z], axis=1)
     near_x, near_y = 2 - 2 * px, 2 - 2 * py
     levels = (
-        (fine_ref, fine_rows, fine_y, fine_z, fine_sides, FINE_ROWS, 4, (1, near_x, 2 - near_x), (1, near_y, 2 - near_y)),
-        (coarse_ref, coarse_rows, coarse_y, coarse_z, coarse_sides, COARSE_ROWS, 2, (1, 2 - near_x, near_x), (1, 2 - near_y, near_y)),
+        (fine_ref, fine_rows, fine_y, fine_z, FINE_ROWS, 4, (1, near_x, 2 - near_x), (1, near_y, 2 - near_y)),
+        (coarse_ref, coarse_rows, coarse_y, coarse_z, COARSE_ROWS, 2, (1, 2 - near_x, near_x), (1, 2 - near_y, near_y)),
     )
     for copy in copies:
         copy.wait()
-    for blocks, rows_out, y_out, z_out, sides_out, rows, nz, order_x, order_y in levels:
+    for n, blocks in enumerate((fine_ref, coarse_ref)):
+        for d in range(3):
+            for m in range(TERMS):
+                matrix = blocks[d, m].astype(F32)
+                plain[n, d, m, 0:K2, :] = matrix
+                turned[n, d, m, 0:K2, :] = matrix.T
+    for n, (blocks, rows_out, y_out, z_out, rows, nz, order_x, order_y) in enumerate(levels):
         spread_rows, spreads, mask = row_constants(rows, nz)
-
-        def term(m, carry, blocks=blocks, rows_out=rows_out, y_out=y_out, z_out=z_out, sides_out=sides_out,
-                 order_x=order_x, order_y=order_y, rows=rows,
-                 spread_rows=spread_rows, spreads=spreads, mask=mask):
-            wide = sum(dot(blocks[d, m], spreads[n]) for n, d in enumerate(order_x))
-            rows_out[m] = (dot(spread_rows, wide.astype(BF)) * mask).astype(BF)
-            wide_y = [dot(flipped(blocks[d, m]), lanes_y).astype(BF) for d in order_y]
-            wide_z = [dot(flipped(blocks[d, m]), lanes_z).astype(BF) for d in (1, 2, 0)]
-            mats = (dot(rows_y, jnp.concatenate(wide_y, axis=1)) * mask3_y).astype(BF)
-            zero = jnp.zeros((128, 128), BF)
-            for n in range(3):
-                y_out[m, 128 * n:128 * n + 128, 0:128] = mats[:, 128 * n:128 * n + 128]
-                y_out[m, 128 * n:128 * n + 128, 128:256] = zero
-            y_out[m, 384:512, 0:128] = zero
-            y_out[m, 384:512, 128:256] = mats[:, 0:128]
-            mats = (dot(rows_z, jnp.concatenate(wide_z, axis=1)) * mask3_z).astype(BF)
-            z_out[m] = mats[:, 0:128]
-            sides_out[m] = mats[:, 128:384]
-            return carry
-
-        lax.fori_loop(0, TERMS, term, 0, unroll=6)
+        count = 3 * TERMS * 32
+        wide = dot(turned[n].reshape(count, K2).astype(BF), both).astype(BF)
+        wide_y[n] = wide[:, 0:128].reshape(3, TERMS, 32, 128)
+        wide_z[n] = wide[:, 128:256].reshape(3, TERMS, 32, 128)
+        wide = sum(dot(plain[n, d].reshape(TERMS * 32, K2).astype(BF), spreads[c]) for c, d in enumerate(order_x))
+        wide_rows[...] = wide.astype(BF).reshape(TERMS, 32, 256)
+        for m in range(TERMS):
+            mats = (dot(spread_rows, wide_rows[m]) * mask).astype(BF)
+            for c in range(2):
+                rows_out[m, c] = mats[:, 128 * c:128 * c + 128]
+        for spread, mask, source_ref, order, out in (
+            (rows_y, mask_y, wide_y, order_y, y_out), (rows_z, mask_z, wide_z, (1, 2, 0), z_out),
+        ):
+            for m in range(0, TERMS, 2):
+                tiles = [source_ref[n, d, m + c] for c in range(2) for d in order]
+                mats = dot(spread, jnp.concatenate(tiles, axis=1))
+                for c in range(2):
+                    for e in range(3):
+                        lane = 384 * c + 128 * e
+                        tile = (mats[:, lane:lane + 128] * mask).astype(BF)
+                        if out is y_out:
+                            out[m + c, e] = tile
+                        else:
+                            out[e, m + c] = tile
 
     first_child, second_child = child_ref[:, 0, :], child_ref[:, 1, :]
 
@@ -136,14 +148,14 @@
     own_y, other_y = chosen(py == 0, first_child, second_child), chosen(py == 0, second_child, first_child)
 
     def lane_matrix(transposed, spread_rows, spread_lanes, mask):
-        return (dot(spread_rows, dot(transposed, spread_lanes).astype(BF)) * mask).astype(BF)
+        return (dot(spread_rows[:, 0:K2], dot(transposed, spread_lanes).astype(BF)) * mask).astype(BF)
 
     down_y[0:128, :] = lane_matrix(flipped(own_y), rows_y, lanes_y, mask_y)
     down_y[128:256, :] = lane_matrix(flipped(other_y), rows_y, lanes_y, mask_y)
     up_y[...] = lane_matrix(own_y, rows_y, lanes_y, mask_y)
     for c, child in enumerate((first_child, second_child)):
         down_z[128 * c:128 * c + 128, :] = lane_matrix(flipped(child), rows_z, lanes_z, mask_z)
-        up_z[:, 128 * c:128 * c + 128] = lane_matrix(child, rows_z, lanes_z, mask_z)
+        up_z[c] = lane_matrix(child, rows_z, lanes_z, mask_z)
     lane = iota((1, 160), 1)
     far = lane >= 80
     lane = jnp.where(far, lane - 80, lane)
@@ -166,14 +178,17 @@
 
     out_shape = ()
     for rows in (FINE_ROWS, COARSE_ROWS):
-        out_shape += (s(TERMS, rows, 3 * rows), s(TERMS, 512, 256), s(TERMS, 128, 128), s(TERMS, 128, 256))
-    out_shape += (s(96, 160), s(256, 128), s(256, 128), s(80, 48), s(128, 128), s(128, 256))
+        out_shape += (s(TERMS, 2, rows, 128), s(TERMS, 3, 128, 128), s(3, TERMS, 128, 128))
+    out_shape += (s(96, 160), s(256, 128), s(256, 128), s(80, 48), s(128, 128), s(2, 128, 128))
     return pl.pallas_call(
         build_kernel, out_shape=out_shape, name="build",
         in_specs=[pl.BlockSpec(memory_space=pltpu.HBM)] * 3,
         scratch_shapes=[
             pltpu.VMEM((3, TERMS, K2, K2), BF), pltpu.VMEM((3, TERMS, K2, K2), BF),
-            pltpu.VMEM((K2, 2, K2), BF), pltpu.SemaphoreType.DMA((3,)),
+            pltpu.VMEM((K2, 2, K2), BF),
+            pltpu.VMEM((2, 3, TERMS, 32, K2), F32), pltpu.VMEM((2, 3, TERMS, 32, K2), F32),
+            pltpu.VMEM((2, 3, TERMS, 32, 128), BF), pltpu.VMEM((2, 3, TERMS, 32, 128), BF),
+            pltpu.VMEM((TERMS, 32, 256), BF), pltpu.SemaphoreType.DMA((3,)),
         ],
         compiler_params=pltpu.CompilerParams(vmem_limit_bytes=32 << 20),
         cost_estimate=pl.CostEstimate(flops=4 * 10**9, bytes_accessed=10 * 10**6, transcendentals=0),
@@ -242,25 +257,33 @@
 
 def level_first(rows, along_x, along_y, row_mats, first):
     for m in range(TERMS):
-        both = dot(row_mats[m], along_x)
-        sides = dot(row_mats[m][:, 0:rows], along_y)
+        mats = jnp.concatenate([row_mats[m, 0], row_mats[m, 1]], axis=1)[:, 0:3 * rows]
+        both = dot(mats, along_x)
+        sides = dot(mats[:, 0:rows], along_y)
         for b in range(4):
             here = pl.ds(b * rows, rows)
-            first[m, here, 0:128] = both[:, 128 * b:128 * b + 128].astype(BF)
-            first[m, here, 128:256] = sides[:, 512 + 128 * b:640 + 128 * b].astype(BF)
-            first[m, here, 256:384] = sides[:, 1024 + 128 * b:1152 + 128 * b].astype(BF)
-            first[m, here, 384:512] = sides[:, 128 * b:128 * b + 128].astype(BF)
-
-
-def level_rest(rows, nz, first, y_mats, z_mats, side_mats, sums, centres):
+            first[m, 0, here, :] = both[:, 128 * b:128 * b + 128].astype(BF)
+            for part, start in ((1, 512), (2, 1024), (3, 0)):
+                first[m, part, here, :] = sides[:, start + 128 * b:start + 128 * b + 128].astype(BF)
+
+
+def level_rest(rows, nz, first, y_mats, z_mats, sums, centres):
+    zero = jnp.zeros((128, 128), BF)
     for m in range(TERMS):
-        result = dot(first[m], y_mats[m])
+        mats = jnp.concatenate([
+            jnp.concatenate([y_mats[m, 0], y_mats[m, 1], y_mats[m, 2], zero], axis=0),
+            jnp.concatenate([zero, zero, zero, y_mats[m, 0]], axis=0),
+        ], axis=1)
+        result = dot(jnp.concatenate([first[m, part] for part in range(4)], axis=1), mats)
         for n, target in enumerate((sums, centres)):
             blocks = exchange([result[b * rows:(b + 1) * rows, 128 * n:128 * n + 128] for b in range(4)])
             for b in range(4):
-                target[b * rows:(b + 1) * rows, 128 * m:128 * m + 128] = blocks[b].astype(BF)
-    total = dot(sums[...], z_mats[...].reshape(TERMS * 128, 128))
-    sides = dot(centres[...], side_mats[...].reshape(TERMS * 128, 256))
+                target[m, b * rows:(b + 1) * rows, :] = blocks[b].astype(BF)
+    total = dot(jnp.concatenate([sums[m] for m in range(TERMS)], axis=1), z_mats[0].reshape(TERMS * 128, 128))
+    sides = dot(
+        jnp.concatenate([centres[m] for m in range(TERMS)], axis=1),
+        jnp.concatenate([z_mats[n].reshape(TERMS * 128, 128) for n in (1, 2)], axis=1),
+    )
     z = iota((4 * rows, 128), 0) & (nz - 1)
     total = total + jnp.where(z == nz - 1, 0.0, pltpu.roll(sides[:, 0:128], 4 * rows - 1, 0))
     return total + jnp.where(z == 0, 0.0, pltpu.roll(sides[:, 128:256], 1, 0))
@@ -268,8 +291,8 @@
 
 def level_scratch(rows):
     return [
-        pltpu.VMEM((4 * rows, TERMS * 128), BF),
-        pltpu.VMEM((4 * rows, TERMS * 128), BF),
+        pltpu.VMEM((TERMS, 4 * rows, 128), BF),
+        pltpu.VMEM((TERMS, 4 * rows, 128), BF),
     ]
 
 
@@ -279,14 +302,14 @@
 
 def fine_first(along_x, along_y, row_mats):
     return pl.pallas_call(
-        fine_first_kernel, out_shape=jax.ShapeDtypeStruct((TERMS, 4 * FINE_ROWS, 512), BF), name="fine_first",
+        fine_first_kernel, out_shape=jax.ShapeDtypeStruct((TERMS, 4, 4 * FINE_ROWS, 128), BF), name="fine_first",
         compiler_params=pltpu.CompilerParams(vmem_limit_bytes=16 << 20),
         cost_estimate=pl.CostEstimate(flops=2 * 10**9, bytes_accessed=10 * 10**6, transcendentals=0),
     )(along_x, along_y, row_mats)
 
 
-def fine_rest_kernel(first, y_mats, z_mats, side_mats, out, sums, centres):
-    out[...] = level_rest(FINE_ROWS, 4, first, y_mats, z_mats, side_mats, sums, centres)
+def fine_rest_kernel(first, y_mats, z_mats, out, sums, centres):
+    out[...] = level_rest(FINE_ROWS, 4, first, y_mats, z_mats, sums, centres)
 
 
 def fine_rest(first, mats):
@@ -298,7 +321,7 @@
     )(first, *mats)
 
 
-def coarse_kernel(own, xfar, xother, yfar, yother, row_mats, y_mats, z_mats, side_mats,
+def coarse_kernel(own, xfar, xother, yfar, yother, row_mats, y_mats, z_mats,
                   up_rows, up_y, up_z, fine_term, out, along_x, along_y, wide, grown, turned, split, first, *scratch):
     along_x[0:48, :] = own[...]
     along_x[48:96, :] = xfar[...]
@@ -307,7 +330,7 @@
     along_y[:, 512:1024] = yfar[...]
     along_y[:, 1024:1536] = yother[...]
     level_first(COARSE_ROWS, along_x[...], along_y[...], row_mats, first)
-    result = level_rest(COARSE_ROWS, 2, first, y_mats, z_mats, side_mats, *scratch)
+    result = level_rest(COARSE_ROWS, 2, first, y_mats, z_mats, *scratch)
     blocks = exchange([result[48 * b:48 * b + 48, :] for b in range(4)])
     for b in range(4):
         wide[:, 128 * b:128 * b + 128] = blocks[b].astype(BF)
@@ -318,7 +341,7 @@
     blocks = exchange([part[80 * b:80 * b + 80, :] for b in range(4)])
     for b in range(4):
         turned[80 * b:80 * b + 80, :] = blocks[b].astype(BF)
-    both = dot(turned[...], up_z[...])
+    both = dot(turned[...], jnp.concatenate([up_z[0], up_z[1]], axis=1))
     expanded = jnp.where((iota((320, 128), 0) & 1) == 0, both[:, 0:128], both[:, 128:256])
     total = fine_term[...] + expanded
     high = total.astype(BF)
@@ -341,7 +364,7 @@
         pltpu.VMEM((320, 128), BF),
         pltpu.VMEM((320, 128), BF),
         pltpu.VMEM((160, 512), BF),
-        pltpu.VMEM((TERMS, 4 * COARSE_ROWS, 512), BF),
+        pltpu.VMEM((TERMS, 4, 4 * COARSE_ROWS, 128), BF),
     ] + level_scratch(COARSE_ROWS)
     return pl.pallas_call(
         coarse_kernel, out_shape=jax.ShapeDtypeStruct((1, 1, 4, 8000), F32),
@@ -370,13 +393,13 @@
     columns = [fine_source, near(fine_source, "gx"), far(fine_source, "gx"),
                near(fine_source, "gy"), far(fine_source, "gy"), corner(fine_source)]
     built = build(fine_blocks, coarse_blocks, child_filter_matrices)
-    along_x, along_y, parent = source(columns, *built[8:11])
+    along_x, along_y, parent = source(columns, *built[6:9])
     x_far, y_far = far(parent, "gx"), far(parent, "gy")
     first = fine_first(along_x, along_y, built[0])
     x_far, y_far, first = lax.optimization_barrier((x_far, y_far, first))
-    fine_term = fine_rest(first, built[1:4])
+    fine_term = fine_rest(first, built[1:3])
     parents = [parent, x_far, near(x_far, "gx"), y_far, near(y_far, "gy")]
-    return coarse(parents, built[4:8], *built[11:14], fine_term)
+    return coarse(parents, built[3:6], *built[9:12], fine_term)
 
 
 def solution(mesh):

time: 44.8 us -> 39.8 us (0.89)
  the two profiles are of different devices: /device:TPU:92 before, /device:TPU:162 now
where the time goes in v2:
time: 39.8 us; the launch traced here: 39.6 us
  starting transfers between devices  15.2 us (38%)
  Pallas kernels  12.8 us (32%)
  waiting for transfers between devices  11.5 us (29%)
    ppermute x4, starting transfers between devices, far(): lax.ppermute(block, axis, [(i, (i + 1 ^ 1) - 1) for i in range(1, count -...  11.9 us
    ppermute x4, waiting for transfers between devices, far(): lax.ppermute(block, axis, [(i, (i + 1 ^ 1) - 1) for i in range(1, count -...  9.15 us
    pallas_call x1, Pallas kernels, build(): pl.pallas_call(build_kernel, out_shape=out_shape, name='build', in_specs=...  4.06 us
    pallas_call x1, Pallas kernels, coarse(): pl.pallas_call(coarse_kernel, out_shape=jax.ShapeDtypeStruct((1, 1, 4, 80...  3.93 us
    ppermute x4, waiting for transfers between devices, near(): lax.ppermute(block, axis, [(i, i ^ 1) for i in range(lax.axis_size(axis))])  2.38 us
    pallas_call x1, Pallas kernels, fine_rest(): pl.pallas_call(fine_rest_kernel, out_shape=jax.ShapeDtypeStruct((4 * FINE...  1.76 us
    ppermute x4, starting transfers between devices, near(): lax.ppermute(block, axis, [(i, i ^ 1) for i in range(lax.axis_size(axis))])  1.67 us
    ppermute x1, starting transfers between devices, corner(): return lax.ppermute(block, ('gx', 'gy'), route)  1.65 us
  transfers between devices with their start and end apart: 9, of which 3 were waited for; matrix products, arithmetic and copies ran while one was open for 0% of the time, Pallas kernels for 19%

profile of v2, /device:TPU:162, one launch (start us, length us, event | category | flops | bytes accessed | tf_op | source)
XLA Modules:
  0.0 39.6 jit_solution(8863013070488544817)
XLA Ops:
  0.0 0.0 collective-permute-start
  0.0 3.0 %collective-permute-start.1 = (bf16[1,1,4,8000]{3,2,1,0:T(4,128)(2,1)}, bf16[1,1,4,8000]{3,2,1,0:T(4,128)(2,1)S(1)}, u32[]{:S(2)}, u32[]{:S(2)}) collective-permute-start(bf16[1,1,4,8000]{3,2,1,0:T(4,128)(2,1)} %own.1), channel_id=1, source_target_pairs={{16,32},{32,16},{48,64},{64,48},{80,96},{96,80},{112,128},{128,112... | collective-permute-start | bytes 192008 | tf_op jit(solution)/shard_map/ppermute | solution.py:383
  3.0 1.7 %collective-permute-start.2 = (bf16[1,1,4,8000]{3,2,1,0:T(4,128)(2,1)}, bf16[1,1,4,8000]{3,2,1,0:T(4,128)(2,1)S(1)}, u32[]{:S(2)}, u32[]{:S(2)}) collective-permute-start(bf16[1,1,4,8000]{3,2,1,0:T(4,128)(2,1)} %own.1), channel_id=1, source_target_pairs={{0,1},{1,0},{2,3},{3,2},{4,5},{5,4},{6,7},{7,6},{8,9},{9,8},{10,11... | collective-permute-start | bytes 192008 | tf_op jit(solution)/shard_map/ppermute | solution.py:378
  4.7 3.2 %collective-permute-start.3 = (bf16[1,1,4,8000]{3,2,1,0:T(4,128)(2,1)}, bf16[1,1,4,8000]{3,2,1,0:T(4,128)(2,1)S(1)}, u32[]{:S(2)}, u32[]{:S(2)}) collective-permute-start(bf16[1,1,4,8000]{3,2,1,0:T(4,128)(2,1)} %own.1), channel_id=1, source_target_pairs={{1,2},{2,1},{3,4},{4,3},{5,6},{6,5},{7,8},{8,7},{9,10},{10,9},{11,... | collective-permute-start | bytes 192008 | tf_op jit(solution)/shard_map/ppermute | solution.py:383
  7.9 1.7 %collective-permute-start.4 = (bf16[1,1,4,8000]{3,2,1,0:T(4,128)(2,1)}, bf16[1,1,4,8000]{3,2,1,0:T(4,128)(2,1)S(1)}, u32[]{:S(2)}, u32[]{:S(2)}) collective-permute-start(bf16[1,1,4,8000]{3,2,1,0:T(4,128)(2,1)} %own.1), channel_id=1, source_target_pairs={{0,17},{1,16},{2,19},{3,18},{4,21},{5,20},{6,23},{7,22},{8,25},{9,... | collective-permute-start | bytes 192008 | tf_op jit(solution)/shard_map/ppermute | solution.py:389
  9.5 4.1 %build.1 = (bf16[12,2,80,128]{3,2,1,0:T(8,128)(2,1)S(1)}, bf16[12,3,128,128]{3,2,1,0:T(8,128)(2,1)S(1)}, bf16[3,12,128,128]{3,2,1,0:T(8,128)(2,1)S(1)}, bf16[12,...) custom-call(bf16[3,12,20,20]{3,2,1,0:T(8,128)(2,1)} %fine_hbm.1, ...), custom_call_target="tpu_custom_call" | custom-call | flops 4000000000 | bytes 10000000 | tf_op jit(solution)/shard_map/build/pallas_call | solution.py:183
  13.6 0.0 collective-permute-done.xnear
  13.6 0.0 collective-permute-done.1.xfar
  13.6 0.0 collective-permute-done.2.ynear
  13.6 2.9 %collective-permute-done.3.yfar = bf16[1,1,4,8000]{3,2,1,0:T(4,128)(2,1)S(1)} collective-permute-done((bf16[1,1,4,8000]{3,2,1,0:T(4,128)(2,1)}, bf16[1,1,4,8000]{3,2,1,0:T(4,128)(2,1)S(1)}, u32[]{:S(2)}, u32[]{:S(2)}) %collective-permute-start.3) | collective-permute-done | bytes 64032 | tf_op jit(solution)/shard_map/ppermute | solution.py:383
  16.5 0.0 collective-permute-done.4.corner
  16.5 0.0 copy-done
  16.5 1.5 %source.1 = (bf16[240,512]{1,0:T(8,128)(2,1)S(1)}, bf16[80,1536]{1,0:T(8,128)(2,1)S(1)}, bf16[48,512]{1,0:T(8,128)(2,1)S(1)}) custom-call(bf16[1,1,4,8000]{3,2,1,0:T(4,128)(2,1)S(1)} %copy-done, bf16[1,1,4,8000]{3,2,1,0:T(4,128)(2,1)S(1)} %collective-permute-done.xnear, bf16[1,1,4,8000]{3,2,1,0:T(4,128)(2,1)S(1)} %collective-permute-done.1.xfar, ...), custom_call_target="tpu_custom_call" | custom-call | flops 1000000000 | bytes 1000000 | tf_op jit(solution)/shard_map/source/pallas_call | solution.py:251
  18.0 1.9 %collective-permute-start.5 = (bf16[48,512]{1,0:T(8,128)(2,1)S(1)}, bf16[48,512]{1,0:T(8,128)(2,1)S(1)}, u32[]{:S(2)}, u32[]{:S(2)}) collective-permute-start(bf16[48,512]{1,0:T(8,128)(2,1)S(1)} %get-tuple-element.26.own), channel_id=1, source_target_pairs={{16,32},{32,16},{48,64},{64,48},{80,96},{96,80},{112,128},{128,112... | collective-permute-start | bytes 147464 | tf_op jit(solution)/shard_map/ppermute | solution.py:383
  20.0 3.8 %collective-permute-start.6 = (bf16[48,512]{1,0:T(8,128)(2,1)S(1)}, bf16[48,512]{1,0:T(8,128)(2,1)S(1)}, u32[]{:S(2)}, u32[]{:S(2)}) collective-permute-start(bf16[48,512]{1,0:T(8,128)(2,1)S(1)} %get-tuple-element.26.own), channel_id=1, source_target_pairs={{1,2},{2,1},{3,4},{4,3},{5,6},{6,5},{7,8},{8,7},{9,10},{10,9},{11,... | collective-permute-start | bytes 147464 | tf_op jit(solution)/shard_map/ppermute | solution.py:383
  23.8 1.5 %fine_first.1.first = bf16[12,4,320,128]{3,2,1,0:T(8,128)(2,1)S(1)} custom-call(bf16[240,512]{1,0:T(8,128)(2,1)S(1)} %get-tuple-element.27.along_x, bf16[80,1536]{1,0:T(8,128)(2,1)S(1)} %get-tuple-element.28.along_y, bf16[12,2,80,128]{3,2,1,0:T(8,128)(2,1)S(1)} %get-tuple-element.29.row_mats), custom_call_target="tpu_custom_call" | custom-call | flops 2000000000 | bytes 10000000 | tf_op jit(solution)/shard_map/fine_first/pallas_call | solution.py:304
  25.3 0.0 collective-permute-done.5.xfar
  25.3 6.2 %collective-permute-done.6.yfar = bf16[48,512]{1,0:T(8,128)(2,1)S(1)} collective-permute-done((bf16[48,512]{1,0:T(8,128)(2,1)S(1)}, bf16[48,512]{1,0:T(8,128)(2,1)S(1)}, u32[]{:S(2)}, u32[]{:S(2)}) %collective-permute-start.6) | collective-permute-done | bytes 49184 | tf_op jit(solution)/shard_map/ppermute | solution.py:383
  31.5 0.0 collective-permute-start.7
  31.5 0.0 collective-permute-start.8
  31.5 1.8 %fine_rest.1.fine_term = f32[320,128]{1,0:T(8,128)S(1)} custom-call(bf16[12,4,320,128]{3,2,1,0:T(8,128)(2,1)S(1)} %fine_first.1.first, bf16[12,3,128,128]{3,2,1,0:T(8,128)(2,1)S(1)} %get-tuple-element.39.y_mats, bf16[3,12,128,128]{3,2,1,0:T(8,128)(2,1)S(1)} %get-tuple-element.40.z_mats), custom_call_target="tpu_custom_call" | custom-call | flops 4000000000 | bytes 10000000 | tf_op jit(solution)/shard_map/fine_rest/pallas_call | solution.py:316
  33.3 0.0 collective-permute-done.7.xother
  33.3 2.4 %collective-permute-done.8.yother = bf16[48,512]{1,0:T(8,128)(2,1)S(1)} collective-permute-done((bf16[48,512]{1,0:T(8,128)(2,1)S(1)}, bf16[48,512]{1,0:T(8,128)(2,1)S(1)}, u32[]{:S(2)}, u32[]{:S(2)}) %collective-permute-start.8) | collective-permute-done | bytes 49184 | tf_op jit(solution)/shard_map/ppermute | solution.py:378
  35.7 3.9 %coarse.1 = f32[1,1,4,8000]{3,2,1,0:T(4,128)} custom-call(bf16[48,512]{1,0:T(8,128)(2,1)S(1)} %get-tuple-element.26.own, bf16[48,512]{1,0:T(8,128)(2,1)S(1)} %collective-permute-done.5.xfar, bf16[48,512]{1,0:T(8,128)(2,1)S(1)} %collective-permute-done.7.xother, bf16[48,512]{1,0:T(8,128)(2,1)S(1)} %collective-permute-done.6.yfar, ...), custom_call_target="tpu_custom_call" | custom-call | flops 4000000000 | bytes 10000000 | tf_op jit(solution)/shard_map/coarse/pallas_call | solution.py:369
  (1 shorter events, 0.0 us)
Async XLA Ops:
  0.0 13.6 %collective-permute-start = (bf16[1,1,4,8000]{3,2,1,0:T(4,128)(2,1)}, bf16[1,1,4,8000]{3,2,1,0:T(4,128)(2,1)S(1)}, u32[]{:S(2)}, u32[]{:S(2)}) collective-permute-start(bf16[1,1,4,8000]{3,2,1,0:T(4,128)(2,1)} %own.1), channel_id=1, source_target_pairs={{0,16},{16,0},{32,48},{48,32},{64,80},{80,64},{96,112},{112,96},{1... | collective-permute-start | bytes 192008 | tf_op jit(solution)/shard_map/ppermute | solution.py:378
  0.0 13.6 %collective-permute-start.1 = (bf16[1,1,4,8000]{3,2,1,0:T(4,128)(2,1)}, bf16[1,1,4,8000]{3,2,1,0:T(4,128)(2,1)S(1)}, u32[]{:S(2)}, u32[]{:S(2)}) collective-permute-start(bf16[1,1,4,8000]{3,2,1,0:T(4,128)(2,1)} %own.1), channel_id=1, source_target_pairs={{16,32},{32,16},{48,64},{64,48},{80,96},{96,80},{112,128},{128,112... | collective-permute-start | bytes 192008 | tf_op jit(solution)/shard_map/ppermute | solution.py:383
  3.0 10.6 %collective-permute-start.2 = (bf16[1,1,4,8000]{3,2,1,0:T(4,128)(2,1)}, bf16[1,1,4,8000]{3,2,1,0:T(4,128)(2,1)S(1)}, u32[]{:S(2)}, u32[]{:S(2)}) collective-permute-start(bf16[1,1,4,8000]{3,2,1,0:T(4,128)(2,1)} %own.1), channel_id=1, source_target_pairs={{0,1},{1,0},{2,3},{3,2},{4,5},{5,4},{6,7},{7,6},{8,9},{9,8},{10,11... | collective-permute-start | bytes 192008 | tf_op jit(solution)/shard_map/ppermute | solution.py:378
  4.7 11.8 %collective-permute-start.3 = (bf16[1,1,4,8000]{3,2,1,0:T(4,128)(2,1)}, bf16[1,1,4,8000]{3,2,1,0:T(4,128)(2,1)S(1)}, u32[]{:S(2)}, u32[]{:S(2)}) collective-permute-start(bf16[1,1,4,8000]{3,2,1,0:T(4,128)(2,1)} %own.1), channel_id=1, source_target_pairs={{1,2},{2,1},{3,4},{4,3},{5,6},{6,5},{7,8},{8,7},{9,10},{10,9},{11,... | collective-permute-start | bytes 192008 | tf_op jit(solution)/shard_map/ppermute | solution.py:383
  7.9 8.7 %collective-permute-start.4 = (bf16[1,1,4,8000]{3,2,1,0:T(4,128)(2,1)}, bf16[1,1,4,8000]{3,2,1,0:T(4,128)(2,1)S(1)}, u32[]{:S(2)}, u32[]{:S(2)}) collective-permute-start(bf16[1,1,4,8000]{3,2,1,0:T(4,128)(2,1)} %own.1), channel_id=1, source_target_pairs={{0,17},{1,16},{2,19},{3,18},{4,21},{5,20},{6,23},{7,22},{8,25},{9,... | collective-permute-start | bytes 192008 | tf_op jit(solution)/shard_map/ppermute | solution.py:389
  9.5 7.0 %copy-start = (bf16[1,1,4,8000]{3,2,1,0:T(4,128)(2,1)S(1)}, bf16[1,1,4,8000]{3,2,1,0:T(4,128)(2,1)}, u32[]{:S(2)}) copy-start(bf16[1,1,4,8000]{3,2,1,0:T(4,128)(2,1)} %own.1) | copy-start | bytes 192004
  18.0 7.3 %collective-permute-start.5 = (bf16[48,512]{1,0:T(8,128)(2,1)S(1)}, bf16[48,512]{1,0:T(8,128)(2,1)S(1)}, u32[]{:S(2)}, u32[]{:S(2)}) collective-permute-start(bf16[48,512]{1,0:T(8,128)(2,1)S(1)} %get-tuple-element.26.own), channel_id=1, source_target_pairs={{16,32},{32,16},{48,64},{64,48},{80,96},{96,80},{112,128},{128,112... | collective-permute-start | bytes 147464 | tf_op jit(solution)/shard_map/ppermute | solution.py:383
  20.0 11.6 %collective-permute-start.6 = (bf16[48,512]{1,0:T(8,128)(2,1)S(1)}, bf16[48,512]{1,0:T(8,128)(2,1)S(1)}, u32[]{:S(2)}, u32[]{:S(2)}) collective-permute-start(bf16[48,512]{1,0:T(8,128)(2,1)S(1)} %get-tuple-element.26.own), channel_id=1, source_target_pairs={{1,2},{2,1},{3,4},{4,3},{5,6},{6,5},{7,8},{8,7},{9,10},{10,9},{11,... | collective-permute-start | bytes 147464 | tf_op jit(solution)/shard_map/ppermute | solution.py:383
  31.5 1.8 %collective-permute-start.7 = (bf16[48,512]{1,0:T(8,128)(2,1)S(1)}, bf16[48,512]{1,0:T(8,128)(2,1)S(1)}, u32[]{:S(2)}, u32[]{:S(2)}) collective-permute-start(bf16[48,512]{1,0:T(8,128)(2,1)S(1)} %collective-permute-done.5.xfar), channel_id=1, source_target_pairs={{0,16},{16,0},{32,48},{48,32},{64,80},{80,64},{96,112},{112,96},{1... | collective-permute-start | bytes 147464 | tf_op jit(solution)/shard_map/ppermute | solution.py:378
  31.5 4.2 %collective-permute-start.8 = (bf16[48,512]{1,0:T(8,128)(2,1)S(1)}, bf16[48,512]{1,0:T(8,128)(2,1)S(1)}, u32[]{:S(2)}, u32[]{:S(2)}) collective-permute-start(bf16[48,512]{1,0:T(8,128)(2,1)S(1)} %collective-permute-done.6.yfar), channel_id=1, source_target_pairs={{0,1},{1,0},{2,3},{3,2},{4,5},{5,4},{6,7},{7,6},{8,9},{9,8},{10,11... | collective-permute-start | bytes 147464 | tf_op jit(solution)/shard_map/ppermute | solution.py:378

commit v3 on v2

--- a/solution.py
+++ b/solution.py
@@ -198,8 +198,8 @@
     ))
 
 
-def source_kernel(own, xnear, xfar, ynear, yfar, corner, down_rows, down_y, down_z,
-                  along_x, along_y, parent, natural, pair, mixed, turned):
+def source_kernel(own, xnear, ynear, corner, down_rows, down_y, down_z,
+                  packet, nears, natural, mixed, turned):
     select = onehot(iota((400, 512), 0) == natural_place(iota((1, 512), 1), True))
 
     def converted(ref, slot):
@@ -208,45 +208,37 @@
             natural[slot, 4 * i:4 * i + 4, :] = values[:, 400 * i:400 * i + 400]
         return dot(natural[slot].astype(BF), select).astype(BF)
 
-    centre = converted(own, 0)
-    x_near, y_near = converted(xnear, 1), converted(ynear, 2)
-    diagonal = converted(corner, 3)
-    along_x[0:80, :] = centre
-    along_x[80:160, :] = x_near
-    along_x[160:240, :] = converted(xfar, 4)
-    along_y[:, 0:512] = centre
-    along_y[:, 512:1024] = y_near
-    along_y[:, 1024:1536] = converted(yfar, 5)
-    pair[0:80, 0:512] = centre
-    pair[80:160, 0:512] = x_near
-    pair[0:80, 512:1024] = y_near
-    pair[80:160, 512:1024] = diagonal
-    rows = dot(down_rows[...], pair[...]).astype(BF)
+    centre, diagonal = converted(own, 0), converted(corner, 1)
+    x_near, y_near = converted(xnear, 2), converted(ynear, 3)
+    for b in range(4):
+        here = slice(128 * b, 128 * b + 128)
+        packet[b, 0:80, :] = centre[:, here]
+        nears[0, b] = x_near[:, here]
+        nears[1, b] = y_near[:, here]
+    for c, (one, two) in enumerate(((centre, x_near), (y_near, diagonal))):
+        rows = dot(down_rows[...], jnp.concatenate([one, two], axis=0)).astype(BF)
+        for b in range(4):
+            mixed[c, 96 * b:96 * b + 96, :] = rows[:, 128 * b:128 * b + 128]
+    summed = dot(jnp.concatenate([mixed[0], mixed[1]], axis=1), down_y[...])
+    blocks = exchange([summed[96 * b:96 * b + 96, :] for b in range(4)])
     for b in range(4):
         for c in range(2):
-            mixed[96 * b:96 * b + 96, 128 * c:128 * c + 128] = rows[:, 512 * c + 128 * b:512 * c + 128 * b + 128]
-    summed = dot(mixed[...], down_y[...])
-    blocks = exchange([summed[96 * b:96 * b + 96, :] for b in range(4)])
-    for b in range(4):
-        for c in range(2):
-            turned[48 * b:48 * b + 48, 128 * c:128 * c + 128] = blocks[b][48 * c:48 * c + 48, :].astype(BF)
-    total = dot(turned[...], down_z[...])
+            turned[c, 48 * b:48 * b + 48, :] = blocks[b][48 * c:48 * c + 48, :].astype(BF)
+    total = dot(jnp.concatenate([turned[0], turned[1]], axis=1), down_z[...])
     blocks = exchange([total[48 * b:48 * b + 48, :] for b in range(4)])
     for b in range(4):
-        parent[:, 128 * b:128 * b + 128] = blocks[b].astype(BF)
+        packet[b, 80:128, :] = blocks[b].astype(BF)
 
 
 def source(columns, down_rows, down_y, down_z):
     out_shape = (
-        jax.ShapeDtypeStruct((3 * FINE_ROWS, 512), BF),
-        jax.ShapeDtypeStruct((FINE_ROWS, 1536), BF),
-        jax.ShapeDtypeStruct((COARSE_ROWS, 512), BF),
+        jax.ShapeDtypeStruct((4, FINE_ROWS + COARSE_ROWS, 128), BF),
+        jax.ShapeDtypeStruct((2, 4, FINE_ROWS, 128), BF),
     )
     scratch = [
-        pltpu.VMEM((6, FINE_ROWS, 400), F32),
-        pltpu.VMEM((2 * FINE_ROWS, 1024), BF),
-        pltpu.VMEM((8 * COARSE_ROWS, 256), BF),
-        pltpu.VMEM((4 * COARSE_ROWS, 256), BF),
+        pltpu.VMEM((4, FINE_ROWS, 400), F32),
+        pltpu.VMEM((2, 8 * COARSE_ROWS, 128), BF),
+        pltpu.VMEM((2, 4 * COARSE_ROWS, 128), BF),
     ]
     return pl.pallas_call(
         source_kernel, out_shape=out_shape, scratch_shapes=scratch, name="source",
@@ -255,26 +247,29 @@
     )(*columns, down_rows, down_y, down_z)
 
 
-def level_first(rows, along_x, along_y, row_mats, first):
+def joined(blocks):
+    return jnp.concatenate(blocks, axis=1)
+
+
+def row_pass(rows, row_mats, stacks, targets):
+    stacks = [[joined(column) for column in stack] for stack in stacks]
+    stacks = [stack[0] if len(stack) == 1 else jnp.concatenate(stack, axis=0) for stack in stacks]
     for m in range(TERMS):
-        mats = jnp.concatenate([row_mats[m, 0], row_mats[m, 1]], axis=1)[:, 0:3 * rows]
-        both = dot(mats, along_x)
-        sides = dot(mats[:, 0:rows], along_y)
-        for b in range(4):
-            here = pl.ds(b * rows, rows)
-            first[m, 0, here, :] = both[:, 128 * b:128 * b + 128].astype(BF)
-            for part, start in ((1, 512), (2, 1024), (3, 0)):
-                first[m, part, here, :] = sides[:, start + 128 * b:start + 128 * b + 128].astype(BF)
-
-
-def level_rest(rows, nz, first, y_mats, z_mats, sums, centres):
+        mats = jnp.concatenate([row_mats[m, 0], row_mats[m, 1]], axis=1)
+        for stack, target in zip(stacks, targets):
+            result = dot(mats[:, 0:stack.shape[0]], stack)
+            for b in range(4):
+                target[m, b * rows:b * rows + rows, :] = result[:, 128 * b:128 * b + 128].astype(BF)
+
+
+def level_rest(rows, nz, parts, y_mats, z_mats, sums, centres):
     zero = jnp.zeros((128, 128), BF)
     for m in range(TERMS):
         mats = jnp.concatenate([
             jnp.concatenate([y_mats[m, 0], y_mats[m, 1], y_mats[m, 2], zero], axis=0),
             jnp.concatenate([zero, zero, zero, y_mats[m, 0]], axis=0),
         ], axis=1)
-        result = dot(jnp.concatenate([first[m, part] for part in range(4)], axis=1), mats)
+        result = dot(jnp.concatenate([part[m] for part in parts], axis=1), mats)
         for n, target in enumerate((sums, centres)):
             blocks = exchange([result[b * rows:(b + 1) * rows, 128 * n:128 * n + 128] for b in range(4)])
             for b in range(4):
@@ -296,41 +291,41 @@
     ]
 
 
-def fine_first_kernel(along_x, along_y, row_mats, first):
-    level_first(FINE_ROWS, along_x[...], along_y[...], row_mats, first)
-
-
-def fine_first(along_x, along_y, row_mats):
+def fine_near_kernel(packet, nears, row_mats, y_near, centre):
+    own = [packet[b, 0:80, :] for b in range(4)]
+    row_pass(FINE_ROWS, row_mats, ([[nears[1, b] for b in range(4)]], [own]), (y_near, centre))
+
+
+def fine_far_kernel(packet, nears, x_packet, y_packet, row_mats, x_sum, y_far, x_parent, y_parent):
+    for b in range(4):
+        x_parent[b] = x_packet[b, 80:128, :]
+        y_parent[b] = y_packet[b, 80:128, :]
+    own, x_far, y_column = ([ref[b, 0:80, :] for b in range(4)] for ref in (packet, x_packet, y_packet))
+    stacks = ([own, [nears[0, b] for b in range(4)], x_far], [y_column])
+    row_pass(FINE_ROWS, row_mats, stacks, (x_sum, y_far))
+
+
+def fine_rest_kernel(x_sum, y_near, y_far, centre, y_mats, z_mats, out, sums, centres):
+    out[...] = level_rest(FINE_ROWS, 4, (x_sum, y_near, y_far, centre), y_mats, z_mats, sums, centres)
+
+
+def small_call(kernel, name, out_shape, flops, *operands, scratch=()):
     return pl.pallas_call(
-        fine_first_kernel, out_shape=jax.ShapeDtypeStruct((TERMS, 4, 4 * FINE_ROWS, 128), BF), name="fine_first",
+        kernel, out_shape=out_shape, name=name, scratch_shapes=scratch,
         compiler_params=pltpu.CompilerParams(vmem_limit_bytes=16 << 20),
-        cost_estimate=pl.CostEstimate(flops=2 * 10**9, bytes_accessed=10 * 10**6, transcendentals=0),
-    )(along_x, along_y, row_mats)
-
-
-def fine_rest_kernel(first, y_mats, z_mats, out, sums, centres):
-    out[...] = level_rest(FINE_ROWS, 4, first, y_mats, z_mats, sums, centres)
-
-
-def fine_rest(first, mats):
-    return pl.pallas_call(
-        fine_rest_kernel, out_shape=jax.ShapeDtypeStruct((4 * FINE_ROWS, 128), F32),
-        scratch_shapes=level_scratch(FINE_ROWS), name="fine_rest",
-        compiler_params=pltpu.CompilerParams(vmem_limit_bytes=16 << 20),
-        cost_estimate=pl.CostEstimate(flops=4 * 10**9, bytes_accessed=10 * 10**6, transcendentals=0),
-    )(first, *mats)
-
-
-def coarse_kernel(own, xfar, xother, yfar, yother, row_mats, y_mats, z_mats,
-                  up_rows, up_y, up_z, fine_term, out, along_x, along_y, wide, grown, turned, split, first, *scratch):
-    along_x[0:48, :] = own[...]
-    along_x[48:96, :] = xfar[...]
-    along_x[96:144, :] = xother[...]
-    along_y[:, 0:512] = own[...]
-    along_y[:, 512:1024] = yfar[...]
-    along_y[:, 1024:1536] = yother[...]
-    level_first(COARSE_ROWS, along_x[...], along_y[...], row_mats, first)
-    result = level_rest(COARSE_ROWS, 2, first, y_mats, z_mats, *scratch)
+        cost_estimate=pl.CostEstimate(flops=flops, bytes_accessed=4 * 10**6, transcendentals=0),
+    )(*operands)
+
+
+def coarse_kernel(packet, xfar, xother, yfar, yother, row_mats, y_mats, z_mats,
+                  up_rows, up_y, up_z, fine_term, out, wide, grown, turned, split,
+                  x_sum, far_side, other_side, centre, *scratch):
+    own = [packet[b, 80:128, :] for b in range(4)]
+    others = [[ref[b] for b in range(4)] for ref in (xfar, xother, yfar, yother)]
+    stacks = ([own, others[0], others[1]], [others[2]], [others[3]], [own])
+    parts = (x_sum, far_side, other_side, centre)
+    row_pass(COARSE_ROWS, row_mats, stacks, parts)
+    result = level_rest(COARSE_ROWS, 2, parts, y_mats, z_mats, *scratch)
     blocks = exchange([result[48 * b:48 * b + 48, :] for b in range(4)])
     for b in range(4):
         wide[:, 128 * b:128 * b + 128] = blocks[b].astype(BF)
@@ -356,22 +351,17 @@
         out[0, 0, :, 400 * i:400 * i + 400] = natural[4 * i:4 * i + 4, :]
 
 
-def coarse(parents, mats, up_rows, up_y, up_z, fine_term):
+def coarse(operands):
+    part = pltpu.VMEM((TERMS, 4 * COARSE_ROWS, 128), BF)
     scratch = [
-        pltpu.VMEM((3 * COARSE_ROWS, 512), BF),
-        pltpu.VMEM((COARSE_ROWS, 1536), BF),
         pltpu.VMEM((COARSE_ROWS, 512), BF),
         pltpu.VMEM((320, 128), BF),
         pltpu.VMEM((320, 128), BF),
         pltpu.VMEM((160, 512), BF),
-        pltpu.VMEM((TERMS, 4, 4 * COARSE_ROWS, 128), BF),
-    ] + level_scratch(COARSE_ROWS)
-    return pl.pallas_call(
-        coarse_kernel, out_shape=jax.ShapeDtypeStruct((1, 1, 4, 8000), F32),
-        scratch_shapes=scratch, name="coarse",
-        compiler_params=pltpu.CompilerParams(vmem_limit_bytes=32 << 20),
-        cost_estimate=pl.CostEstimate(flops=4 * 10**9, bytes_accessed=10 * 10**6, transcendentals=0),
-    )(*parents, *mats, up_rows, up_y, up_z, fine_term)
+    ] + [part] * 4 + level_scratch(COARSE_ROWS)
+    return small_call(
+        coarse_kernel, "coarse", jax.ShapeDtypeStruct((1, 1, 4, 8000), F32), 4 * 10**9, *operands, scratch=scratch
+    )
 
 
 def near(block, axis):
@@ -390,16 +380,23 @@
 
 
 def shards(fine_source, fine_blocks, coarse_blocks, child_filter_matrices):
-    columns = [fine_source, near(fine_source, "gx"), far(fine_source, "gx"),
-               near(fine_source, "gy"), far(fine_source, "gy"), corner(fine_source)]
+    columns = [fine_source, near(fine_source, "gx"), near(fine_source, "gy"), corner(fine_source)]
     built = build(fine_blocks, coarse_blocks, child_filter_matrices)
-    along_x, along_y, parent = source(columns, *built[6:9])
-    x_far, y_far = far(parent, "gx"), far(parent, "gy")
-    first = fine_first(along_x, along_y, built[0])
-    x_far, y_far, first = lax.optimization_barrier((x_far, y_far, first))
-    fine_term = fine_rest(first, built[1:3])
-    parents = [parent, x_far, near(x_far, "gx"), y_far, near(y_far, "gy")]
-    return coarse(parents, built[3:6], *built[9:12], fine_term)
+    packet, nears = source(columns, *built[6:9])
+    x_packet, y_packet = far(packet, "gx"), far(packet, "gy")
+    part = jax.ShapeDtypeStruct((TERMS, 4 * FINE_ROWS, 128), BF)
+    parent = jax.ShapeDtypeStruct((4, COARSE_ROWS, 128), BF)
+    y_near, centre = small_call(fine_near_kernel, "fine_near", (part, part), 10**9, packet, nears, built[0])
+    x_sum, y_far, x_parent, y_parent = small_call(
+        fine_far_kernel, "fine_far", (part, part, parent, parent), 10**9,
+        packet, nears, x_packet, y_packet, built[0],
+    )
+    x_other, y_other = near(x_parent, "gx"), near(y_parent, "gy")
+    fine_term = small_call(
+        fine_rest_kernel, "fine_rest", jax.ShapeDtypeStruct((4 * FINE_ROWS, 128), F32), 4 * 10**9,
+        x_sum, y_near, y_far, centre, *built[1:3], scratch=level_scratch(FINE_ROWS),
+    )
+    return coarse((packet, x_parent, x_other, y_parent, y_other, *built[3:6], *built[9:12], fine_term))
 
 
 def solution(mesh):

time: 39.8 us -> 32.5 us (0.82)
  the two profiles are of different devices: /device:TPU:162 before, /device:TPU:130 now
where the time goes in v3:
time: 32.5 us; the launch traced here: 31.9 us
  Pallas kernels  12.5 us (38%)
  waiting for transfers between devices  9.66 us (30%)
  starting transfers between devices  9.64 us (30%)
    ppermute x2, waiting for transfers between devices, far(): lax.ppermute(block, axis, [(i, (i + 1 ^ 1) - 1) for i in range(1, count -...  7.31 us
    ppermute x2, starting transfers between devices, far(): lax.ppermute(block, axis, [(i, (i + 1 ^ 1) - 1) for i in range(1, count -...  7.14 us
    pallas_call x4, Pallas kernels, small_call(): pl.pallas_call(kernel, out_shape=out_shape, name=name, scratch_shapes=scr...  7.09 us
    pallas_call x1, Pallas kernels, build(): pl.pallas_call(build_kernel, out_shape=out_shape, name='build', in_specs=...  4.06 us
    ppermute x4, waiting for transfers between devices, near(): lax.ppermute(block, axis, [(i, i ^ 1) for i in range(lax.axis_size(axis))])  2.34 us
    ppermute x4, starting transfers between devices, near(): lax.ppermute(block, axis, [(i, i ^ 1) for i in range(lax.axis_size(axis))])  1.95 us
    pallas_call x1, Pallas kernels, source(): pl.pallas_call(source_kernel, out_shape=out_shape, scratch_shapes=scratch...  1.38 us
  transfers between devices with their start and end apart: 7, of which 2 were waited for; matrix products, arithmetic and copies ran while one was open for 0% of the time, Pallas kernels for 20%

profile of v3, /device:TPU:130, one launch (start us, length us, event | category | flops | bytes accessed | tf_op | source)
XLA Modules:
  0.0 31.9 jit_solution(9489791090971307078)
XLA Ops:
  0.0 1.6 %collective-permute-start.1 = (bf16[1,1,4,8000]{3,2,1,0:T(4,128)(2,1)}, bf16[1,1,4,8000]{3,2,1,0:T(4,128)(2,1)S(1)}, u32[]{:S(2)}, u32[]{:S(2)}) collective-permute-start(bf16[1,1,4,8000]{3,2,1,0:T(4,128)(2,1)} %own.1), channel_id=1, source_target_pairs={{0,1},{1,0},{2,3},{3,2},{4,5},{5,4},{6,7},{7,6},{8,9},{9,8},{10,11... | collective-permute-start | bytes 192008 | tf_op jit(solution)/shard_map/ppermute | solution.py:368
  1.6 0.0 collective-permute-start
  1.6 0.6 %collective-permute-start.2 = (bf16[1,1,4,8000]{3,2,1,0:T(4,128)(2,1)}, bf16[1,1,4,8000]{3,2,1,0:T(4,128)(2,1)S(1)}, u32[]{:S(2)}, u32[]{:S(2)}) collective-permute-start(bf16[1,1,4,8000]{3,2,1,0:T(4,128)(2,1)} %own.1), channel_id=1, source_target_pairs={{0,17},{1,16},{2,19},{3,18},{4,21},{5,20},{6,23},{7,22},{8,25},{9,... | collective-permute-start | bytes 192008 | tf_op jit(solution)/shard_map/ppermute | solution.py:379
  2.1 0.0 copy-start
  2.1 4.1 %build.1 = (bf16[12,2,80,128]{3,2,1,0:T(8,128)(2,1)S(1)}, bf16[12,3,128,128]{3,2,1,0:T(8,128)(2,1)S(1)}, bf16[3,12,128,128]{3,2,1,0:T(8,128)(2,1)S(1)}, bf16[12,...) custom-call(bf16[3,12,20,20]{3,2,1,0:T(8,128)(2,1)} %fine_hbm.1, ...), custom_call_target="tpu_custom_call" | custom-call | flops 4000000000 | bytes 10000000 | tf_op jit(solution)/shard_map/build/pallas_call | solution.py:183
  6.2 0.0 collective-permute-done.1.ynear
  6.2 0.0 collective-permute-done.xnear
  6.2 0.0 collective-permute-done.2.corner
  6.2 0.0 copy-done
  6.3 1.4 %source.1 = (bf16[4,128,128]{2,1,0:T(8,128)(2,1)S(1)}, bf16[2,4,80,128]{3,2,1,0:T(8,128)(2,1)S(1)}) custom-call(bf16[1,1,4,8000]{3,2,1,0:T(4,128)(2,1)S(1)} %copy-done, bf16[1,1,4,8000]{3,2,1,0:T(4,128)(2,1)S(1)} %collective-permute-done.xnear, bf16[1,1,4,8000]{3,2,1,0:T(4,128)(2,1)S(1)} %collective-permute-done.1.ynear, ...), custom_call_target="tpu_custom_call" | custom-call | flops 1000000000 | bytes 1000000 | tf_op jit(solution)/shard_map/source/pallas_call | solution.py:243
  7.6 4.0 %collective-permute-start.4 = (bf16[4,128,128]{2,1,0:T(8,128)(2,1)S(1)}, bf16[4,128,128]{2,1,0:T(8,128)(2,1)S(1)}, u32[]{:S(2)}, u32[]{:S(2)}) collective-permute-start(bf16[4,128,128]{2,1,0:T(8,128)(2,1)S(1)} %get-tuple-element.28.packet), channel_id=1, source_target_pairs={{1,2},{2,1},{3,4},{4,3},{5,6},{6,5},{7,8},{8,7},{9,10},{10,9},{11,... | collective-permute-start | bytes 393224 | tf_op jit(solution)/shard_map/ppermute | solution.py:373
  11.7 3.1 %collective-permute-start.3 = (bf16[4,128,128]{2,1,0:T(8,128)(2,1)S(1)}, bf16[4,128,128]{2,1,0:T(8,128)(2,1)S(1)}, u32[]{:S(2)}, u32[]{:S(2)}) collective-permute-start(bf16[4,128,128]{2,1,0:T(8,128)(2,1)S(1)} %get-tuple-element.28.packet), channel_id=1, source_target_pairs={{16,32},{32,16},{48,64},{64,48},{80,96},{96,80},{112,128},{128,112... | collective-permute-start | bytes 393224 | tf_op jit(solution)/shard_map/ppermute | solution.py:373
  14.8 0.6 %fine_near.1 = (bf16[12,320,128]{2,1,0:T(8,128)(2,1)S(1)}, bf16[12,320,128]{2,1,0:T(8,128)(2,1)S(1)}) custom-call(bf16[4,128,128]{2,1,0:T(8,128)(2,1)S(1)} %get-tuple-element.28.packet, bf16[2,4,80,128]{3,2,1,0:T(8,128)(2,1)S(1)} %get-tuple-element.29.nears, bf16[12,2,80,128]{3,2,1,0:T(8,128)(2,1)S(1)} %get-tuple-element.30.row_mats), custom_call_target="tpu_custom_call" | custom-call | flops 1000000000 | bytes 4000000 | tf_op jit(solution)/shard_map/fine_near/pallas_call | solution.py:313
  15.4 7.3 %collective-permute-done.4.y_packet = bf16[4,128,128]{2,1,0:T(8,128)(2,1)S(1)} collective-permute-done((bf16[4,128,128]{2,1,0:T(8,128)(2,1)S(1)}, bf16[4,128,128]{2,1,0:T(8,128)(2,1)S(1)}, u32[]{:S(2)}, u32[]{:S(2)}) %collective-permute-start.4) | collective-permute-done | bytes 131104 | tf_op jit(solution)/shard_map/ppermute | solution.py:373
  22.8 0.0 collective-permute-done.3.x_packet
  22.8 1.0 %fine_far.1 = (bf16[12,320,128]{2,1,0:T(8,128)(2,1)S(1)}, bf16[12,320,128]{2,1,0:T(8,128)(2,1)S(1)}, bf16[4,48,128]{2,1,0:T(8,128)(2,1)S(1)}, bf16[4,48,128]{2,1,0:T(8,128)(2,1)S(1)}) custom-call(bf16[4,128,128]{2,1,0:T(8,128)(2,1)S(1)} %get-tuple-element.28.packet, bf16[2,4,80,128]{3,2,1,0:T(8,128)(2,1)S(1)} %get-tuple-element.29.nears, ...), custom_call_target="tpu_custom_call" | custom-call | flops 1000000000 | bytes 4000000 | tf_op jit(solution)/shard_map/fine_far/pallas_call | solution.py:313
  23.7 0.1 collective-permute-start.5
  23.8 0.3 collective-permute-start.6
  24.1 1.7 %fine_rest.1.fine_term = f32[320,128]{1,0:T(8,128)S(1)} custom-call(bf16[12,320,128]{2,1,0:T(8,128)(2,1)S(1)} %get-tuple-element.39.x_sum, bf16[12,320,128]{2,1,0:T(8,128)(2,1)S(1)} %get-tuple-element.40.y_near, bf16[12,320,128]{2,1,0:T(8,128)(2,1)S(1)} %get-tuple-element.41.y_far, bf16[12,320,128]{2,1,0:T(8,128)(2,1)S(1)} %get-tuple-element.42.centre, ...), custom_call_target="tpu_custom_call" | custom-call | flops 4000000000 | bytes 4000000 | tf_op jit(solution)/shard_map/fine_rest/pallas_call | solution.py:313
  25.8 0.0 collective-permute-done.5.xother
  25.8 2.3 %collective-permute-done.6.yother = bf16[4,48,128]{2,1,0:T(8,128)(2,1)S(1)} collective-permute-done((bf16[4,48,128]{2,1,0:T(8,128)(2,1)S(1)}, bf16[4,48,128]{2,1,0:T(8,128)(2,1)S(1)}, u32[]{:S(2)}, u32[]{:S(2)}) %collective-permute-start.6) | collective-permute-done | bytes 49184 | tf_op jit(solution)/shard_map/ppermute | solution.py:368
  28.2 3.8 %coarse.1 = f32[1,1,4,8000]{3,2,1,0:T(4,128)} custom-call(bf16[4,128,128]{2,1,0:T(8,128)(2,1)S(1)} %get-tuple-element.28.packet, bf16[4,48,128]{2,1,0:T(8,128)(2,1)S(1)} %get-tuple-element.31.xfar, bf16[4,48,128]{2,1,0:T(8,128)(2,1)S(1)} %collective-permute-done.5.xother, bf16[4,48,128]{2,1,0:T(8,128)(2,1)S(1)} %get-tuple-element.32.yfar, ...), custom_call_target="tpu_custom_call" | custom-call | flops 4000000000 | bytes 4000000 | tf_op jit(solution)/shard_map/coarse/pallas_call | solution.py:313
Async XLA Ops:
  0.0 6.2 %collective-permute-start.1 = (bf16[1,1,4,8000]{3,2,1,0:T(4,128)(2,1)}, bf16[1,1,4,8000]{3,2,1,0:T(4,128)(2,1)S(1)}, u32[]{:S(2)}, u32[]{:S(2)}) collective-permute-start(bf16[1,1,4,8000]{3,2,1,0:T(4,128)(2,1)} %own.1), channel_id=1, source_target_pairs={{0,1},{1,0},{2,3},{3,2},{4,5},{5,4},{6,7},{7,6},{8,9},{9,8},{10,11... | collective-permute-start | bytes 192008 | tf_op jit(solution)/shard_map/ppermute | solution.py:368
  1.6 4.6 %collective-permute-start = (bf16[1,1,4,8000]{3,2,1,0:T(4,128)(2,1)}, bf16[1,1,4,8000]{3,2,1,0:T(4,128)(2,1)S(1)}, u32[]{:S(2)}, u32[]{:S(2)}) collective-permute-start(bf16[1,1,4,8000]{3,2,1,0:T(4,128)(2,1)} %own.1), channel_id=1, source_target_pairs={{0,16},{16,0},{32,48},{48,32},{64,80},{80,64},{96,112},{112,96},{1... | collective-permute-start | bytes 192008 | tf_op jit(solution)/shard_map/ppermute | solution.py:368
  1.6 4.7 %collective-permute-start.2 = (bf16[1,1,4,8000]{3,2,1,0:T(4,128)(2,1)}, bf16[1,1,4,8000]{3,2,1,0:T(4,128)(2,1)S(1)}, u32[]{:S(2)}, u32[]{:S(2)}) collective-permute-start(bf16[1,1,4,8000]{3,2,1,0:T(4,128)(2,1)} %own.1), channel_id=1, source_target_pairs={{0,17},{1,16},{2,19},{3,18},{4,21},{5,20},{6,23},{7,22},{8,25},{9,... | collective-permute-start | bytes 192008 | tf_op jit(solution)/shard_map/ppermute | solution.py:379
  2.1 4.1 %copy-start = (bf16[1,1,4,8000]{3,2,1,0:T(4,128)(2,1)S(1)}, bf16[1,1,4,8000]{3,2,1,0:T(4,128)(2,1)}, u32[]{:S(2)}) copy-start(bf16[1,1,4,8000]{3,2,1,0:T(4,128)(2,1)} %own.1) | copy-start | bytes 192004
  7.6 15.1 %collective-permute-start.4 = (bf16[4,128,128]{2,1,0:T(8,128)(2,1)S(1)}, bf16[4,128,128]{2,1,0:T(8,128)(2,1)S(1)}, u32[]{:S(2)}, u32[]{:S(2)}) collective-permute-start(bf16[4,128,128]{2,1,0:T(8,128)(2,1)S(1)} %get-tuple-element.28.packet), channel_id=1, source_target_pairs={{1,2},{2,1},{3,4},{4,3},{5,6},{6,5},{7,8},{8,7},{9,10},{10,9},{11,... | collective-permute-start | bytes 393224 | tf_op jit(solution)/shard_map/ppermute | solution.py:373
  11.7 11.1 %collective-permute-start.3 = (bf16[4,128,128]{2,1,0:T(8,128)(2,1)S(1)}, bf16[4,128,128]{2,1,0:T(8,128)(2,1)S(1)}, u32[]{:S(2)}, u32[]{:S(2)}) collective-permute-start(bf16[4,128,128]{2,1,0:T(8,128)(2,1)S(1)} %get-tuple-element.28.packet), channel_id=1, source_target_pairs={{16,32},{32,16},{48,64},{64,48},{80,96},{96,80},{112,128},{128,112... | collective-permute-start | bytes 393224 | tf_op jit(solution)/shard_map/ppermute | solution.py:373
  23.7 2.1 %collective-permute-start.5 = (bf16[4,48,128]{2,1,0:T(8,128)(2,1)S(1)}, bf16[4,48,128]{2,1,0:T(8,128)(2,1)S(1)}, u32[]{:S(2)}, u32[]{:S(2)}) collective-permute-start(bf16[4,48,128]{2,1,0:T(8,128)(2,1)S(1)} %get-tuple-element.31.xfar), channel_id=1, source_target_pairs={{0,16},{16,0},{32,48},{48,32},{64,80},{80,64},{96,112},{112,96},{1... | collective-permute-start | bytes 147464 | tf_op jit(solution)/shard_map/ppermute | solution.py:368
  23.8 4.4 %collective-permute-start.6 = (bf16[4,48,128]{2,1,0:T(8,128)(2,1)S(1)}, bf16[4,48,128]{2,1,0:T(8,128)(2,1)S(1)}, u32[]{:S(2)}, u32[]{:S(2)}) collective-permute-start(bf16[4,48,128]{2,1,0:T(8,128)(2,1)S(1)} %get-tuple-element.32.yfar), channel_id=1, source_target_pairs={{0,1},{1,0},{2,3},{3,2},{4,5},{5,4},{6,7},{7,6},{8,9},{9,8},{10,11... | collective-permute-start | bytes 147464 | tf_op jit(solution)/shard_map/ppermute | solution.py:368

commit v4 on v3

--- a/solution.py
+++ b/solution.py
@@ -27,18 +27,16 @@
     return piece, jj, t - 5 * jj, t < 25
 
 
-def natural_place(n, y_order):
-    block = n >> 7
+def natural_place(n):
     piece, jj, kk, ok = place(n & 127)
-    j, k = (piece, block) if y_order else (block, piece)
-    return jnp.where(ok, (5 * j + jj) * 20 + 5 * k + kk, -1)
+    return jnp.where(ok, (5 * piece + jj) * 20 + 5 * (n >> 7) + kk, -1)
 
 
 def onehot(condition, dtype=BF):
     return jnp.where(condition, 1.0, 0.0).astype(dtype)
 
 
-def lane_constants(on_j):
+def lane_constants(on_j, natural=False):
     def index(n):
         piece, jj, kk, ok = place(n)
         return jnp.where(ok, piece * 5 + (jj if on_j else kk), -1)
@@ -48,8 +46,14 @@
         return jnp.where(ok, kk if on_j else jj, none)
 
     spread_rows = onehot(index(iota((128, 1), 0)) == iota((128, 32), 1))
-    spread_lanes = onehot(index(iota((1, 128), 1)) == iota((K2, 128), 0))
-    mask = onehot(fixed(iota((128, 1), 0), -1) == fixed(iota((1, 128), 1), -2), F32)
+    lane = iota((1, 128), 1)
+    lane_index, lane_fixed = index(lane), fixed(lane, -2)
+    if natural:
+        lane_fixed = (lane * 205) >> 12
+        lane_index = jnp.where(lane < 100, lane - 20 * lane_fixed, -1)
+        lane_fixed = jnp.where(lane < 100, lane_fixed, -2)
+    spread_lanes = onehot(lane_index == iota((K2, 128), 0))
+    mask = onehot(fixed(iota((128, 1), 0), -1) == lane_fixed, F32)
     return spread_rows, spread_lanes, mask
 
 
@@ -83,10 +87,32 @@
     return a, b, c, d
 
 
-def build_kernel(fine_hbm, coarse_hbm, child_hbm, *refs):
-    (fine_rows, fine_y, fine_z, coarse_rows, coarse_y, coarse_z,
-     down_rows, down_y, down_z, up_rows, up_y, up_z,
-     fine_ref, coarse_ref, child_ref, plain, turned, wide_y, wide_z, wide_rows, sems) = refs
+def spread_rows_of(out, plain, rows, nz, order):
+    spread_rows, spreads, mask = row_constants(rows, nz)
+    wide = sum(dot(plain[d].reshape(TERMS * 32, K2).astype(BF), spreads[c]) for c, d in enumerate(order))
+    wide = wide.astype(BF).reshape(TERMS, 32, 256)
+    for m in range(TERMS):
+        mats = (dot(spread_rows, wide[m]) * mask).astype(BF)
+        for c in range(2):
+            out[m, c] = mats[:, 128 * c:128 * c + 128]
+
+
+def lane_matrix(transposed, constants):
+    spread_rows, spread_lanes, mask = constants
+    return (dot(spread_rows[:, 0:K2], dot(transposed, spread_lanes).astype(BF)) * mask).astype(BF)
+
+
+def parity():
+    return lax.axis_index("gx") & 1, lax.axis_index("gy") & 1
+
+
+def chosen(child_ref, which):
+    first, second = child_ref[:, 0, :].astype(F32), child_ref[:, 1, :].astype(F32)
+    return jnp.where(which == 0, first, second).astype(BF), jnp.where(which == 0, second, first).astype(BF)
+
+
+def early_kernel(fine_hbm, coarse_hbm, child_hbm, fine_ref, coarse_ref, child_ref,
+                 fine_rows, down_rows, down_y, down_z, plain, sems):
     copies = [
         pltpu.make_async_copy(src, dst, sems.at[n])
         for n, (src, dst) in enumerate(((fine_hbm, fine_ref), (coarse_hbm, coarse_ref), (child_hbm, child_ref)))
@@ -94,38 +120,57 @@
     for copy in copies:
         copy.start()
     plain[...] = jnp.zeros(plain.shape, F32)
-    turned[...] = jnp.zeros(turned.shape, F32)
-    px, py = lax.axis_index("gx") & 1, lax.axis_index("gy") & 1
-    rows_y, lanes_y, mask_y = lane_constants(True)
-    rows_z, lanes_z, mask_z = lane_constants(False)
-    both = jnp.concatenate([lanes_y, lanes_z], axis=1)
-    near_x, near_y = 2 - 2 * px, 2 - 2 * py
-    levels = (
-        (fine_ref, fine_rows, fine_y, fine_z, FINE_ROWS, 4, (1, near_x, 2 - near_x), (1, near_y, 2 - near_y)),
-        (coarse_ref, coarse_rows, coarse_y, coarse_z, COARSE_ROWS, 2, (1, 2 - near_x, near_x), (1, 2 - near_y, near_y)),
-    )
+    px, py = parity()
+    on_j, on_k = lane_constants(True), lane_constants(False)
     for copy in copies:
         copy.wait()
+    for d in range(3):
+        for m in range(TERMS):
+            plain[d, m, 0:K2, :] = fine_ref[d, m].astype(F32)
+    near_x = 2 - 2 * px
+    spread_rows_of(fine_rows, plain, FINE_ROWS, 4, (1, near_x, 2 - near_x))
+    own_x, other_x = chosen(child_ref, px)
+    own_y, other_y = chosen(child_ref, py)
+    down_y[0:128, :] = lane_matrix(flipped(own_y), on_j)
+    down_y[128:256, :] = lane_matrix(flipped(other_y), on_j)
+    for c in range(2):
+        down_z[128 * c:128 * c + 128, :] = lane_matrix(flipped(child_ref[:, c, :]), on_k)
+    lane = iota((1, 160), 1)
+    far = lane >= 80
+    lane = jnp.where(far, lane - 80, lane)
+    wide = dot(own_x, onehot(jnp.where(far, -1, lane >> 2) == iota((K2, 160), 0)))
+    wide = wide + dot(other_x, onehot(jnp.where(far, lane >> 2, -1) == iota((K2, 160), 0)))
+    r = iota((96, 1), 0)
+    cz = jnp.where(r >= 48, 1, 0)
+    r = r - 48 * cz
+    mixed = dot(onehot((r >> 1) == iota((96, K2), 1)), wide.astype(BF))
+    down_rows[...] = (mixed * onehot((2 * (r & 1) + cz) == (lane & 3), F32)).astype(BF)
+
+
+def late_kernel(fine_ref, coarse_ref, child_ref, fine_y, fine_z, coarse_rows, coarse_y, coarse_z,
+                up_rows, up_y, up_z, plain, turned, wide_y, wide_z):
+    plain[...] = jnp.zeros(plain.shape, F32)
+    turned[...] = jnp.zeros(turned.shape, F32)
+    px, py = parity()
+    on_j, on_k, to_natural = lane_constants(True), lane_constants(False), lane_constants(False, True)
+    near_x, near_y = 2 - 2 * px, 2 - 2 * py
     for n, blocks in enumerate((fine_ref, coarse_ref)):
         for d in range(3):
             for m in range(TERMS):
                 matrix = blocks[d, m].astype(F32)
-                plain[n, d, m, 0:K2, :] = matrix
                 turned[n, d, m, 0:K2, :] = matrix.T
-    for n, (blocks, rows_out, y_out, z_out, rows, nz, order_x, order_y) in enumerate(levels):
-        spread_rows, spreads, mask = row_constants(rows, nz)
-        count = 3 * TERMS * 32
-        wide = dot(turned[n].reshape(count, K2).astype(BF), both).astype(BF)
+                if n == 1:
+                    plain[d, m, 0:K2, :] = matrix
+    levels = (
+        (fine_y, fine_z, to_natural, (1, near_y, 2 - near_y)), (coarse_y, coarse_z, on_k, (1, 2 - near_y, near_y)),
+    )
+    for n, (y_out, z_out, along_k, order_y) in enumerate(levels):
+        both = jnp.concatenate([on_j[1], along_k[1]], axis=1)
+        wide = dot(turned[n].reshape(3 * TERMS * 32, K2).astype(BF), both).astype(BF)
         wide_y[n] = wide[:, 0:128].reshape(3, TERMS, 32, 128)
         wide_z[n] = wide[:, 128:256].reshape(3, TERMS, 32, 128)
-        wide = sum(dot(plain[n, d].reshape(TERMS * 32, K2).astype(BF), spreads[c]) for c, d in enumerate(order_x))
-        wide_rows[...] = wide.astype(BF).reshape(TERMS, 32, 256)
-        for m in range(TERMS):
-            mats = (dot(spread_rows, wide_rows[m]) * mask).astype(BF)
-            for c in range(2):
-                rows_out[m, c] = mats[:, 128 * c:128 * c + 128]
-        for spread, mask, source_ref, order, out in (
-            (rows_y, mask_y, wide_y, order_y, y_out), (rows_z, mask_z, wide_z, (1, 2, 0), z_out),
+        for (spread, _, mask), source_ref, order, out in (
+            (on_j, wide_y, order_y, y_out), (along_k, wide_z, (1, 2, 0), z_out),
         ):
             for m in range(0, TERMS, 2):
                 tiles = [source_ref[n, d, m + c] for c in range(2) for d in order]
@@ -138,69 +183,53 @@
                             out[m + c, e] = tile
                         else:
                             out[e, m + c] = tile
-
-    first_child, second_child = child_ref[:, 0, :], child_ref[:, 1, :]
-
-    def chosen(condition, a, b):
-        return jnp.where(condition, a.astype(F32), b.astype(F32)).astype(BF)
-
-    own_x, other_x = chosen(px == 0, first_child, second_child), chosen(px == 0, second_child, first_child)
-    own_y, other_y = chosen(py == 0, first_child, second_child), chosen(py == 0, second_child, first_child)
-
-    def lane_matrix(transposed, spread_rows, spread_lanes, mask):
-        return (dot(spread_rows[:, 0:K2], dot(transposed, spread_lanes).astype(BF)) * mask).astype(BF)
-
-    down_y[0:128, :] = lane_matrix(flipped(own_y), rows_y, lanes_y, mask_y)
-    down_y[128:256, :] = lane_matrix(flipped(other_y), rows_y, lanes_y, mask_y)
-    up_y[...] = lane_matrix(own_y, rows_y, lanes_y, mask_y)
-    for c, child in enumerate((first_child, second_child)):
-        down_z[128 * c:128 * c + 128, :] = lane_matrix(flipped(child), rows_z, lanes_z, mask_z)
-        up_z[c] = lane_matrix(child, rows_z, lanes_z, mask_z)
-    lane = iota((1, 160), 1)
-    far = lane >= 80
-    lane = jnp.where(far, lane - 80, lane)
-    wide = dot(own_x, onehot(jnp.where(far, -1, lane >> 2) == iota((K2, 160), 0)))
-    wide = wide + dot(other_x, onehot(jnp.where(far, lane >> 2, -1) == iota((K2, 160), 0)))
-    r = iota((96, 1), 0)
-    cz = jnp.where(r >= 48, 1, 0)
-    r = r - 48 * cz
-    mixed = dot(onehot((r >> 1) == iota((96, K2), 1)), wide.astype(BF))
-    down_rows[...] = (mixed * onehot((2 * (r & 1) + cz) == (lane & 3), F32)).astype(BF)
+    spread_rows_of(coarse_rows, plain, COARSE_ROWS, 2, (1, 2 - near_x, near_x))
+    own_x, _ = chosen(child_ref, px)
+    own_y, _ = chosen(child_ref, py)
+    up_y[...] = lane_matrix(own_y, on_j)
+    for c in range(2):
+        up_z[c] = lane_matrix(child_ref[:, c, :], to_natural)
     wide = dot(flipped(own_x), onehot((iota((1, 48), 1) >> 1) == iota((K2, 48), 0)))
     mixed = dot(onehot((iota((80, 1), 0) >> 2) == iota((80, K2), 1)), wide.astype(BF))
     keep = ((iota((80, 1), 0) & 3) >> 1) == (iota((1, 48), 1) & 1)
     up_rows[...] = (mixed * onehot(keep, F32)).astype(BF)
 
 
-def build(fine_blocks, coarse_blocks, child):
-    def s(*shape):
-        return jax.ShapeDtypeStruct(shape, BF)
-
-    out_shape = ()
-    for rows in (FINE_ROWS, COARSE_ROWS):
-        out_shape += (s(TERMS, 2, rows, 128), s(TERMS, 3, 128, 128), s(3, TERMS, 128, 128))
-    out_shape += (s(96, 160), s(256, 128), s(256, 128), s(80, 48), s(128, 128), s(2, 128, 128))
-    return pl.pallas_call(
-        build_kernel, out_shape=out_shape, name="build",
-        in_specs=[pl.BlockSpec(memory_space=pltpu.HBM)] * 3,
-        scratch_shapes=[
-            pltpu.VMEM((3, TERMS, K2, K2), BF), pltpu.VMEM((3, TERMS, K2, K2), BF),
-            pltpu.VMEM((K2, 2, K2), BF),
-            pltpu.VMEM((2, 3, TERMS, 32, K2), F32), pltpu.VMEM((2, 3, TERMS, 32, K2), F32),
-            pltpu.VMEM((2, 3, TERMS, 32, 128), BF), pltpu.VMEM((2, 3, TERMS, 32, 128), BF),
-            pltpu.VMEM((TERMS, 32, 256), BF), pltpu.SemaphoreType.DMA((3,)),
-        ],
-        compiler_params=pltpu.CompilerParams(vmem_limit_bytes=32 << 20),
-        cost_estimate=pl.CostEstimate(flops=4 * 10**9, bytes_accessed=10 * 10**6, transcendentals=0),
-    )(*(
+def bf16(*shape):
+    return jax.ShapeDtypeStruct(shape, BF)
+
+
+def early(fine_blocks, coarse_blocks, child):
+    operands = [
         pltpu.with_memory_space_constraint(x, pltpu.HBM)
         for x in (fine_blocks, coarse_blocks, jnp.transpose(child, (1, 0, 2)))
-    ))
+    ]
+    out_shape = tuple(bf16(*x.shape) for x in operands) + (
+        bf16(TERMS, 2, FINE_ROWS, 128), bf16(96, 160), bf16(256, 128), bf16(256, 128),
+    )
+    return pl.pallas_call(
+        early_kernel, out_shape=out_shape, name="early",
+        in_specs=[pl.BlockSpec(memory_space=pltpu.HBM)] * 3,
+        scratch_shapes=[pltpu.VMEM((3, TERMS, 32, K2), F32), pltpu.SemaphoreType.DMA((3,))],
+        compiler_params=pltpu.CompilerParams(vmem_limit_bytes=16 << 20),
+        cost_estimate=pl.CostEstimate(flops=2 * 10**9, bytes_accessed=4 * 10**6, transcendentals=0),
+    )(*operands)
+
+
+def late(blocks):
+    level = (bf16(TERMS, 3, 128, 128), bf16(3, TERMS, 128, 128))
+    out_shape = level + (bf16(TERMS, 2, COARSE_ROWS, 128),) + level
+    out_shape += (bf16(80, 48), bf16(128, 128), bf16(2, 128, 128))
+    scratch = [
+        pltpu.VMEM((3, TERMS, 32, K2), F32), pltpu.VMEM((2, 3, TERMS, 32, K2), F32),
+        pltpu.VMEM((2, 3, TERMS, 32, 128), BF), pltpu.VMEM((2, 3, TERMS, 32, 128), BF),
+    ]
+    return small_call(late_kernel, "late", out_shape, 2 * 10**9, *blocks, scratch=scratch)
 
 
 def source_kernel(own, xnear, ynear, corner, down_rows, down_y, down_z,
                   packet, nears, natural, mixed, turned):
-    select = onehot(iota((400, 512), 0) == natural_place(iota((1, 512), 1), True))
+    select = onehot(iota((400, 512), 0) == natural_place(iota((1, 512), 1)))
 
     def converted(ref, slot):
         values = ref[0, 0].astype(F32)
@@ -318,7 +347,7 @@
 
 
 def coarse_kernel(packet, xfar, xother, yfar, yother, row_mats, y_mats, z_mats,
-                  up_rows, up_y, up_z, fine_term, out, wide, grown, turned, split,
+                  up_rows, up_y, up_z, fine_term, out, wide, grown, turned,
                   x_sum, far_side, other_side, centre, *scratch):
     own = [packet[b, 80:128, :] for b in range(4)]
     others = [[ref[b] for b in range(4)] for ref in (xfar, xother, yfar, yother)]
@@ -339,16 +368,10 @@
     both = dot(turned[...], jnp.concatenate([up_z[0], up_z[1]], axis=1))
     expanded = jnp.where((iota((320, 128), 0) & 1) == 0, both[:, 0:128], both[:, 128:256])
     total = fine_term[...] + expanded
-    high = total.astype(BF)
-    low = (total - high.astype(F32)).astype(BF)
-    for b in range(4):
-        split[0:80, 128 * b:128 * b + 128] = high[80 * b:80 * b + 80, :]
-        split[80:160, 128 * b:128 * b + 128] = low[80 * b:80 * b + 80, :]
-    select = onehot(natural_place(iota((512, 1), 0), False) == iota((512, 400), 1))
-    natural = dot(split[...], select)
-    natural = natural[0:80, :] + natural[80:160, :]
     for i in range(K2):
-        out[0, 0, :, 400 * i:400 * i + 400] = natural[4 * i:4 * i + 4, :]
+        for b in range(4):
+            here = 400 * i + 100 * b
+            out[0, 0, :, here:here + 100] = total[80 * b + 4 * i:80 * b + 4 * i + 4, 0:100]
 
 
 def coarse(operands):
@@ -357,7 +380,6 @@
         pltpu.VMEM((COARSE_ROWS, 512), BF),
         pltpu.VMEM((320, 128), BF),
         pltpu.VMEM((320, 128), BF),
-        pltpu.VMEM((160, 512), BF),
     ] + [part] * 4 + level_scratch(COARSE_ROWS)
     return small_call(
         coarse_kernel, "coarse", jax.ShapeDtypeStruct((1, 1, 4, 8000), F32), 4 * 10**9, *operands, scratch=scratch
@@ -381,22 +403,23 @@
 
 def shards(fine_source, fine_blocks, coarse_blocks, child_filter_matrices):
     columns = [fine_source, near(fine_source, "gx"), near(fine_source, "gy"), corner(fine_source)]
-    built = build(fine_blocks, coarse_blocks, child_filter_matrices)
-    packet, nears = source(columns, *built[6:9])
+    *blocks, fine_rows, down_rows, down_y, down_z = early(fine_blocks, coarse_blocks, child_filter_matrices)
+    packet, nears = source(columns, down_rows, down_y, down_z)
     x_packet, y_packet = far(packet, "gx"), far(packet, "gy")
+    fine_y, fine_z, *mats = late(blocks)
     part = jax.ShapeDtypeStruct((TERMS, 4 * FINE_ROWS, 128), BF)
     parent = jax.ShapeDtypeStruct((4, COARSE_ROWS, 128), BF)
-    y_near, centre = small_call(fine_near_kernel, "fine_near", (part, part), 10**9, packet, nears, built[0])
+    y_near, centre = small_call(fine_near_kernel, "fine_near", (part, part), 10**9, packet, nears, fine_rows)
     x_sum, y_far, x_parent, y_parent = small_call(
         fine_far_kernel, "fine_far", (part, part, parent, parent), 10**9,
-        packet, nears, x_packet, y_packet, built[0],
+        packet, nears, x_packet, y_packet, fine_rows,
     )
     x_other, y_other = near(x_parent, "gx"), near(y_parent, "gy")
     fine_term = small_call(
         fine_rest_kernel, "fine_rest", jax.ShapeDtypeStruct((4 * FINE_ROWS, 128), F32), 4 * 10**9,
-        x_sum, y_near, y_far, centre, *built[1:3], scratch=level_scratch(FINE_ROWS),
-    )
-    return coarse((packet, x_parent, x_other, y_parent, y_other, *built[3:6], *built[9:12], fine_term))
+        x_sum, y_near, y_far, centre, fine_y, fine_z, scratch=level_scratch(FINE_ROWS),
+    )
+    return coarse((packet, x_parent, x_other, y_parent, y_other, *mats, fine_term))
 
 
 def solution(mesh):

time: 32.5 us -> 34.4 us (1.058)
  the two profiles are of different devices: /device:TPU:130 before, /device:TPU:90 now
where the time goes in v4:
time: 34.4 us; the launch traced here: 34.2 us
  Pallas kernels  14.1 us (41%)
  starting transfers between devices  11.1 us (32%)
  waiting for transfers between devices  8.86 us (26%)
    pallas_call x5, Pallas kernels, small_call(): pl.pallas_call(kernel, out_shape=out_shape, name=name, scratch_shapes=scr...  10.4 us
    ppermute x2, starting transfers between devices, far(): lax.ppermute(block, axis, [(i, (i + 1 ^ 1) - 1) for i in range(1, count -...  8.92 us
    ppermute x2, waiting for transfers between devices, far(): lax.ppermute(block, axis, [(i, (i + 1 ^ 1) - 1) for i in range(1, count -...  5.19 us
    ppermute x4, waiting for transfers between devices, near(): lax.ppermute(block, axis, [(i, i ^ 1) for i in range(lax.axis_size(axis))])  3.22 us
    pallas_call x1, Pallas kernels, early(): pl.pallas_call(early_kernel, out_shape=out_shape, name='early', in_specs=...  2.36 us
    pallas_call x1, Pallas kernels, source(): pl.pallas_call(source_kernel, out_shape=out_shape, scratch_shapes=scratch...  1.38 us
    ppermute x1, starting transfers between devices, corner(): return lax.ppermute(block, ('gx', 'gy'), route)  1.11 us
    ppermute x4, starting transfers between devices, near(): lax.ppermute(block, axis, [(i, i ^ 1) for i in range(lax.axis_size(axis))])  1.11 us
  transfers between devices with their start and end apart: 7, of which 4 were waited for; matrix products, arithmetic and copies ran while one was open for 0% of the time, Pallas kernels for 24%

profile of v4, /device:TPU:90, one launch (start us, length us, event | category | flops | bytes accessed | tf_op | source)
XLA Modules:
  0.0 34.2 jit_solution(14004889810225871983)
XLA Ops:
  0.0 0.0 collective-permute-start
  0.0 0.7 %collective-permute-start.1 = (bf16[1,1,4,8000]{3,2,1,0:T(4,128)(2,1)}, bf16[1,1,4,8000]{3,2,1,0:T(4,128)(2,1)S(1)}, u32[]{:S(2)}, u32[]{:S(2)}) collective-permute-start(bf16[1,1,4,8000]{3,2,1,0:T(4,128)(2,1)} %own.1), channel_id=1, source_target_pairs={{0,1},{1,0},{2,3},{3,2},{4,5},{5,4},{6,7},{7,6},{8,9},{9,8},{10,11... | collective-permute-start | bytes 192008 | tf_op jit(solution)/shard_map/ppermute | solution.py:390
  0.7 1.1 %collective-permute-start.2 = (bf16[1,1,4,8000]{3,2,1,0:T(4,128)(2,1)}, bf16[1,1,4,8000]{3,2,1,0:T(4,128)(2,1)S(1)}, u32[]{:S(2)}, u32[]{:S(2)}) collective-permute-start(bf16[1,1,4,8000]{3,2,1,0:T(4,128)(2,1)} %own.1), channel_id=1, source_target_pairs={{0,17},{1,16},{2,19},{3,18},{4,21},{5,20},{6,23},{7,22},{8,25},{9,... | collective-permute-start | bytes 192008 | tf_op jit(solution)/shard_map/ppermute | solution.py:401
  1.9 0.0 copy-start
  1.9 2.4 %early.1 = (bf16[3,12,20,20]{3,2,1,0:T(8,128)(2,1)S(1)}, bf16[3,12,20,20]{3,2,1,0:T(8,128)(2,1)S(1)}, bf16[20,2,20]{2,1,0:T(2,128)(2,1)S(1)}, bf16[12,2,80,128]{...) custom-call(bf16[3,12,20,20]{3,2,1,0:T(8,128)(2,1)} %fine_hbm.1, ...), custom_call_target="tpu_custom_call" | custom-call | flops 2000000000 | bytes 4000000 | tf_op jit(solution)/shard_map/early/pallas_call | solution.py:210
  4.2 0.0 collective-permute-done.xnear
  4.2 0.9 %collective-permute-done.1.ynear = bf16[1,1,4,8000]{3,2,1,0:T(4,128)(2,1)S(1)} collective-permute-done((bf16[1,1,4,8000]{3,2,1,0:T(4,128)(2,1)}, bf16[1,1,4,8000]{3,2,1,0:T(4,128)(2,1)S(1)}, u32[]{:S(2)}, u32[]{:S(2)}) %collective-permute-start.1) | collective-permute-done | bytes 64032 | tf_op jit(solution)/shard_map/ppermute | solution.py:390
  5.2 0.5 %collective-permute-done.2.corner = bf16[1,1,4,8000]{3,2,1,0:T(4,128)(2,1)S(1)} collective-permute-done((bf16[1,1,4,8000]{3,2,1,0:T(4,128)(2,1)}, bf16[1,1,4,8000]{3,2,1,0:T(4,128)(2,1)S(1)}, u32[]{:S(2)}, u32[]{:S(2)}) %collective-permute-start.2) | collective-permute-done | bytes 64032 | tf_op jit(solution)/shard_map/ppermute | solution.py:401
  5.6 0.0 copy-done
  5.6 1.4 %source.1 = (bf16[4,128,128]{2,1,0:T(8,128)(2,1)S(1)}, bf16[2,4,80,128]{3,2,1,0:T(8,128)(2,1)S(1)}) custom-call(bf16[1,1,4,8000]{3,2,1,0:T(4,128)(2,1)S(1)} %copy-done, bf16[1,1,4,8000]{3,2,1,0:T(4,128)(2,1)S(1)} %collective-permute-done.xnear, bf16[1,1,4,8000]{3,2,1,0:T(4,128)(2,1)S(1)} %collective-permute-done.1.ynear, ...), custom_call_target="tpu_custom_call" | custom-call | flops 1000000000 | bytes 1000000 | tf_op jit(solution)/shard_map/source/pallas_call | solution.py:272
  7.0 3.7 %collective-permute-start.3 = (bf16[4,128,128]{2,1,0:T(8,128)(2,1)S(1)}, bf16[4,128,128]{2,1,0:T(8,128)(2,1)S(1)}, u32[]{:S(2)}, u32[]{:S(2)}) collective-permute-start(bf16[4,128,128]{2,1,0:T(8,128)(2,1)S(1)} %get-tuple-element.31.packet), channel_id=1, source_target_pairs={{16,32},{32,16},{48,64},{64,48},{80,96},{96,80},{112,128},{128,112... | collective-permute-start | bytes 393224 | tf_op jit(solution)/shard_map/ppermute | solution.py:395
  10.7 5.2 %collective-permute-start.4 = (bf16[4,128,128]{2,1,0:T(8,128)(2,1)S(1)}, bf16[4,128,128]{2,1,0:T(8,128)(2,1)S(1)}, u32[]{:S(2)}, u32[]{:S(2)}) collective-permute-start(bf16[4,128,128]{2,1,0:T(8,128)(2,1)S(1)} %get-tuple-element.31.packet), channel_id=1, source_target_pairs={{1,2},{2,1},{3,4},{4,3},{5,6},{6,5},{7,8},{8,7},{9,10},{10,9},{11,... | collective-permute-start | bytes 393224 | tf_op jit(solution)/shard_map/ppermute | solution.py:395
  15.9 3.5 %late.1 = (bf16[12,3,128,128]{3,2,1,0:T(8,128)(2,1)S(1)}, bf16[3,12,128,128]{3,2,1,0:T(8,128)(2,1)S(1)}, bf16[12,2,48,128]{3,2,1,0:T(8,128)(2,1)S(1)}, bf16[12,3...) custom-call(bf16[3,12,20,20]{3,2,1,0:T(8,128)(2,1)S(1)} %get-tuple-e, ...), custom_call_target="tpu_custom_call" | custom-call | flops 2000000000 | bytes 4000000 | tf_op jit(solution)/shard_map/late/pallas_call | solution.py:342
  19.4 0.7 %fine_near.1 = (bf16[12,320,128]{2,1,0:T(8,128)(2,1)S(1)}, bf16[12,320,128]{2,1,0:T(8,128)(2,1)S(1)}) custom-call(bf16[4,128,128]{2,1,0:T(8,128)(2,1)S(1)} %get-tuple-element.31.packet, bf16[2,4,80,128]{3,2,1,0:T(8,128)(2,1)S(1)} %get-tuple-element.32.nears, bf16[12,2,80,128]{3,2,1,0:T(8,128)(2,1)S(1)} %get-tuple-element.33.row_mats), custom_call_target="tpu_custom_call" | custom-call | flops 1000000000 | bytes 4000000 | tf_op jit(solution)/shard_map/fine_near/pallas_call | solution.py:342
  20.1 0.0 collective-permute-done.3.x_packet
  20.1 5.2 %collective-permute-done.4.y_packet = bf16[4,128,128]{2,1,0:T(8,128)(2,1)S(1)} collective-permute-done((bf16[4,128,128]{2,1,0:T(8,128)(2,1)S(1)}, bf16[4,128,128]{2,1,0:T(8,128)(2,1)S(1)}, u32[]{:S(2)}, u32[]{:S(2)}) %collective-permute-start.4) | collective-permute-done | bytes 131104 | tf_op jit(solution)/shard_map/ppermute | solution.py:395
  25.3 1.0 %fine_far.1 = (bf16[12,320,128]{2,1,0:T(8,128)(2,1)S(1)}, bf16[12,320,128]{2,1,0:T(8,128)(2,1)S(1)}, bf16[4,48,128]{2,1,0:T(8,128)(2,1)S(1)}, bf16[4,48,128]{2,1,0:T(8,128)(2,1)S(1)}) custom-call(bf16[4,128,128]{2,1,0:T(8,128)(2,1)S(1)} %get-tuple-element.31.packet, bf16[2,4,80,128]{3,2,1,0:T(8,128)(2,1)S(1)} %get-tuple-element.32.nears, ...), custom_call_target="tpu_custom_call" | custom-call | flops 1000000000 | bytes 4000000 | tf_op jit(solution)/shard_map/fine_far/pallas_call | solution.py:342
  26.2 0.1 collective-permute-start.5
  26.3 0.3 collective-permute-start.6
  26.6 1.8 %fine_rest.1.fine_term = f32[320,128]{1,0:T(8,128)S(1)} custom-call(bf16[12,320,128]{2,1,0:T(8,128)(2,1)S(1)} %get-tuple-element.45.x_sum, bf16[12,320,128]{2,1,0:T(8,128)(2,1)S(1)} %get-tuple-element.46.y_near, bf16[12,320,128]{2,1,0:T(8,128)(2,1)S(1)} %get-tuple-element.47.y_far, bf16[12,320,128]{2,1,0:T(8,128)(2,1)S(1)} %get-tuple-element.48.centre, ...), custom_call_target="tpu_custom_call" | custom-call | flops 4000000000 | bytes 4000000 | tf_op jit(solution)/shard_map/fine_rest/pallas_call | solution.py:342
  28.4 0.0 collective-permute-done.5.xother
  28.4 2.3 %collective-permute-done.6.yother = bf16[4,48,128]{2,1,0:T(8,128)(2,1)S(1)} collective-permute-done((bf16[4,48,128]{2,1,0:T(8,128)(2,1)S(1)}, bf16[4,48,128]{2,1,0:T(8,128)(2,1)S(1)}, u32[]{:S(2)}, u32[]{:S(2)}) %collective-permute-start.6) | collective-permute-done | bytes 49184 | tf_op jit(solution)/shard_map/ppermute | solution.py:390
  30.7 3.5 %coarse.1 = f32[1,1,4,8000]{3,2,1,0:T(4,128)} custom-call(bf16[4,128,128]{2,1,0:T(8,128)(2,1)S(1)} %get-tuple-element.31.packet, bf16[4,48,128]{2,1,0:T(8,128)(2,1)S(1)} %get-tuple-element.34.xfar, bf16[4,48,128]{2,1,0:T(8,128)(2,1)S(1)} %collective-permute-done.5.xother, bf16[4,48,128]{2,1,0:T(8,128)(2,1)S(1)} %get-tuple-element.35.yfar, ...), custom_call_target="tpu_custom_call" | custom-call | flops 4000000000 | bytes 4000000 | tf_op jit(solution)/shard_map/coarse/pallas_call | solution.py:342
Async XLA Ops:
  0.0 4.2 %collective-permute-start = (bf16[1,1,4,8000]{3,2,1,0:T(4,128)(2,1)}, bf16[1,1,4,8000]{3,2,1,0:T(4,128)(2,1)S(1)}, u32[]{:S(2)}, u32[]{:S(2)}) collective-permute-start(bf16[1,1,4,8000]{3,2,1,0:T(4,128)(2,1)} %own.1), channel_id=1, source_target_pairs={{0,16},{16,0},{32,48},{48,32},{64,80},{80,64},{96,112},{112,96},{1... | collective-permute-start | bytes 192008 | tf_op jit(solution)/shard_map/ppermute | solution.py:390
  0.0 5.2 %collective-permute-start.1 = (bf16[1,1,4,8000]{3,2,1,0:T(4,128)(2,1)}, bf16[1,1,4,8000]{3,2,1,0:T(4,128)(2,1)S(1)}, u32[]{:S(2)}, u32[]{:S(2)}) collective-permute-start(bf16[1,1,4,8000]{3,2,1,0:T(4,128)(2,1)} %own.1), channel_id=1, source_target_pairs={{0,1},{1,0},{2,3},{3,2},{4,5},{5,4},{6,7},{7,6},{8,9},{9,8},{10,11... | collective-permute-start | bytes 192008 | tf_op jit(solution)/shard_map/ppermute | solution.py:390
  0.7 4.9 %collective-permute-start.2 = (bf16[1,1,4,8000]{3,2,1,0:T(4,128)(2,1)}, bf16[1,1,4,8000]{3,2,1,0:T(4,128)(2,1)S(1)}, u32[]{:S(2)}, u32[]{:S(2)}) collective-permute-start(bf16[1,1,4,8000]{3,2,1,0:T(4,128)(2,1)} %own.1), channel_id=1, source_target_pairs={{0,17},{1,16},{2,19},{3,18},{4,21},{5,20},{6,23},{7,22},{8,25},{9,... | collective-permute-start | bytes 192008 | tf_op jit(solution)/shard_map/ppermute | solution.py:401
  1.9 3.8 %copy-start = (bf16[1,1,4,8000]{3,2,1,0:T(4,128)(2,1)S(1)}, bf16[1,1,4,8000]{3,2,1,0:T(4,128)(2,1)}, u32[]{:S(2)}) copy-start(bf16[1,1,4,8000]{3,2,1,0:T(4,128)(2,1)} %own.1) | copy-start | bytes 192004
  7.0 13.1 %collective-permute-start.3 = (bf16[4,128,128]{2,1,0:T(8,128)(2,1)S(1)}, bf16[4,128,128]{2,1,0:T(8,128)(2,1)S(1)}, u32[]{:S(2)}, u32[]{:S(2)}) collective-permute-start(bf16[4,128,128]{2,1,0:T(8,128)(2,1)S(1)} %get-tuple-element.31.packet), channel_id=1, source_target_pairs={{16,32},{32,16},{48,64},{64,48},{80,96},{96,80},{112,128},{128,112... | collective-permute-start | bytes 393224 | tf_op jit(solution)/shard_map/ppermute | solution.py:395
  10.7 14.6 %collective-permute-start.4 = (bf16[4,128,128]{2,1,0:T(8,128)(2,1)S(1)}, bf16[4,128,128]{2,1,0:T(8,128)(2,1)S(1)}, u32[]{:S(2)}, u32[]{:S(2)}) collective-permute-start(bf16[4,128,128]{2,1,0:T(8,128)(2,1)S(1)} %get-tuple-element.31.packet), channel_id=1, source_target_pairs={{1,2},{2,1},{3,4},{4,3},{5,6},{6,5},{7,8},{8,7},{9,10},{10,9},{11,... | collective-permute-start | bytes 393224 | tf_op jit(solution)/shard_map/ppermute | solution.py:395
  26.2 2.2 %collective-permute-start.5 = (bf16[4,48,128]{2,1,0:T(8,128)(2,1)S(1)}, bf16[4,48,128]{2,1,0:T(8,128)(2,1)S(1)}, u32[]{:S(2)}, u32[]{:S(2)}) collective-permute-start(bf16[4,48,128]{2,1,0:T(8,128)(2,1)S(1)} %get-tuple-element.34.xfar), channel_id=1, source_target_pairs={{0,16},{16,0},{32,48},{48,32},{64,80},{80,64},{96,112},{112,96},{1... | collective-permute-start | bytes 147464 | tf_op jit(solution)/shard_map/ppermute | solution.py:390
  26.3 4.4 %collective-permute-start.6 = (bf16[4,48,128]{2,1,0:T(8,128)(2,1)S(1)}, bf16[4,48,128]{2,1,0:T(8,128)(2,1)S(1)}, u32[]{:S(2)}, u32[]{:S(2)}) collective-permute-start(bf16[4,48,128]{2,1,0:T(8,128)(2,1)S(1)} %get-tuple-element.35.yfar), channel_id=1, source_target_pairs={{0,1},{1,0},{2,3},{3,2},{4,5},{5,4},{6,7},{7,6},{8,9},{9,8},{10,11... | collective-permute-start | bytes 147464 | tf_op jit(solution)/shard_map/ppermute | solution.py:390

commit v5 on v4

--- a/solution.py
+++ b/solution.py
@@ -11,6 +11,7 @@
 F32 = jnp.float32
 FINE_ROWS = 80
 COARSE_ROWS = 48
+PARENT_ROWS = 40
 
 
 def iota(shape, dim):
@@ -58,12 +59,13 @@
 
 
 def row_constants(rows, nz):
+    taken = K2 * nz
     shift = nz.bit_length() - 1
     spread_rows = onehot((iota((rows, 1), 0) >> shift) == iota((rows, 32), 1))
     wide = 256
     lane = iota((1, wide), 1)
-    which = sum(jnp.where(lane >= c * rows, 1, 0) for c in range(1, 4))
-    lane = lane - which * rows
+    which = sum(jnp.where(lane >= c * taken, 1, 0) for c in range(1, 4))
+    lane = lane - which * taken
     spreads = [
         onehot(jnp.where(which == c, lane >> shift, -1) == iota((K2, wide), 0)) for c in range(3)
     ]
@@ -256,12 +258,12 @@
     total = dot(jnp.concatenate([turned[0], turned[1]], axis=1), down_z[...])
     blocks = exchange([total[48 * b:48 * b + 48, :] for b in range(4)])
     for b in range(4):
-        packet[b, 80:128, :] = blocks[b].astype(BF)
+        packet[b, 80:120, :] = blocks[b][0:PARENT_ROWS, :].astype(BF)
 
 
 def source(columns, down_rows, down_y, down_z):
     out_shape = (
-        jax.ShapeDtypeStruct((4, FINE_ROWS + COARSE_ROWS, 128), BF),
+        jax.ShapeDtypeStruct((4, FINE_ROWS + PARENT_ROWS, 128), BF),
         jax.ShapeDtypeStruct((2, 4, FINE_ROWS, 128), BF),
     )
     scratch = [
@@ -282,7 +284,7 @@
 
 def row_pass(rows, row_mats, stacks, targets):
     stacks = [[joined(column) for column in stack] for stack in stacks]
-    stacks = [stack[0] if len(stack) == 1 else jnp.concatenate(stack, axis=0) for stack in stacks]
+    stacks = [(stack[0] if len(stack) == 1 else jnp.concatenate(stack, axis=0)).astype(BF) for stack in stacks]
     for m in range(TERMS):
         mats = jnp.concatenate([row_mats[m, 0], row_mats[m, 1]], axis=1)
         for stack, target in zip(stacks, targets):
@@ -325,10 +327,10 @@
     row_pass(FINE_ROWS, row_mats, ([[nears[1, b] for b in range(4)]], [own]), (y_near, centre))
 
 
-def fine_far_kernel(packet, nears, x_packet, y_packet, row_mats, x_sum, y_far, x_parent, y_parent):
-    for b in range(4):
-        x_parent[b] = x_packet[b, 80:128, :]
-        y_parent[b] = y_packet[b, 80:128, :]
+def fine_far_kernel(packet, nears, y_packet, x_packet, row_mats, x_sum, y_far, x_parent, y_parent):
+    for b in range(4):
+        x_parent[b] = x_packet[b, 80:120, :]
+        y_parent[b] = y_packet[b, 80:120, :]
     own, x_far, y_column = ([ref[b, 0:80, :] for b in range(4)] for ref in (packet, x_packet, y_packet))
     stacks = ([own, [nears[0, b] for b in range(4)], x_far], [y_column])
     row_pass(FINE_ROWS, row_mats, stacks, (x_sum, y_far))
@@ -349,8 +351,8 @@
 def coarse_kernel(packet, xfar, xother, yfar, yother, row_mats, y_mats, z_mats,
                   up_rows, up_y, up_z, fine_term, out, wide, grown, turned,
                   x_sum, far_side, other_side, centre, *scratch):
-    own = [packet[b, 80:128, :] for b in range(4)]
-    others = [[ref[b] for b in range(4)] for ref in (xfar, xother, yfar, yother)]
+    own = [packet[b, 80:120, :].astype(F32) for b in range(4)]
+    others = [[ref[b].astype(F32) for b in range(4)] for ref in (xfar, xother, yfar, yother)]
     stacks = ([own, others[0], others[1]], [others[2]], [others[3]], [own])
     parts = (x_sum, far_side, other_side, centre)
     row_pass(COARSE_ROWS, row_mats, stacks, parts)
@@ -405,14 +407,14 @@
     columns = [fine_source, near(fine_source, "gx"), near(fine_source, "gy"), corner(fine_source)]
     *blocks, fine_rows, down_rows, down_y, down_z = early(fine_blocks, coarse_blocks, child_filter_matrices)
     packet, nears = source(columns, down_rows, down_y, down_z)
-    x_packet, y_packet = far(packet, "gx"), far(packet, "gy")
+    y_packet, x_packet = far(packet, "gy"), far(packet, "gx")
     fine_y, fine_z, *mats = late(blocks)
     part = jax.ShapeDtypeStruct((TERMS, 4 * FINE_ROWS, 128), BF)
-    parent = jax.ShapeDtypeStruct((4, COARSE_ROWS, 128), BF)
+    parent = jax.ShapeDtypeStruct((4, PARENT_ROWS, 128), BF)
     y_near, centre = small_call(fine_near_kernel, "fine_near", (part, part), 10**9, packet, nears, fine_rows)
     x_sum, y_far, x_parent, y_parent = small_call(
         fine_far_kernel, "fine_far", (part, part, parent, parent), 10**9,
-        packet, nears, x_packet, y_packet, fine_rows,
+        packet, nears, y_packet, x_packet, fine_rows,
     )
     x_other, y_other = near(x_parent, "gx"), near(y_parent, "gy")
     fine_term = small_call(

time: 34.4 us -> 31.4 us (0.913)
  the two profiles are of different devices: /device:TPU:90 before, /device:TPU:130 now
where the time goes in v5:
time: 31.4 us; the launch traced here: 30.9 us
  Pallas kernels  13.7 us (44%)
  starting transfers between devices  9.51 us (30%)
  waiting for transfers between devices  7.54 us (24%)
    pallas_call x5, Pallas kernels, small_call(): pl.pallas_call(kernel, out_shape=out_shape, name=name, scratch_shapes=scr...  9.97 us
    ppermute x2, starting transfers between devices, far(): lax.ppermute(block, axis, [(i, (i + 1 ^ 1) - 1) for i in range(1, count -...  7.28 us
    ppermute x2, waiting for transfers between devices, far(): lax.ppermute(block, axis, [(i, (i + 1 ^ 1) - 1) for i in range(1, count -...  3.88 us
    ppermute x4, waiting for transfers between devices, near(): lax.ppermute(block, axis, [(i, i ^ 1) for i in range(lax.axis_size(axis))])  2.61 us
    pallas_call x1, Pallas kernels, early(): pl.pallas_call(early_kernel, out_shape=out_shape, name='early', in_specs=...  2.36 us
    ppermute x4, starting transfers between devices, near(): lax.ppermute(block, axis, [(i, i ^ 1) for i in range(lax.axis_size(axis))])  1.95 us
    pallas_call x1, Pallas kernels, source(): pl.pallas_call(source_kernel, out_shape=out_shape, scratch_shapes=scratch...  1.38 us
    ppermute x1, waiting for transfers between devices, corner(): return lax.ppermute(block, ('gx', 'gy'), route)  1.05 us
  transfers between devices with their start and end apart: 7, of which 4 were waited for; matrix products, arithmetic and copies ran while one was open for 0% of the time, Pallas kernels for 25%

profile of v5, /device:TPU:130, one launch (start us, length us, event | category | flops | bytes accessed | tf_op | source)
XLA Modules:
  0.0 30.9 jit_solution(10806919335965290512)
XLA Ops:
  0.0 0.0 collective-permute-start
  0.0 1.6 %collective-permute-start.1 = (bf16[1,1,4,8000]{3,2,1,0:T(4,128)(2,1)}, bf16[1,1,4,8000]{3,2,1,0:T(4,128)(2,1)S(1)}, u32[]{:S(2)}, u32[]{:S(2)}) collective-permute-start(bf16[1,1,4,8000]{3,2,1,0:T(4,128)(2,1)} %own.1), channel_id=1, source_target_pairs={{0,1},{1,0},{2,3},{3,2},{4,5},{5,4},{6,7},{7,6},{8,9},{9,8},{10,11... | collective-permute-start | bytes 192008 | tf_op jit(solution)/shard_map/ppermute | solution.py:392
  1.6 0.3 collective-permute-start.2
  1.9 0.0 copy-start
  1.9 2.4 %early.1 = (bf16[3,12,20,20]{3,2,1,0:T(8,128)(2,1)S(1)}, bf16[3,12,20,20]{3,2,1,0:T(8,128)(2,1)S(1)}, bf16[20,2,20]{2,1,0:T(2,128)(2,1)S(1)}, bf16[12,2,80,128]{...) custom-call(bf16[3,12,20,20]{3,2,1,0:T(8,128)(2,1)} %fine_hbm.1, ...), custom_call_target="tpu_custom_call" | custom-call | flops 2000000000 | bytes 4000000 | tf_op jit(solution)/shard_map/early/pallas_call | solution.py:212
  4.2 0.0 collective-permute-done.xnear
  4.2 0.5 %collective-permute-done.1.ynear = bf16[1,1,4,8000]{3,2,1,0:T(4,128)(2,1)S(1)} collective-permute-done((bf16[1,1,4,8000]{3,2,1,0:T(4,128)(2,1)}, bf16[1,1,4,8000]{3,2,1,0:T(4,128)(2,1)S(1)}, u32[]{:S(2)}, u32[]{:S(2)}) %collective-permute-start.1) | collective-permute-done | bytes 64032 | tf_op jit(solution)/shard_map/ppermute | solution.py:392
  4.7 1.1 %collective-permute-done.2.corner = bf16[1,1,4,8000]{3,2,1,0:T(4,128)(2,1)S(1)} collective-permute-done((bf16[1,1,4,8000]{3,2,1,0:T(4,128)(2,1)}, bf16[1,1,4,8000]{3,2,1,0:T(4,128)(2,1)S(1)}, u32[]{:S(2)}, u32[]{:S(2)}) %collective-permute-start.2) | collective-permute-done | bytes 64032 | tf_op jit(solution)/shard_map/ppermute | solution.py:403
  5.8 0.0 copy-done
  5.8 1.4 %source.1 = (bf16[4,120,128]{2,1,0:T(8,128)(2,1)S(1)}, bf16[2,4,80,128]{3,2,1,0:T(8,128)(2,1)S(1)}) custom-call(bf16[1,1,4,8000]{3,2,1,0:T(4,128)(2,1)S(1)} %copy-done, bf16[1,1,4,8000]{3,2,1,0:T(4,128)(2,1)S(1)} %collective-permute-done.xnear, bf16[1,1,4,8000]{3,2,1,0:T(4,128)(2,1)S(1)} %collective-permute-done.1.ynear, ...), custom_call_target="tpu_custom_call" | custom-call | flops 1000000000 | bytes 1000000 | tf_op jit(solution)/shard_map/source/pallas_call | solution.py:274
  7.1 3.9 %collective-permute-start.3 = (bf16[4,120,128]{2,1,0:T(8,128)(2,1)S(1)}, bf16[4,120,128]{2,1,0:T(8,128)(2,1)S(1)}, u32[]{:S(2)}, u32[]{:S(2)}) collective-permute-start(bf16[4,120,128]{2,1,0:T(8,128)(2,1)S(1)} %get-tuple-element.31.packet), channel_id=1, source_target_pairs={{1,2},{2,1},{3,4},{4,3},{5,6},{6,5},{7,8},{8,7},{9,10},{10,9},{11,... | collective-permute-start | bytes 368648 | tf_op jit(solution)/shard_map/ppermute | solution.py:397
  11.0 3.4 %collective-permute-start.4 = (bf16[4,120,128]{2,1,0:T(8,128)(2,1)S(1)}, bf16[4,120,128]{2,1,0:T(8,128)(2,1)S(1)}, u32[]{:S(2)}, u32[]{:S(2)}) collective-permute-start(bf16[4,120,128]{2,1,0:T(8,128)(2,1)S(1)} %get-tuple-element.31.packet), channel_id=1, source_target_pairs={{16,32},{32,16},{48,64},{64,48},{80,96},{96,80},{112,128},{128,112... | collective-permute-start | bytes 368648 | tf_op jit(solution)/shard_map/ppermute | solution.py:397
  14.4 3.0 %late.1 = (bf16[12,3,128,128]{3,2,1,0:T(8,128)(2,1)S(1)}, bf16[3,12,128,128]{3,2,1,0:T(8,128)(2,1)S(1)}, bf16[12,2,48,128]{3,2,1,0:T(8,128)(2,1)S(1)}, bf16[12,3...) custom-call(bf16[3,12,20,20]{3,2,1,0:T(8,128)(2,1)S(1)} %get-tuple-e, ...), custom_call_target="tpu_custom_call" | custom-call | flops 2000000000 | bytes 4000000 | tf_op jit(solution)/shard_map/late/pallas_call | solution.py:344
  17.4 0.6 %fine_near.1 = (bf16[12,320,128]{2,1,0:T(8,128)(2,1)S(1)}, bf16[12,320,128]{2,1,0:T(8,128)(2,1)S(1)}) custom-call(bf16[4,120,128]{2,1,0:T(8,128)(2,1)S(1)} %get-tuple-element.31.packet, bf16[2,4,80,128]{3,2,1,0:T(8,128)(2,1)S(1)} %get-tuple-element.32.nears, bf16[12,2,80,128]{3,2,1,0:T(8,128)(2,1)S(1)} %get-tuple-element.33.row_mats), custom_call_target="tpu_custom_call" | custom-call | flops 1000000000 | bytes 4000000 | tf_op jit(solution)/shard_map/fine_near/pallas_call | solution.py:344
  18.1 3.9 %collective-permute-done.3.y_packet = bf16[4,120,128]{2,1,0:T(8,128)(2,1)S(1)} collective-permute-done((bf16[4,120,128]{2,1,0:T(8,128)(2,1)S(1)}, bf16[4,120,128]{2,1,0:T(8,128)(2,1)S(1)}, u32[]{:S(2)}, u32[]{:S(2)}) %collective-permute-start.3) | collective-permute-done | bytes 122912 | tf_op jit(solution)/shard_map/ppermute | solution.py:397
  22.0 0.0 collective-permute-done.4.x_packet
  22.0 1.0 %fine_far.1 = (bf16[12,320,128]{2,1,0:T(8,128)(2,1)S(1)}, bf16[12,320,128]{2,1,0:T(8,128)(2,1)S(1)}, bf16[4,40,128]{2,1,0:T(8,128)(2,1)S(1)}, bf16[4,40,128]{2,1,0:T(8,128)(2,1)S(1)}) custom-call(bf16[4,120,128]{2,1,0:T(8,128)(2,1)S(1)} %get-tuple-element.31.packet, bf16[2,4,80,128]{3,2,1,0:T(8,128)(2,1)S(1)} %get-tuple-element.32.nears, ...), custom_call_target="tpu_custom_call" | custom-call | flops 1000000000 | bytes 4000000 | tf_op jit(solution)/shard_map/fine_far/pallas_call | solution.py:344
  22.9 0.1 collective-permute-start.5
  23.0 0.3 collective-permute-start.6
  23.3 1.8 %fine_rest.1.fine_term = f32[320,128]{1,0:T(8,128)S(1)} custom-call(bf16[12,320,128]{2,1,0:T(8,128)(2,1)S(1)} %get-tuple-element.45.x_sum, bf16[12,320,128]{2,1,0:T(8,128)(2,1)S(1)} %get-tuple-element.46.y_near, bf16[12,320,128]{2,1,0:T(8,128)(2,1)S(1)} %get-tuple-element.47.y_far, bf16[12,320,128]{2,1,0:T(8,128)(2,1)S(1)} %get-tuple-element.48.centre, ...), custom_call_target="tpu_custom_call" | custom-call | flops 4000000000 | bytes 4000000 | tf_op jit(solution)/shard_map/fine_rest/pallas_call | solution.py:344
  25.1 0.0 collective-permute-done.5.xother
  25.2 2.2 %collective-permute-done.6.yother = bf16[4,40,128]{2,1,0:T(8,128)(2,1)S(1)} collective-permute-done((bf16[4,40,128]{2,1,0:T(8,128)(2,1)S(1)}, bf16[4,40,128]{2,1,0:T(8,128)(2,1)S(1)}, u32[]{:S(2)}, u32[]{:S(2)}) %collective-permute-start.6) | collective-permute-done | bytes 40992 | tf_op jit(solution)/shard_map/ppermute | solution.py:392
  27.3 3.6 %coarse.1 = f32[1,1,4,8000]{3,2,1,0:T(4,128)} custom-call(bf16[4,120,128]{2,1,0:T(8,128)(2,1)S(1)} %get-tuple-element.31.packet, bf16[4,40,128]{2,1,0:T(8,128)(2,1)S(1)} %get-tuple-element.34.xfar, bf16[4,40,128]{2,1,0:T(8,128)(2,1)S(1)} %collective-permute-done.5.xother, bf16[4,40,128]{2,1,0:T(8,128)(2,1)S(1)} %get-tuple-element.35.yfar, ...), custom_call_target="tpu_custom_call" | custom-call | flops 4000000000 | bytes 4000000 | tf_op jit(solution)/shard_map/coarse/pallas_call | solution.py:344
Async XLA Ops:
  0.0 4.2 %collective-permute-start = (bf16[1,1,4,8000]{3,2,1,0:T(4,128)(2,1)}, bf16[1,1,4,8000]{3,2,1,0:T(4,128)(2,1)S(1)}, u32[]{:S(2)}, u32[]{:S(2)}) collective-permute-start(bf16[1,1,4,8000]{3,2,1,0:T(4,128)(2,1)} %own.1), channel_id=1, source_target_pairs={{0,16},{16,0},{32,48},{48,32},{64,80},{80,64},{96,112},{112,96},{1... | collective-permute-start | bytes 192008 | tf_op jit(solution)/shard_map/ppermute | solution.py:392
  0.0 4.7 %collective-permute-start.1 = (bf16[1,1,4,8000]{3,2,1,0:T(4,128)(2,1)}, bf16[1,1,4,8000]{3,2,1,0:T(4,128)(2,1)S(1)}, u32[]{:S(2)}, u32[]{:S(2)}) collective-permute-start(bf16[1,1,4,8000]{3,2,1,0:T(4,128)(2,1)} %own.1), channel_id=1, source_target_pairs={{0,1},{1,0},{2,3},{3,2},{4,5},{5,4},{6,7},{7,6},{8,9},{9,8},{10,11... | collective-permute-start | bytes 192008 | tf_op jit(solution)/shard_map/ppermute | solution.py:392
  1.6 4.2 %collective-permute-start.2 = (bf16[1,1,4,8000]{3,2,1,0:T(4,128)(2,1)}, bf16[1,1,4,8000]{3,2,1,0:T(4,128)(2,1)S(1)}, u32[]{:S(2)}, u32[]{:S(2)}) collective-permute-start(bf16[1,1,4,8000]{3,2,1,0:T(4,128)(2,1)} %own.1), channel_id=1, source_target_pairs={{0,17},{1,16},{2,19},{3,18},{4,21},{5,20},{6,23},{7,22},{8,25},{9,... | collective-permute-start | bytes 192008 | tf_op jit(solution)/shard_map/ppermute | solution.py:403
  1.9 3.9 %copy-start = (bf16[1,1,4,8000]{3,2,1,0:T(4,128)(2,1)S(1)}, bf16[1,1,4,8000]{3,2,1,0:T(4,128)(2,1)}, u32[]{:S(2)}) copy-start(bf16[1,1,4,8000]{3,2,1,0:T(4,128)(2,1)} %own.1) | copy-start | bytes 192004
  7.1 14.8 %collective-permute-start.3 = (bf16[4,120,128]{2,1,0:T(8,128)(2,1)S(1)}, bf16[4,120,128]{2,1,0:T(8,128)(2,1)S(1)}, u32[]{:S(2)}, u32[]{:S(2)}) collective-permute-start(bf16[4,120,128]{2,1,0:T(8,128)(2,1)S(1)} %get-tuple-element.31.packet), channel_id=1, source_target_pairs={{1,2},{2,1},{3,4},{4,3},{5,6},{6,5},{7,8},{8,7},{9,10},{10,9},{11,... | collective-permute-start | bytes 368648 | tf_op jit(solution)/shard_map/ppermute | solution.py:397
  11.0 10.9 %collective-permute-start.4 = (bf16[4,120,128]{2,1,0:T(8,128)(2,1)S(1)}, bf16[4,120,128]{2,1,0:T(8,128)(2,1)S(1)}, u32[]{:S(2)}, u32[]{:S(2)}) collective-permute-start(bf16[4,120,128]{2,1,0:T(8,128)(2,1)S(1)} %get-tuple-element.31.packet), channel_id=1, source_target_pairs={{16,32},{32,16},{48,64},{64,48},{80,96},{96,80},{112,128},{128,112... | collective-permute-start | bytes 368648 | tf_op jit(solution)/shard_map/ppermute | solution.py:397
  22.9 2.2 %collective-permute-start.5 = (bf16[4,40,128]{2,1,0:T(8,128)(2,1)S(1)}, bf16[4,40,128]{2,1,0:T(8,128)(2,1)S(1)}, u32[]{:S(2)}, u32[]{:S(2)}) collective-permute-start(bf16[4,40,128]{2,1,0:T(8,128)(2,1)S(1)} %get-tuple-element.34.xfar), channel_id=1, source_target_pairs={{0,16},{16,0},{32,48},{48,32},{64,80},{80,64},{96,112},{112,96},{1... | collective-permute-start | bytes 122888 | tf_op jit(solution)/shard_map/ppermute | solution.py:392
  23.0 4.3 %collective-permute-start.6 = (bf16[4,40,128]{2,1,0:T(8,128)(2,1)S(1)}, bf16[4,40,128]{2,1,0:T(8,128)(2,1)S(1)}, u32[]{:S(2)}, u32[]{:S(2)}) collective-permute-start(bf16[4,40,128]{2,1,0:T(8,128)(2,1)S(1)} %get-tuple-element.35.yfar), channel_id=1, source_target_pairs={{0,1},{1,0},{2,3},{3,2},{4,5},{5,4},{6,7},{7,6},{8,9},{9,8},{10,11... | collective-permute-start | bytes 122888 | tf_op jit(solution)/shard_map/ppermute | solution.py:392

commit v6 on v5

--- a/solution.py
+++ b/solution.py
@@ -113,8 +113,29 @@
     return jnp.where(which == 0, first, second).astype(BF), jnp.where(which == 0, second, first).astype(BF)
 
 
-def early_kernel(fine_hbm, coarse_hbm, child_hbm, fine_ref, coarse_ref, child_ref,
-                 fine_rows, down_rows, down_y, down_z, plain, sems):
+def lane_level(turned, wide_y, wide_z, y_out, z_out, on_j, along_k, order_y):
+    both = jnp.concatenate([on_j[1], along_k[1]], axis=1)
+    wide = dot(turned[...].reshape(3 * TERMS * 32, K2).astype(BF), both).astype(BF)
+    wide_y[...] = wide[:, 0:128].reshape(3, TERMS, 32, 128)
+    wide_z[...] = wide[:, 128:256].reshape(3, TERMS, 32, 128)
+    for (spread, _, mask), source_ref, order, out in (
+        (on_j, wide_y, order_y, y_out), (along_k, wide_z, (1, 2, 0), z_out),
+    ):
+        for m in range(0, TERMS, 2):
+            tiles = [source_ref[d, m + c] for c in range(2) for d in order]
+            mats = dot(spread, jnp.concatenate(tiles, axis=1))
+            for c in range(2):
+                for e in range(3):
+                    lane = 384 * c + 128 * e
+                    tile = (mats[:, lane:lane + 128] * mask).astype(BF)
+                    if out is y_out:
+                        out[m + c, e] = tile
+                    else:
+                        out[e, m + c] = tile
+
+
+def early_kernel(fine_hbm, coarse_hbm, child_hbm, coarse_ref, child_ref,
+                 fine_rows, fine_y, fine_z, down_rows, down_y, down_z, fine_ref, plain, turned, wide_y, wide_z, sems):
     copies = [
         pltpu.make_async_copy(src, dst, sems.at[n])
         for n, (src, dst) in enumerate(((fine_hbm, fine_ref), (coarse_hbm, coarse_ref), (child_hbm, child_ref)))
@@ -122,14 +143,18 @@
     for copy in copies:
         copy.start()
     plain[...] = jnp.zeros(plain.shape, F32)
+    turned[...] = jnp.zeros(turned.shape, F32)
     px, py = parity()
-    on_j, on_k = lane_constants(True), lane_constants(False)
+    on_j, on_k, to_natural = lane_constants(True), lane_constants(False), lane_constants(False, True)
     for copy in copies:
         copy.wait()
     for d in range(3):
         for m in range(TERMS):
-            plain[d, m, 0:K2, :] = fine_ref[d, m].astype(F32)
-    near_x = 2 - 2 * px
+            matrix = fine_ref[d, m].astype(F32)
+            plain[d, m, 0:K2, :] = matrix
+            turned[d, m, 0:K2, :] = matrix.T
+    near_x, near_y = 2 - 2 * px, 2 - 2 * py
+    lane_level(turned, wide_y, wide_z, fine_y, fine_z, on_j, to_natural, (1, near_y, 2 - near_y))
     spread_rows_of(fine_rows, plain, FINE_ROWS, 4, (1, near_x, 2 - near_x))
     own_x, other_x = chosen(child_ref, px)
     own_y, other_y = chosen(child_ref, py)
@@ -149,42 +174,19 @@
     down_rows[...] = (mixed * onehot((2 * (r & 1) + cz) == (lane & 3), F32)).astype(BF)
 
 
-def late_kernel(fine_ref, coarse_ref, child_ref, fine_y, fine_z, coarse_rows, coarse_y, coarse_z,
+def late_kernel(coarse_ref, child_ref, coarse_rows, coarse_y, coarse_z,
                 up_rows, up_y, up_z, plain, turned, wide_y, wide_z):
     plain[...] = jnp.zeros(plain.shape, F32)
     turned[...] = jnp.zeros(turned.shape, F32)
     px, py = parity()
     on_j, on_k, to_natural = lane_constants(True), lane_constants(False), lane_constants(False, True)
     near_x, near_y = 2 - 2 * px, 2 - 2 * py
-    for n, blocks in enumerate((fine_ref, coarse_ref)):
-        for d in range(3):
-            for m in range(TERMS):
-                matrix = blocks[d, m].astype(F32)
-                turned[n, d, m, 0:K2, :] = matrix.T
-                if n == 1:
-                    plain[d, m, 0:K2, :] = matrix
-    levels = (
-        (fine_y, fine_z, to_natural, (1, near_y, 2 - near_y)), (coarse_y, coarse_z, on_k, (1, 2 - near_y, near_y)),
-    )
-    for n, (y_out, z_out, along_k, order_y) in enumerate(levels):
-        both = jnp.concatenate([on_j[1], along_k[1]], axis=1)
-        wide = dot(turned[n].reshape(3 * TERMS * 32, K2).astype(BF), both).astype(BF)
-        wide_y[n] = wide[:, 0:128].reshape(3, TERMS, 32, 128)
-        wide_z[n] = wide[:, 128:256].reshape(3, TERMS, 32, 128)
-        for (spread, _, mask), source_ref, order, out in (
-            (on_j, wide_y, order_y, y_out), (along_k, wide_z, (1, 2, 0), z_out),
-        ):
-            for m in range(0, TERMS, 2):
-                tiles = [source_ref[n, d, m + c] for c in range(2) for d in order]
-                mats = dot(spread, jnp.concatenate(tiles, axis=1))
-                for c in range(2):
-                    for e in range(3):
-                        lane = 384 * c + 128 * e
-                        tile = (mats[:, lane:lane + 128] * mask).astype(BF)
-                        if out is y_out:
-                            out[m + c, e] = tile
-                        else:
-                            out[e, m + c] = tile
+    for d in range(3):
+        for m in range(TERMS):
+            matrix = coarse_ref[d, m].astype(F32)
+            plain[d, m, 0:K2, :] = matrix
+            turned[d, m, 0:K2, :] = matrix.T
+    lane_level(turned, wide_y, wide_z, coarse_y, coarse_z, on_j, on_k, (1, 2 - near_y, near_y))
     spread_rows_of(coarse_rows, plain, COARSE_ROWS, 2, (1, 2 - near_x, near_x))
     own_x, _ = chosen(child_ref, px)
     own_y, _ = chosen(child_ref, py)
@@ -206,27 +208,27 @@
         pltpu.with_memory_space_constraint(x, pltpu.HBM)
         for x in (fine_blocks, coarse_blocks, jnp.transpose(child, (1, 0, 2)))
     ]
-    out_shape = tuple(bf16(*x.shape) for x in operands) + (
-        bf16(TERMS, 2, FINE_ROWS, 128), bf16(96, 160), bf16(256, 128), bf16(256, 128),
+    out_shape = tuple(bf16(*x.shape) for x in operands[1:]) + (
+        bf16(TERMS, 2, FINE_ROWS, 128), bf16(TERMS, 3, 128, 128), bf16(3, TERMS, 128, 128),
+        bf16(96, 160), bf16(256, 128), bf16(256, 128),
     )
     return pl.pallas_call(
         early_kernel, out_shape=out_shape, name="early",
         in_specs=[pl.BlockSpec(memory_space=pltpu.HBM)] * 3,
-        scratch_shapes=[pltpu.VMEM((3, TERMS, 32, K2), F32), pltpu.SemaphoreType.DMA((3,))],
+        scratch_shapes=[pltpu.VMEM(operands[0].shape, BF)] + lane_scratch() + [pltpu.SemaphoreType.DMA((3,))],
         compiler_params=pltpu.CompilerParams(vmem_limit_bytes=16 << 20),
         cost_estimate=pl.CostEstimate(flops=2 * 10**9, bytes_accessed=4 * 10**6, transcendentals=0),
     )(*operands)
 
 
+def lane_scratch():
+    return [pltpu.VMEM((3, TERMS, 32, K2), F32)] * 2 + [pltpu.VMEM((3, TERMS, 32, 128), BF)] * 2
+
+
 def late(blocks):
-    level = (bf16(TERMS, 3, 128, 128), bf16(3, TERMS, 128, 128))
-    out_shape = level + (bf16(TERMS, 2, COARSE_ROWS, 128),) + level
+    out_shape = (bf16(TERMS, 2, COARSE_ROWS, 128), bf16(TERMS, 3, 128, 128), bf16(3, TERMS, 128, 128))
     out_shape += (bf16(80, 48), bf16(128, 128), bf16(2, 128, 128))
-    scratch = [
-        pltpu.VMEM((3, TERMS, 32, K2), F32), pltpu.VMEM((2, 3, TERMS, 32, K2), F32),
-        pltpu.VMEM((2, 3, TERMS, 32, 128), BF), pltpu.VMEM((2, 3, TERMS, 32, 128), BF),
-    ]
-    return small_call(late_kernel, "late", out_shape, 2 * 10**9, *blocks, scratch=scratch)
+    return small_call(late_kernel, "late", out_shape, 2 * 10**9, *blocks, scratch=lane_scratch())
 
 
 def source_kernel(own, xnear, ynear, corner, down_rows, down_y, down_z,
@@ -285,12 +287,16 @@
 def row_pass(rows, row_mats, stacks, targets):
     stacks = [[joined(column) for column in stack] for stack in stacks]
     stacks = [(stack[0] if len(stack) == 1 else jnp.concatenate(stack, axis=0)).astype(BF) for stack in stacks]
-    for m in range(TERMS):
-        mats = jnp.concatenate([row_mats[m, 0], row_mats[m, 1]], axis=1)
-        for stack, target in zip(stacks, targets):
-            result = dot(mats[:, 0:stack.shape[0]], stack)
-            for b in range(4):
-                target[m, b * rows:b * rows + rows, :] = result[:, 128 * b:128 * b + 128].astype(BF)
+    chunk = 3
+    for stack, target in zip(stacks, targets):
+        for start in range(0, TERMS, chunk):
+            mats = [row_mats[start:start + chunk, c].reshape(chunk * rows, 128) for c in range(2)]
+            result = dot(jnp.concatenate(mats, axis=1)[:, 0:stack.shape[0]], stack)
+            for c in range(chunk):
+                for b in range(4):
+                    target[start + c, b * rows:b * rows + rows, :] = (
+                        result[c * rows:(c + 1) * rows, 128 * b:128 * b + 128].astype(BF)
+                    )
 
 
 def level_rest(rows, nz, parts, y_mats, z_mats, sums, centres):
@@ -327,10 +333,13 @@
     row_pass(FINE_ROWS, row_mats, ([[nears[1, b] for b in range(4)]], [own]), (y_near, centre))
 
 
-def fine_far_kernel(packet, nears, y_packet, x_packet, row_mats, x_sum, y_far, x_parent, y_parent):
-    for b in range(4):
+def parents_kernel(x_packet, y_packet, y_parent, x_parent):
+    for b in range(4):
+        y_parent[b] = y_packet[b, 80:120, :]
         x_parent[b] = x_packet[b, 80:120, :]
-        y_parent[b] = y_packet[b, 80:120, :]
+
+
+def fine_far_kernel(packet, nears, y_packet, x_packet, row_mats, x_sum, y_far):
     own, x_far, y_column = ([ref[b, 0:80, :] for b in range(4)] for ref in (packet, x_packet, y_packet))
     stacks = ([own, [nears[0, b] for b in range(4)], x_far], [y_column])
     row_pass(FINE_ROWS, row_mats, stacks, (x_sum, y_far))
@@ -405,18 +414,18 @@
 
 def shards(fine_source, fine_blocks, coarse_blocks, child_filter_matrices):
     columns = [fine_source, near(fine_source, "gx"), near(fine_source, "gy"), corner(fine_source)]
-    *blocks, fine_rows, down_rows, down_y, down_z = early(fine_blocks, coarse_blocks, child_filter_matrices)
+    *blocks, fine_rows, fine_y, fine_z, down_rows, down_y, down_z = early(fine_blocks, coarse_blocks, child_filter_matrices)
     packet, nears = source(columns, down_rows, down_y, down_z)
     y_packet, x_packet = far(packet, "gy"), far(packet, "gx")
-    fine_y, fine_z, *mats = late(blocks)
+    mats = late(blocks)
     part = jax.ShapeDtypeStruct((TERMS, 4 * FINE_ROWS, 128), BF)
     parent = jax.ShapeDtypeStruct((4, PARENT_ROWS, 128), BF)
     y_near, centre = small_call(fine_near_kernel, "fine_near", (part, part), 10**9, packet, nears, fine_rows)
-    x_sum, y_far, x_parent, y_parent = small_call(
-        fine_far_kernel, "fine_far", (part, part, parent, parent), 10**9,
-        packet, nears, y_packet, x_packet, fine_rows,
-    )
-    x_other, y_other = near(x_parent, "gx"), near(y_parent, "gy")
+    y_parent, x_parent = small_call(parents_kernel, "parents", (parent, parent), 10**6, x_packet, y_packet)
+    y_other, x_other = near(y_parent, "gy"), near(x_parent, "gx")
+    x_sum, y_far = small_call(
+        fine_far_kernel, "fine_far", (part, part), 10**9, packet, nears, y_packet, x_packet, fine_rows,
+    )
     fine_term = small_call(
         fine_rest_kernel, "fine_rest", jax.ShapeDtypeStruct((4 * FINE_ROWS, 128), F32), 4 * 10**9,
         x_sum, y_near, y_far, centre, fine_y, fine_z, scratch=level_scratch(FINE_ROWS),

time: 31.4 us -> 30.3 us (0.965)
  the two profiles are of different devices: /device:TPU:130 before, /device:TPU:120 now
where the time goes in v6:
time: 30.3 us; the launch traced here: 30.2 us
  Pallas kernels  13.2 us (44%)
  starting transfers between devices  12.2 us (40%)
  waiting for transfers between devices  4.64 us (15%)
    pallas_call x6, Pallas kernels, small_call(): pl.pallas_call(kernel, out_shape=out_shape, name=name, scratch_shapes=scr...  8.6 us
    ppermute x2, starting transfers between devices, far(): lax.ppermute(block, axis, [(i, (i + 1 ^ 1) - 1) for i in range(1, count -...  7.94 us
    pallas_call x1, Pallas kernels, early(): pl.pallas_call(early_kernel, out_shape=out_shape, name='early', in_specs=...  3.24 us
    ppermute x2, waiting for transfers between devices, far(): lax.ppermute(block, axis, [(i, (i + 1 ^ 1) - 1) for i in range(1, count -...  3.13 us
    ppermute x4, starting transfers between devices, near(): lax.ppermute(block, axis, [(i, i ^ 1) for i in range(lax.axis_size(axis))])  2.9 us
    ppermute x4, waiting for transfers between devices, near(): lax.ppermute(block, axis, [(i, i ^ 1) for i in range(lax.axis_size(axis))])  1.5 us
    ppermute x1, starting transfers between devices, corner(): return lax.ppermute(block, ('gx', 'gy'), route)  1.39 us
    pallas_call x1, Pallas kernels, source(): pl.pallas_call(source_kernel, out_shape=out_shape, scratch_shapes=scratch...  1.38 us
  transfers between devices with their start and end apart: 7, of which 3 were waited for; matrix products, arithmetic and copies ran while one was open for 0% of the time, Pallas kernels for 28%

profile of v6, /device:TPU:120, one launch (start us, length us, event | category | flops | bytes accessed | tf_op | source)
XLA Modules:
  0.0 30.2 jit_solution(13629454321815797838)
XLA Ops:
  0.0 0.7 %collective-permute-start.1 = (bf16[1,1,4,8000]{3,2,1,0:T(4,128)(2,1)}, bf16[1,1,4,8000]{3,2,1,0:T(4,128)(2,1)S(1)}, u32[]{:S(2)}, u32[]{:S(2)}) collective-permute-start(bf16[1,1,4,8000]{3,2,1,0:T(4,128)(2,1)} %own.1), channel_id=1, source_target_pairs={{0,1},{1,0},{2,3},{3,2},{4,5},{5,4},{6,7},{7,6},{8,9},{9,8},{10,11... | collective-permute-start | bytes 192008 | tf_op jit(solution)/shard_map/ppermute | solution.py:401
  0.7 0.0 collective-permute-start
  0.7 1.4 %collective-permute-start.2 = (bf16[1,1,4,8000]{3,2,1,0:T(4,128)(2,1)}, bf16[1,1,4,8000]{3,2,1,0:T(4,128)(2,1)S(1)}, u32[]{:S(2)}, u32[]{:S(2)}) collective-permute-start(bf16[1,1,4,8000]{3,2,1,0:T(4,128)(2,1)} %own.1), channel_id=1, source_target_pairs={{0,17},{1,16},{2,19},{3,18},{4,21},{5,20},{6,23},{7,22},{8,25},{9,... | collective-permute-start | bytes 192008 | tf_op jit(solution)/shard_map/ppermute | solution.py:412
  2.1 0.0 copy-start
  2.1 3.2 %early.1 = (bf16[3,12,20,20]{3,2,1,0:T(8,128)(2,1)S(1)}, bf16[20,2,20]{2,1,0:T(2,128)(2,1)S(1)}, bf16[12,2,80,128]{3,2,1,0:T(8,128)(2,1)S(1)}, bf16[12,3,128,128...) custom-call(bf16[3,12,20,20]{3,2,1,0:T(8,128)(2,1)} %fine_hbm.1, ...), custom_call_target="tpu_custom_call" | custom-call | flops 2000000000 | bytes 4000000 | tf_op jit(solution)/shard_map/early/pallas_call | solution.py:215
  5.4 0.0 collective-permute-done.1.ynear
  5.4 0.0 collective-permute-done.xnear
  5.4 0.0 collective-permute-done.2.corner
  5.4 0.0 copy-done
  5.4 1.4 %source.1 = (bf16[4,120,128]{2,1,0:T(8,128)(2,1)S(1)}, bf16[2,4,80,128]{3,2,1,0:T(8,128)(2,1)S(1)}) custom-call(bf16[1,1,4,8000]{3,2,1,0:T(4,128)(2,1)S(1)} %copy-done, bf16[1,1,4,8000]{3,2,1,0:T(4,128)(2,1)S(1)} %collective-permute-done.xnear, bf16[1,1,4,8000]{3,2,1,0:T(4,128)(2,1)S(1)} %collective-permute-done.1.ynear, ...), custom_call_target="tpu_custom_call" | custom-call | flops 1000000000 | bytes 1000000 | tf_op jit(solution)/shard_map/source/pallas_call | solution.py:276
  6.8 5.2 %collective-permute-start.4 = (bf16[4,120,128]{2,1,0:T(8,128)(2,1)S(1)}, bf16[4,120,128]{2,1,0:T(8,128)(2,1)S(1)}, u32[]{:S(2)}, u32[]{:S(2)}) collective-permute-start(bf16[4,120,128]{2,1,0:T(8,128)(2,1)S(1)} %get-tuple-element.30.packet), channel_id=1, source_target_pairs={{1,2},{2,1},{3,4},{4,3},{5,6},{6,5},{7,8},{8,7},{9,10},{10,9},{11,... | collective-permute-start | bytes 368648 | tf_op jit(solution)/shard_map/ppermute | solution.py:406
  12.0 2.8 %collective-permute-start.3 = (bf16[4,120,128]{2,1,0:T(8,128)(2,1)S(1)}, bf16[4,120,128]{2,1,0:T(8,128)(2,1)S(1)}, u32[]{:S(2)}, u32[]{:S(2)}) collective-permute-start(bf16[4,120,128]{2,1,0:T(8,128)(2,1)S(1)} %get-tuple-element.30.packet), channel_id=1, source_target_pairs={{16,32},{32,16},{48,64},{64,48},{80,96},{96,80},{112,128},{128,112... | collective-permute-start | bytes 368648 | tf_op jit(solution)/shard_map/ppermute | solution.py:406
  14.8 2.0 %late.1 = (bf16[12,2,48,128]{3,2,1,0:T(8,128)(2,1)S(1)}, bf16[12,3,128,128]{3,2,1,0:T(8,128)(2,1)S(1)}, bf16[3,12,128,128]{3,2,1,0:T(8,128)(2,1)S(1)}, bf16[80,4...) custom-call(bf16[3,12,20,20]{3,2,1,0:T(8,128)(2,1)S(1)} %get-tuple-element.33.coarse_ref, ...), custom_call_target="tpu_custom_call" | custom-call | flops 2000000000 | bytes 4000000 | tf_op jit(solution)/shard_map/late/pallas_call | solution.py:353
  16.8 0.6 %fine_near.1 = (bf16[12,320,128]{2,1,0:T(8,128)(2,1)S(1)}, bf16[12,320,128]{2,1,0:T(8,128)(2,1)S(1)}) custom-call(bf16[4,120,128]{2,1,0:T(8,128)(2,1)S(1)} %get-tuple-element.30.packet, bf16[2,4,80,128]{3,2,1,0:T(8,128)(2,1)S(1)} %get-tuple-element.41.nears, bf16[12,2,80,128]{3,2,1,0:T(8,128)(2,1)S(1)} %get-tuple-element.42.row_mats), custom_call_target="tpu_custom_call" | custom-call | flops 1000000000 | bytes 4000000 | tf_op jit(solution)/shard_map/fine_near/pallas_call | solution.py:353
  17.4 1.7 %collective-permute-done.4.y_packet = bf16[4,120,128]{2,1,0:T(8,128)(2,1)S(1)} collective-permute-done((bf16[4,120,128]{2,1,0:T(8,128)(2,1)S(1)}, bf16[4,120,128]{2,1,0:T(8,128)(2,1)S(1)}, u32[]{:S(2)}, u32[]{:S(2)}) %collective-permute-start.4) | collective-permute-done | bytes 122912 | tf_op jit(solution)/shard_map/ppermute | solution.py:406
  19.1 1.4 %collective-permute-done.3.x_packet = bf16[4,120,128]{2,1,0:T(8,128)(2,1)S(1)} collective-permute-done((bf16[4,120,128]{2,1,0:T(8,128)(2,1)S(1)}, bf16[4,120,128]{2,1,0:T(8,128)(2,1)S(1)}, u32[]{:S(2)}, u32[]{:S(2)}) %collective-permute-start.3) | collective-permute-done | bytes 122912 | tf_op jit(solution)/shard_map/ppermute | solution.py:406
  20.6 2.2 %collective-permute-start.5 = (bf16[4,40,128]{2,1,0:T(8,128)(2,1)S(1)}, bf16[4,40,128]{2,1,0:T(8,128)(2,1)S(1)}, u32[]{:S(2)}, u32[]{:S(2)}) collective-permute-start(bf16[4,40,128]{2,1,0:T(8,128)(2,1)S(1)} %get-tuple-element.31.xfar), channel_id=1, source_target_pairs={{0,16},{16,0},{32,48},{48,32},{64,80},{80,64},{96,112},{112,96},{1... | collective-permute-start | bytes 122888 | tf_op jit(solution)/shard_map/ppermute | solution.py:401
  22.7 0.0 collective-permute-start.6
  22.7 0.7 %fine_far.1 = (bf16[12,320,128]{2,1,0:T(8,128)(2,1)S(1)}, bf16[12,320,128]{2,1,0:T(8,128)(2,1)S(1)}) custom-call(bf16[4,120,128]{2,1,0:T(8,128)(2,1)S(1)} %get-tuple-element.30.packet, bf16[2,4,80,128]{3,2,1,0:T(8,128)(2,1)S(1)} %get-tuple-element.41.nears, bf16[4,120,128]{2,1,0:T(8,128)(2,1)S(1)} %collective-permute-done.4.y_packet, ...), custom_call_target="tpu_custom_call" | custom-call | flops 1000000000 | bytes 4000000 | tf_op jit(solution)/shard_map/fine_far/pallas_call | solution.py:353
  23.4 1.8 %fine_rest.1.fine_term = f32[320,128]{1,0:T(8,128)S(1)} custom-call(bf16[12,320,128]{2,1,0:T(8,128)(2,1)S(1)} %get-tuple-element.43.x_sum, bf16[12,320,128]{2,1,0:T(8,128)(2,1)S(1)} %get-tuple-element.44.y_near, bf16[12,320,128]{2,1,0:T(8,128)(2,1)S(1)} %get-tuple-element.45.y_far, bf16[12,320,128]{2,1,0:T(8,128)(2,1)S(1)} %get-tuple-element.46.centre, ...), custom_call_target="tpu_custom_call" | custom-call | flops 4000000000 | bytes 4000000 | tf_op jit(solution)/shard_map/fine_rest/pallas_call | solution.py:353
  25.2 0.0 collective-permute-done.5.xother
  25.2 1.5 %collective-permute-done.6.yother = bf16[4,40,128]{2,1,0:T(8,128)(2,1)S(1)} collective-permute-done((bf16[4,40,128]{2,1,0:T(8,128)(2,1)S(1)}, bf16[4,40,128]{2,1,0:T(8,128)(2,1)S(1)}, u32[]{:S(2)}, u32[]{:S(2)}) %collective-permute-start.6) | collective-permute-done | bytes 40992 | tf_op jit(solution)/shard_map/ppermute | solution.py:401
  26.7 3.5 %coarse.1 = f32[1,1,4,8000]{3,2,1,0:T(4,128)} custom-call(bf16[4,120,128]{2,1,0:T(8,128)(2,1)S(1)} %get-tuple-element.30.packet, bf16[4,40,128]{2,1,0:T(8,128)(2,1)S(1)} %get-tuple-element.31.xfar, bf16[4,40,128]{2,1,0:T(8,128)(2,1)S(1)} %collective-permute-done.5.xother, bf16[4,40,128]{2,1,0:T(8,128)(2,1)S(1)} %get-tuple-element.32.yfar, ...), custom_call_target="tpu_custom_call" | custom-call | flops 4000000000 | bytes 4000000 | tf_op jit(solution)/shard_map/coarse/pallas_call | solution.py:353
  (1 shorter events, 0.0 us)
Async XLA Ops:
  0.0 5.4 %collective-permute-start.1 = (bf16[1,1,4,8000]{3,2,1,0:T(4,128)(2,1)}, bf16[1,1,4,8000]{3,2,1,0:T(4,128)(2,1)S(1)}, u32[]{:S(2)}, u32[]{:S(2)}) collective-permute-start(bf16[1,1,4,8000]{3,2,1,0:T(4,128)(2,1)} %own.1), channel_id=1, source_target_pairs={{0,1},{1,0},{2,3},{3,2},{4,5},{5,4},{6,7},{7,6},{8,9},{9,8},{10,11... | collective-permute-start | bytes 192008 | tf_op jit(solution)/shard_map/ppermute | solution.py:401
  0.7 4.7 %collective-permute-start = (bf16[1,1,4,8000]{3,2,1,0:T(4,128)(2,1)}, bf16[1,1,4,8000]{3,2,1,0:T(4,128)(2,1)S(1)}, u32[]{:S(2)}, u32[]{:S(2)}) collective-permute-start(bf16[1,1,4,8000]{3,2,1,0:T(4,128)(2,1)} %own.1), channel_id=1, source_target_pairs={{0,16},{16,0},{32,48},{48,32},{64,80},{80,64},{96,112},{112,96},{1... | collective-permute-start | bytes 192008 | tf_op jit(solution)/shard_map/ppermute | solution.py:401
  0.7 4.7 %collective-permute-start.2 = (bf16[1,1,4,8000]{3,2,1,0:T(4,128)(2,1)}, bf16[1,1,4,8000]{3,2,1,0:T(4,128)(2,1)S(1)}, u32[]{:S(2)}, u32[]{:S(2)}) collective-permute-start(bf16[1,1,4,8000]{3,2,1,0:T(4,128)(2,1)} %own.1), channel_id=1, source_target_pairs={{0,17},{1,16},{2,19},{3,18},{4,21},{5,20},{6,23},{7,22},{8,25},{9,... | collective-permute-start | bytes 192008 | tf_op jit(solution)/shard_map/ppermute | solution.py:412
  2.1 3.3 %copy-start = (bf16[1,1,4,8000]{3,2,1,0:T(4,128)(2,1)S(1)}, bf16[1,1,4,8000]{3,2,1,0:T(4,128)(2,1)}, u32[]{:S(2)}) copy-start(bf16[1,1,4,8000]{3,2,1,0:T(4,128)(2,1)} %own.1) | copy-start | bytes 192004
  6.8 12.3 %collective-permute-start.4 = (bf16[4,120,128]{2,1,0:T(8,128)(2,1)S(1)}, bf16[4,120,128]{2,1,0:T(8,128)(2,1)S(1)}, u32[]{:S(2)}, u32[]{:S(2)}) collective-permute-start(bf16[4,120,128]{2,1,0:T(8,128)(2,1)S(1)} %get-tuple-element.30.packet), channel_id=1, source_target_pairs={{1,2},{2,1},{3,4},{4,3},{5,6},{6,5},{7,8},{8,7},{9,10},{10,9},{11,... | collective-permute-start | bytes 368648 | tf_op jit(solution)/shard_map/ppermute | solution.py:406
  12.0 8.5 %collective-permute-start.3 = (bf16[4,120,128]{2,1,0:T(8,128)(2,1)S(1)}, bf16[4,120,128]{2,1,0:T(8,128)(2,1)S(1)}, u32[]{:S(2)}, u32[]{:S(2)}) collective-permute-start(bf16[4,120,128]{2,1,0:T(8,128)(2,1)S(1)} %get-tuple-element.30.packet), channel_id=1, source_target_pairs={{16,32},{32,16},{48,64},{64,48},{80,96},{96,80},{112,128},{128,112... | collective-permute-start | bytes 368648 | tf_op jit(solution)/shard_map/ppermute | solution.py:406
  20.6 4.7 %collective-permute-start.5 = (bf16[4,40,128]{2,1,0:T(8,128)(2,1)S(1)}, bf16[4,40,128]{2,1,0:T(8,128)(2,1)S(1)}, u32[]{:S(2)}, u32[]{:S(2)}) collective-permute-start(bf16[4,40,128]{2,1,0:T(8,128)(2,1)S(1)} %get-tuple-element.31.xfar), channel_id=1, source_target_pairs={{0,16},{16,0},{32,48},{48,32},{64,80},{80,64},{96,112},{112,96},{1... | collective-permute-start | bytes 122888 | tf_op jit(solution)/shard_map/ppermute | solution.py:401
  22.7 4.0 %collective-permute-start.6 = (bf16[4,40,128]{2,1,0:T(8,128)(2,1)S(1)}, bf16[4,40,128]{2,1,0:T(8,128)(2,1)S(1)}, u32[]{:S(2)}, u32[]{:S(2)}) collective-permute-start(bf16[4,40,128]{2,1,0:T(8,128)(2,1)S(1)} %get-tuple-element.32.yfar), channel_id=1, source_target_pairs={{0,1},{1,0},{2,3},{3,2},{4,5},{5,4},{6,7},{7,6},{8,9},{9,8},{10,11... | collective-permute-start | bytes 122888 | tf_op jit(solution)/shard_map/ppermute | solution.py:401

commit v7 on v6

--- a/solution.py
+++ b/solution.py
@@ -299,41 +299,50 @@
                     )
 
 
-def level_rest(rows, nz, parts, y_mats, z_mats, sums, centres):
-    zero = jnp.zeros((128, 128), BF)
-    for m in range(TERMS):
-        mats = jnp.concatenate([
-            jnp.concatenate([y_mats[m, 0], y_mats[m, 1], y_mats[m, 2], zero], axis=0),
-            jnp.concatenate([zero, zero, zero, y_mats[m, 0]], axis=0),
-        ], axis=1)
-        result = dot(jnp.concatenate([part[m] for part in parts], axis=1), mats)
-        for n, target in enumerate((sums, centres)):
-            blocks = exchange([result[b * rows:(b + 1) * rows, 128 * n:128 * n + 128] for b in range(4)])
+def y_pass(rows, parts, y_mats, target):
+    zero = jnp.zeros((128 * len(parts), 128), BF)
+    for m in range(0, TERMS, 2):
+        one, two = (jnp.concatenate([y_mats[m + c, n] for n in range(len(parts))], axis=0) for c in range(2))
+        mats = jnp.concatenate(
+            [jnp.concatenate([one, zero], axis=0), jnp.concatenate([zero, two], axis=0)], axis=1
+        )
+        values = jnp.concatenate([part[m + c] for c in range(2) for part in parts], axis=1)
+        result = dot(values, mats)
+        for c in range(2):
+            blocks = exchange([result[b * rows:(b + 1) * rows, 128 * c:128 * c + 128] for b in range(4)])
             for b in range(4):
-                target[m, b * rows:(b + 1) * rows, :] = blocks[b].astype(BF)
-    total = dot(jnp.concatenate([sums[m] for m in range(TERMS)], axis=1), z_mats[0].reshape(TERMS * 128, 128))
+                target[m + c, b * rows:(b + 1) * rows, :] = blocks[b].astype(BF)
+
+
+def level_vertical(rows, nz, centre, y_mats, z_mats, scratch):
+    y_pass(rows, (centre,), y_mats, scratch)
     sides = dot(
-        jnp.concatenate([centres[m] for m in range(TERMS)], axis=1),
-        jnp.concatenate([z_mats[n].reshape(TERMS * 128, 128) for n in (1, 2)], axis=1),
+        joined([scratch[m] for m in range(TERMS)]),
+        joined([z_mats[n].reshape(TERMS * 128, 128) for n in (1, 2)]),
     )
     z = iota((4 * rows, 128), 0) & (nz - 1)
-    total = total + jnp.where(z == nz - 1, 0.0, pltpu.roll(sides[:, 0:128], 4 * rows - 1, 0))
-    return total + jnp.where(z == 0, 0.0, pltpu.roll(sides[:, 128:256], 1, 0))
-
-
-def level_scratch(rows):
-    return [
-        pltpu.VMEM((TERMS, 4 * rows, 128), BF),
-        pltpu.VMEM((TERMS, 4 * rows, 128), BF),
-    ]
-
-
-def fine_near_kernel(packet, nears, row_mats, y_near, centre):
+    upper = jnp.where(z == nz - 1, 0.0, pltpu.roll(sides[:, 0:128], 4 * rows - 1, 0))
+    return upper + jnp.where(z == 0, 0.0, pltpu.roll(sides[:, 128:256], 1, 0))
+
+
+def level_rest(rows, parts, y_mats, z_mats, scratch):
+    y_pass(rows, parts, y_mats, scratch)
+    return dot(joined([scratch[m] for m in range(TERMS)]), z_mats[0].reshape(TERMS * 128, 128))
+
+
+def fine_near_kernel(packet, nears, row_mats, y_mats, z_mats, y_near, vertical, centre, scratch):
     own = [packet[b, 0:80, :] for b in range(4)]
     row_pass(FINE_ROWS, row_mats, ([[nears[1, b] for b in range(4)]], [own]), (y_near, centre))
-
-
-def parents_kernel(x_packet, y_packet, y_parent, x_parent):
+    vertical[...] = level_vertical(FINE_ROWS, 4, centre, y_mats, z_mats, scratch)
+
+
+def coarse_near_kernel(packet, row_mats, y_mats, z_mats, vertical, centre, scratch):
+    own = [packet[b, 80:120, :].astype(F32) for b in range(4)]
+    row_pass(COARSE_ROWS, row_mats, ([own],), (centre,))
+    vertical[...] = level_vertical(COARSE_ROWS, 2, centre, y_mats, z_mats, scratch)
+
+
+def parents_kernel(y_packet, x_packet, y_parent, x_parent):
     for b in range(4):
         y_parent[b] = y_packet[b, 80:120, :]
         x_parent[b] = x_packet[b, 80:120, :]
@@ -345,8 +354,8 @@
     row_pass(FINE_ROWS, row_mats, stacks, (x_sum, y_far))
 
 
-def fine_rest_kernel(x_sum, y_near, y_far, centre, y_mats, z_mats, out, sums, centres):
-    out[...] = level_rest(FINE_ROWS, 4, (x_sum, y_near, y_far, centre), y_mats, z_mats, sums, centres)
+def fine_rest_kernel(x_sum, y_near, y_far, vertical, y_mats, z_mats, out, scratch):
+    out[...] = vertical[...] + level_rest(FINE_ROWS, (x_sum, y_near, y_far), y_mats, z_mats, scratch)
 
 
 def small_call(kernel, name, out_shape, flops, *operands, scratch=()):
@@ -357,15 +366,13 @@
     )(*operands)
 
 
-def coarse_kernel(packet, xfar, xother, yfar, yother, row_mats, y_mats, z_mats,
-                  up_rows, up_y, up_z, fine_term, out, wide, grown, turned,
-                  x_sum, far_side, other_side, centre, *scratch):
+def coarse_kernel(packet, xfar, xother, yfar, yother, vertical, row_mats, y_mats, z_mats,
+                  up_rows, up_y, up_z, fine_term, out, wide, grown, turned, x_sum, far_side, other_side, scratch):
     own = [packet[b, 80:120, :].astype(F32) for b in range(4)]
     others = [[ref[b].astype(F32) for b in range(4)] for ref in (xfar, xother, yfar, yother)]
-    stacks = ([own, others[0], others[1]], [others[2]], [others[3]], [own])
-    parts = (x_sum, far_side, other_side, centre)
-    row_pass(COARSE_ROWS, row_mats, stacks, parts)
-    result = level_rest(COARSE_ROWS, 2, parts, y_mats, z_mats, *scratch)
+    parts = (x_sum, far_side, other_side)
+    row_pass(COARSE_ROWS, row_mats, ([own, others[0], others[1]], [others[2]], [others[3]]), parts)
+    result = vertical[...] + level_rest(COARSE_ROWS, parts, y_mats, z_mats, scratch)
     blocks = exchange([result[48 * b:48 * b + 48, :] for b in range(4)])
     for b in range(4):
         wide[:, 128 * b:128 * b + 128] = blocks[b].astype(BF)
@@ -391,7 +398,7 @@
         pltpu.VMEM((COARSE_ROWS, 512), BF),
         pltpu.VMEM((320, 128), BF),
         pltpu.VMEM((320, 128), BF),
-    ] + [part] * 4 + level_scratch(COARSE_ROWS)
+    ] + [part] * 4
     return small_call(
         coarse_kernel, "coarse", jax.ShapeDtypeStruct((1, 1, 4, 8000), F32), 4 * 10**9, *operands, scratch=scratch
     )
@@ -417,20 +424,31 @@
     *blocks, fine_rows, fine_y, fine_z, down_rows, down_y, down_z = early(fine_blocks, coarse_blocks, child_filter_matrices)
     packet, nears = source(columns, down_rows, down_y, down_z)
     y_packet, x_packet = far(packet, "gy"), far(packet, "gx")
+    blocks, _ = lax.optimization_barrier((tuple(blocks), packet))
     mats = late(blocks)
     part = jax.ShapeDtypeStruct((TERMS, 4 * FINE_ROWS, 128), BF)
     parent = jax.ShapeDtypeStruct((4, PARENT_ROWS, 128), BF)
-    y_near, centre = small_call(fine_near_kernel, "fine_near", (part, part), 10**9, packet, nears, fine_rows)
-    y_parent, x_parent = small_call(parents_kernel, "parents", (parent, parent), 10**6, x_packet, y_packet)
+    fine_part = pltpu.VMEM((TERMS, 4 * FINE_ROWS, 128), BF)
+    coarse_part = pltpu.VMEM((TERMS, 4 * COARSE_ROWS, 128), BF)
+    fine_sum = jax.ShapeDtypeStruct((4 * FINE_ROWS, 128), F32)
+    coarse_sum = jax.ShapeDtypeStruct((4 * COARSE_ROWS, 128), F32)
+    y_near, fine_vertical = small_call(
+        fine_near_kernel, "fine_near", (part, fine_sum), 2 * 10**9,
+        packet, nears, fine_rows, fine_y, fine_z, scratch=[fine_part] * 2,
+    )
+    coarse_vertical = small_call(
+        coarse_near_kernel, "coarse_near", coarse_sum, 10**9, packet, *mats[0:3], scratch=[coarse_part] * 2,
+    )
+    y_parent, x_parent = small_call(parents_kernel, "parents", (parent, parent), 10**6, y_packet, x_packet)
     y_other, x_other = near(y_parent, "gy"), near(x_parent, "gx")
     x_sum, y_far = small_call(
         fine_far_kernel, "fine_far", (part, part), 10**9, packet, nears, y_packet, x_packet, fine_rows,
     )
     fine_term = small_call(
-        fine_rest_kernel, "fine_rest", jax.ShapeDtypeStruct((4 * FINE_ROWS, 128), F32), 4 * 10**9,
-        x_sum, y_near, y_far, centre, fine_y, fine_z, scratch=level_scratch(FINE_ROWS),
-    )
-    return coarse((packet, x_parent, x_other, y_parent, y_other, *mats, fine_term))
+        fine_rest_kernel, "fine_rest", fine_sum, 4 * 10**9,
+        x_sum, y_near, y_far, fine_vertical, fine_y, fine_z, scratch=[fine_part],
+    )
+    return coarse((packet, x_parent, x_other, y_parent, y_other, coarse_vertical, *mats, fine_term))
 
 
 def solution(mesh):

time: 30.3 us -> 30 us (0.990)
  the two profiles are of different devices: /device:TPU:120 before, /device:TPU:130 now
where the time goes in v7:
time: 30 us; the launch traced here: 29.4 us
  Pallas kernels  14.9 us (50%)
  starting transfers between devices  9.51 us (32%)
  waiting for transfers between devices  4.89 us (16%)
    pallas_call x7, Pallas kernels, small_call(): pl.pallas_call(kernel, out_shape=out_shape, name=name, scratch_shapes=scr...  10.3 us
    ppermute x2, starting transfers between devices, far(): lax.ppermute(block, axis, [(i, (i + 1 ^ 1) - 1) for i in range(1, count -...  7.28 us
    pallas_call x1, Pallas kernels, early(): pl.pallas_call(early_kernel, out_shape=out_shape, name='early', in_specs=...  3.25 us
    ppermute x2, waiting for transfers between devices, far(): lax.ppermute(block, axis, [(i, (i + 1 ^ 1) - 1) for i in range(1, count -...  2.34 us
    ppermute x4, starting transfers between devices, near(): lax.ppermute(block, axis, [(i, i ^ 1) for i in range(lax.axis_size(axis))])  1.95 us
    ppermute x4, waiting for transfers between devices, near(): lax.ppermute(block, axis, [(i, i ^ 1) for i in range(lax.axis_size(axis))])  1.94 us
    pallas_call x1, Pallas kernels, source(): pl.pallas_call(source_kernel, out_shape=out_shape, scratch_shapes=scratch...  1.38 us
    ppermute x1, waiting for transfers between devices, corner(): return lax.ppermute(block, ('gx', 'gy'), route)  0.61 us
  transfers between devices with their start and end apart: 7, of which 3 were waited for; matrix products, arithmetic and copies ran while one was open for 0% of the time, Pallas kernels for 36%

profile of v7, /device:TPU:130, one launch (start us, length us, event | category | flops | bytes accessed | tf_op | source)
XLA Modules:
  0.0 29.4 jit_solution(6574709338703086891)
XLA Ops:
  0.0 0.0 collective-permute-start
  0.0 1.6 %collective-permute-start.1 = (bf16[1,1,4,8000]{3,2,1,0:T(4,128)(2,1)}, bf16[1,1,4,8000]{3,2,1,0:T(4,128)(2,1)S(1)}, u32[]{:S(2)}, u32[]{:S(2)}) collective-permute-start(bf16[1,1,4,8000]{3,2,1,0:T(4,128)(2,1)} %own.1), channel_id=1, source_target_pairs={{0,1},{1,0},{2,3},{3,2},{4,5},{5,4},{6,7},{7,6},{8,9},{9,8},{10,11... | collective-permute-start | bytes 192008 | tf_op jit(solution)/shard_map/ppermute | solution.py:408
  1.6 0.3 collective-permute-start.2
  1.9 0.0 copy-start
  1.9 3.2 %early.1 = (bf16[3,12,20,20]{3,2,1,0:T(8,128)(2,1)S(1)}, bf16[20,2,20]{2,1,0:T(2,128)(2,1)S(1)}, bf16[12,2,80,128]{3,2,1,0:T(8,128)(2,1)S(1)}, bf16[12,3,128,128...) custom-call(bf16[3,12,20,20]{3,2,1,0:T(8,128)(2,1)} %fine_hbm.1, ...), custom_call_target="tpu_custom_call" | custom-call | flops 2000000000 | bytes 4000000 | tf_op jit(solution)/shard_map/early/pallas_call | solution.py:215
  5.1 0.0 collective-permute-done.xnear
  5.1 0.0 collective-permute-done.1.ynear
  5.1 0.6 %collective-permute-done.2.corner = bf16[1,1,4,8000]{3,2,1,0:T(4,128)(2,1)S(1)} collective-permute-done((bf16[1,1,4,8000]{3,2,1,0:T(4,128)(2,1)}, bf16[1,1,4,8000]{3,2,1,0:T(4,128)(2,1)S(1)}, u32[]{:S(2)}, u32[]{:S(2)}) %collective-permute-start.2) | collective-permute-done | bytes 64032 | tf_op jit(solution)/shard_map/ppermute | solution.py:419
  5.8 0.0 copy-done
  5.8 1.4 %source.1 = (bf16[4,120,128]{2,1,0:T(8,128)(2,1)S(1)}, bf16[2,4,80,128]{3,2,1,0:T(8,128)(2,1)S(1)}) custom-call(bf16[1,1,4,8000]{3,2,1,0:T(4,128)(2,1)S(1)} %copy-done, bf16[1,1,4,8000]{3,2,1,0:T(4,128)(2,1)S(1)} %collective-permute-done.xnear, bf16[1,1,4,8000]{3,2,1,0:T(4,128)(2,1)S(1)} %collective-permute-done.1.ynear, ...), custom_call_target="tpu_custom_call" | custom-call | flops 1000000000 | bytes 1000000 | tf_op jit(solution)/shard_map/source/pallas_call | solution.py:276
  7.1 3.9 %collective-permute-start.3 = (bf16[4,120,128]{2,1,0:T(8,128)(2,1)S(1)}, bf16[4,120,128]{2,1,0:T(8,128)(2,1)S(1)}, u32[]{:S(2)}, u32[]{:S(2)}) collective-permute-start(bf16[4,120,128]{2,1,0:T(8,128)(2,1)S(1)} %get-tuple-element.32.packet), channel_id=1, source_target_pairs={{1,2},{2,1},{3,4},{4,3},{5,6},{6,5},{7,8},{8,7},{9,10},{10,9},{11,... | collective-permute-start | bytes 368648 | tf_op jit(solution)/shard_map/ppermute | solution.py:413
  11.0 3.4 %collective-permute-start.4 = (bf16[4,120,128]{2,1,0:T(8,128)(2,1)S(1)}, bf16[4,120,128]{2,1,0:T(8,128)(2,1)S(1)}, u32[]{:S(2)}, u32[]{:S(2)}) collective-permute-start(bf16[4,120,128]{2,1,0:T(8,128)(2,1)S(1)} %get-tuple-element.32.packet), channel_id=1, source_target_pairs={{16,32},{32,16},{48,64},{64,48},{80,96},{96,80},{112,128},{128,112... | collective-permute-start | bytes 368648 | tf_op jit(solution)/shard_map/ppermute | solution.py:413
  14.4 2.0 %late.1 = (bf16[12,2,48,128]{3,2,1,0:T(8,128)(2,1)S(1)}, bf16[12,3,128,128]{3,2,1,0:T(8,128)(2,1)S(1)}, bf16[3,12,128,128]{3,2,1,0:T(8,128)(2,1)S(1)}, bf16[80,4...) custom-call(bf16[3,12,20,20]{3,2,1,0:T(8,128)(2,1)S(1)} %get-tuple-element.37.coarse_ref, ...), custom_call_target="tpu_custom_call" | custom-call | flops 2000000000 | bytes 4000000 | tf_op jit(solution)/shard_map/late/pallas_call | solution.py:362
  16.4 2.0 %fine_near.1 = (bf16[12,320,128]{2,1,0:T(8,128)(2,1)S(1)}, f32[320,128]{1,0:T(8,128)S(1)}) custom-call(bf16[4,120,128]{2,1,0:T(8,128)(2,1)S(1)} %get-tuple-element.32.packet, bf16[2,4,80,128]{3,2,1,0:T(8,128)(2,1)S(1)} %get-tuple-element.45.nears, bf16[12,2,80,128]{3,2,1,0:T(8,128)(2,1)S(1)} %get-tuple-element.46.row_mats, ...), custom_call_target="tpu_custom_call" | custom-call | flops 2000000000 | bytes 4000000 | tf_op jit(solution)/shard_map/fine_near/pallas_call | solution.py:362
  18.4 1.2 %coarse_near.1.vertical = f32[192,128]{1,0:T(8,128)S(1)} custom-call(bf16[4,120,128]{2,1,0:T(8,128)(2,1)S(1)} %get-tuple-element.32.packet, bf16[12,2,48,128]{3,2,1,0:T(8,128)(2,1)S(1)} %get-tuple-element.39.row_mats, bf16[12,3,128,128]{3,2,1,0:T(8,128)(2,1)S(1)} %get-tuple-element.40.y_mats, bf16[3,12,128,128]{3,2,1,0:T(8,128)(2,1)S(1)} %get-tuple-element.41.z_mats), custom_call_target="tpu_custom_call" | custom-call | flops 1000000000 | bytes 4000000 | tf_op jit(solution)/shard_map/coarse_near/pallas_call | solution.py:362
  19.6 2.3 %collective-permute-done.3.y_packet = bf16[4,120,128]{2,1,0:T(8,128)(2,1)S(1)} collective-permute-done((bf16[4,120,128]{2,1,0:T(8,128)(2,1)S(1)}, bf16[4,120,128]{2,1,0:T(8,128)(2,1)S(1)}, u32[]{:S(2)}, u32[]{:S(2)}) %collective-permute-start.3) | collective-permute-done | bytes 122912 | tf_op jit(solution)/shard_map/ppermute | solution.py:413
  22.0 0.0 collective-permute-done.4.x_packet
  22.0 0.1 collective-permute-start.5
  22.1 0.3 collective-permute-start.6
  22.4 0.7 %fine_far.1 = (bf16[12,320,128]{2,1,0:T(8,128)(2,1)S(1)}, bf16[12,320,128]{2,1,0:T(8,128)(2,1)S(1)}) custom-call(bf16[4,120,128]{2,1,0:T(8,128)(2,1)S(1)} %get-tuple-element.32.packet, bf16[2,4,80,128]{3,2,1,0:T(8,128)(2,1)S(1)} %get-tuple-element.45.nears, bf16[4,120,128]{2,1,0:T(8,128)(2,1)S(1)} %collective-permute-done.3.y_packet, ...), custom_call_target="tpu_custom_call" | custom-call | flops 1000000000 | bytes 4000000 | tf_op jit(solution)/shard_map/fine_far/pallas_call | solution.py:362
  23.0 1.4 %fine_rest.1.fine_term = f32[320,128]{1,0:T(8,128)S(1)} custom-call(bf16[12,320,128]{2,1,0:T(8,128)(2,1)S(1)} %get-tuple-element.47.x_sum, bf16[12,320,128]{2,1,0:T(8,128)(2,1)S(1)} %get-tuple-element.50.y_near, bf16[12,320,128]{2,1,0:T(8,128)(2,1)S(1)} %get-tuple-element.51.y_far, f32[320,128]{1,0:T(8,128)S(1)} %get-tuple-element.52.vertical, ...), custom_call_target="tpu_custom_call" | custom-call | flops 4000000000 | bytes 4000000 | tf_op jit(solution)/shard_map/fine_rest/pallas_call | solution.py:362
  24.4 0.0 collective-permute-done.5.xother
  24.4 1.9 %collective-permute-done.6.yother = bf16[4,40,128]{2,1,0:T(8,128)(2,1)S(1)} collective-permute-done((bf16[4,40,128]{2,1,0:T(8,128)(2,1)S(1)}, bf16[4,40,128]{2,1,0:T(8,128)(2,1)S(1)}, u32[]{:S(2)}, u32[]{:S(2)}) %collective-permute-start.6) | collective-permute-done | bytes 40992 | tf_op jit(solution)/shard_map/ppermute | solution.py:408
  26.3 3.1 %coarse.1 = f32[1,1,4,8000]{3,2,1,0:T(4,128)} custom-call(bf16[4,120,128]{2,1,0:T(8,128)(2,1)S(1)} %get-tuple-element.32.packet, bf16[4,40,128]{2,1,0:T(8,128)(2,1)S(1)} %get-tuple-element.33.xfar, bf16[4,40,128]{2,1,0:T(8,128)(2,1)S(1)} %collective-permute-done.5.xother, bf16[4,40,128]{2,1,0:T(8,128)(2,1)S(1)} %get-tuple-element.34.yfar, ...), custom_call_target="tpu_custom_call" | custom-call | flops 4000000000 | bytes 4000000 | tf_op jit(solution)/shard_map/coarse/pallas_call | solution.py:362
  (1 shorter events, 0.0 us)
Async XLA Ops:
  0.0 5.1 %collective-permute-start = (bf16[1,1,4,8000]{3,2,1,0:T(4,128)(2,1)}, bf16[1,1,4,8000]{3,2,1,0:T(4,128)(2,1)S(1)}, u32[]{:S(2)}, u32[]{:S(2)}) collective-permute-start(bf16[1,1,4,8000]{3,2,1,0:T(4,128)(2,1)} %own.1), channel_id=1, source_target_pairs={{0,16},{16,0},{32,48},{48,32},{64,80},{80,64},{96,112},{112,96},{1... | collective-permute-start | bytes 192008 | tf_op jit(solution)/shard_map/ppermute | solution.py:408
  0.0 5.1 %collective-permute-start.1 = (bf16[1,1,4,8000]{3,2,1,0:T(4,128)(2,1)}, bf16[1,1,4,8000]{3,2,1,0:T(4,128)(2,1)S(1)}, u32[]{:S(2)}, u32[]{:S(2)}) collective-permute-start(bf16[1,1,4,8000]{3,2,1,0:T(4,128)(2,1)} %own.1), channel_id=1, source_target_pairs={{0,1},{1,0},{2,3},{3,2},{4,5},{5,4},{6,7},{7,6},{8,9},{9,8},{10,11... | collective-permute-start | bytes 192008 | tf_op jit(solution)/shard_map/ppermute | solution.py:408
  1.6 4.2 %collective-permute-start.2 = (bf16[1,1,4,8000]{3,2,1,0:T(4,128)(2,1)}, bf16[1,1,4,8000]{3,2,1,0:T(4,128)(2,1)S(1)}, u32[]{:S(2)}, u32[]{:S(2)}) collective-permute-start(bf16[1,1,4,8000]{3,2,1,0:T(4,128)(2,1)} %own.1), channel_id=1, source_target_pairs={{0,17},{1,16},{2,19},{3,18},{4,21},{5,20},{6,23},{7,22},{8,25},{9,... | collective-permute-start | bytes 192008 | tf_op jit(solution)/shard_map/ppermute | solution.py:419
  1.9 3.9 %copy-start = (bf16[1,1,4,8000]{3,2,1,0:T(4,128)(2,1)S(1)}, bf16[1,1,4,8000]{3,2,1,0:T(4,128)(2,1)}, u32[]{:S(2)}) copy-start(bf16[1,1,4,8000]{3,2,1,0:T(4,128)(2,1)} %own.1) | copy-start | bytes 192004
  7.1 14.8 %collective-permute-start.3 = (bf16[4,120,128]{2,1,0:T(8,128)(2,1)S(1)}, bf16[4,120,128]{2,1,0:T(8,128)(2,1)S(1)}, u32[]{:S(2)}, u32[]{:S(2)}) collective-permute-start(bf16[4,120,128]{2,1,0:T(8,128)(2,1)S(1)} %get-tuple-element.32.packet), channel_id=1, source_target_pairs={{1,2},{2,1},{3,4},{4,3},{5,6},{6,5},{7,8},{8,7},{9,10},{10,9},{11,... | collective-permute-start | bytes 368648 | tf_op jit(solution)/shard_map/ppermute | solution.py:413
  11.0 10.9 %collective-permute-start.4 = (bf16[4,120,128]{2,1,0:T(8,128)(2,1)S(1)}, bf16[4,120,128]{2,1,0:T(8,128)(2,1)S(1)}, u32[]{:S(2)}, u32[]{:S(2)}) collective-permute-start(bf16[4,120,128]{2,1,0:T(8,128)(2,1)S(1)} %get-tuple-element.32.packet), channel_id=1, source_target_pairs={{16,32},{32,16},{48,64},{64,48},{80,96},{96,80},{112,128},{128,112... | collective-permute-start | bytes 368648 | tf_op jit(solution)/shard_map/ppermute | solution.py:413
  22.0 2.4 %collective-permute-start.5 = (bf16[4,40,128]{2,1,0:T(8,128)(2,1)S(1)}, bf16[4,40,128]{2,1,0:T(8,128)(2,1)S(1)}, u32[]{:S(2)}, u32[]{:S(2)}) collective-permute-start(bf16[4,40,128]{2,1,0:T(8,128)(2,1)S(1)} %get-tuple-element.33.xfar), channel_id=1, source_target_pairs={{0,16},{16,0},{32,48},{48,32},{64,80},{80,64},{96,112},{112,96},{1... | collective-permute-start | bytes 122888 | tf_op jit(solution)/shard_map/ppermute | solution.py:408
  22.1 4.3 %collective-permute-start.6 = (bf16[4,40,128]{2,1,0:T(8,128)(2,1)S(1)}, bf16[4,40,128]{2,1,0:T(8,128)(2,1)S(1)}, u32[]{:S(2)}, u32[]{:S(2)}) collective-permute-start(bf16[4,40,128]{2,1,0:T(8,128)(2,1)S(1)} %get-tuple-element.34.yfar), channel_id=1, source_target_pairs={{0,1},{1,0},{2,3},{3,2},{4,5},{5,4},{6,7},{7,6},{8,9},{9,8},{10,11... | collective-permute-start | bytes 122888 | tf_op jit(solution)/shard_map/ppermute | solution.py:408

commit v8 on v7

--- a/solution.py
+++ b/solution.py
@@ -134,11 +134,20 @@
                         out[e, m + c] = tile
 
 
-def early_kernel(fine_hbm, coarse_hbm, child_hbm, coarse_ref, child_ref,
-                 fine_rows, fine_y, fine_z, down_rows, down_y, down_z, fine_ref, plain, turned, wide_y, wide_z, sems):
+def converted(ref, natural, select):
+    values = ref[0, 0].astype(F32)
+    for i in range(K2):
+        natural[4 * i:4 * i + 4, :] = values[:, 400 * i:400 * i + 400]
+    return dot(natural[...].astype(BF), select[...]).astype(BF)
+
+
+def early_kernel(fine_hbm, coarse_hbm, child_hbm, own_hbm, coarse_ref, child_ref, own_blocks, select_out,
+                 fine_rows, fine_y, fine_z, down_rows, down_y, down_z, fine_ref, own_ref, natural, plain, turned, wide_y, wide_z, sems):
     copies = [
         pltpu.make_async_copy(src, dst, sems.at[n])
-        for n, (src, dst) in enumerate(((fine_hbm, fine_ref), (coarse_hbm, coarse_ref), (child_hbm, child_ref)))
+        for n, (src, dst) in enumerate((
+            (fine_hbm, fine_ref), (coarse_hbm, coarse_ref), (child_hbm, child_ref), (own_hbm, own_ref),
+        ))
     ]
     for copy in copies:
         copy.start()
@@ -162,6 +171,10 @@
     down_y[128:256, :] = lane_matrix(flipped(other_y), on_j)
     for c in range(2):
         down_z[128 * c:128 * c + 128, :] = lane_matrix(flipped(child_ref[:, c, :]), on_k)
+    select_out[...] = onehot(iota((400, 512), 0) == natural_place(iota((1, 512), 1)))
+    centre = converted(own_ref, natural, select_out)
+    for b in range(4):
+        own_blocks[b] = centre[:, 128 * b:128 * b + 128]
     lane = iota((1, 160), 1)
     far = lane >= 80
     lane = jnp.where(far, lane - 80, lane)
@@ -203,19 +216,22 @@
     return jax.ShapeDtypeStruct(shape, BF)
 
 
-def early(fine_blocks, coarse_blocks, child):
+def early(fine_blocks, coarse_blocks, child, own):
     operands = [
         pltpu.with_memory_space_constraint(x, pltpu.HBM)
-        for x in (fine_blocks, coarse_blocks, jnp.transpose(child, (1, 0, 2)))
+        for x in (fine_blocks, coarse_blocks, jnp.transpose(child, (1, 0, 2)), own)
     ]
-    out_shape = tuple(bf16(*x.shape) for x in operands[1:]) + (
+    out_shape = tuple(bf16(*x.shape) for x in operands[1:3]) + (
+        bf16(4, FINE_ROWS, 128), bf16(400, 512),
         bf16(TERMS, 2, FINE_ROWS, 128), bf16(TERMS, 3, 128, 128), bf16(3, TERMS, 128, 128),
         bf16(96, 160), bf16(256, 128), bf16(256, 128),
     )
     return pl.pallas_call(
         early_kernel, out_shape=out_shape, name="early",
-        in_specs=[pl.BlockSpec(memory_space=pltpu.HBM)] * 3,
-        scratch_shapes=[pltpu.VMEM(operands[0].shape, BF)] + lane_scratch() + [pltpu.SemaphoreType.DMA((3,))],
+        in_specs=[pl.BlockSpec(memory_space=pltpu.HBM)] * 4,
+        scratch_shapes=[
+            pltpu.VMEM(operands[0].shape, BF), pltpu.VMEM(operands[3].shape, BF), pltpu.VMEM((FINE_ROWS, 400), F32),
+        ] + lane_scratch() + [pltpu.SemaphoreType.DMA((4,))],
         compiler_params=pltpu.CompilerParams(vmem_limit_bytes=16 << 20),
         cost_estimate=pl.CostEstimate(flops=2 * 10**9, bytes_accessed=4 * 10**6, transcendentals=0),
     )(*operands)
@@ -231,18 +247,10 @@
     return small_call(late_kernel, "late", out_shape, 2 * 10**9, *blocks, scratch=lane_scratch())
 
 
-def source_kernel(own, xnear, ynear, corner, down_rows, down_y, down_z,
+def source_kernel(own, select, xnear, ynear, corner, down_rows, down_y, down_z,
                   packet, nears, natural, mixed, turned):
-    select = onehot(iota((400, 512), 0) == natural_place(iota((1, 512), 1)))
-
-    def converted(ref, slot):
-        values = ref[0, 0].astype(F32)
-        for i in range(K2):
-            natural[slot, 4 * i:4 * i + 4, :] = values[:, 400 * i:400 * i + 400]
-        return dot(natural[slot].astype(BF), select).astype(BF)
-
-    centre, diagonal = converted(own, 0), converted(corner, 1)
-    x_near, y_near = converted(xnear, 2), converted(ynear, 3)
+    centre, diagonal = joined([own[b] for b in range(4)]), converted(corner, natural.at[0], select)
+    x_near, y_near = converted(xnear, natural.at[1], select), converted(ynear, natural.at[2], select)
     for b in range(4):
         here = slice(128 * b, 128 * b + 128)
         packet[b, 0:80, :] = centre[:, here]
@@ -269,7 +277,7 @@
         jax.ShapeDtypeStruct((2, 4, FINE_ROWS, 128), BF),
     )
     scratch = [
-        pltpu.VMEM((4, FINE_ROWS, 400), F32),
+        pltpu.VMEM((3, FINE_ROWS, 400), F32),
         pltpu.VMEM((2, 8 * COARSE_ROWS, 128), BF),
         pltpu.VMEM((2, 4 * COARSE_ROWS, 128), BF),
     ]
@@ -366,7 +374,7 @@
     )(*operands)
 
 
-def coarse_kernel(packet, xfar, xother, yfar, yother, vertical, row_mats, y_mats, z_mats,
+def coarse_kernel(packet, yfar, yother, xfar, xother, vertical, row_mats, y_mats, z_mats,
                   up_rows, up_y, up_z, fine_term, out, wide, grown, turned, x_sum, far_side, other_side, scratch):
     own = [packet[b, 80:120, :].astype(F32) for b in range(4)]
     others = [[ref[b].astype(F32) for b in range(4)] for ref in (xfar, xother, yfar, yother)]
@@ -420,11 +428,13 @@
 
 
 def shards(fine_source, fine_blocks, coarse_blocks, child_filter_matrices):
-    columns = [fine_source, near(fine_source, "gx"), near(fine_source, "gy"), corner(fine_source)]
-    *blocks, fine_rows, fine_y, fine_z, down_rows, down_y, down_z = early(fine_blocks, coarse_blocks, child_filter_matrices)
-    packet, nears = source(columns, down_rows, down_y, down_z)
+    columns = [near(fine_source, "gx"), near(fine_source, "gy"), corner(fine_source)]
+    coarse_ref, child_ref, own, select, fine_rows, fine_y, fine_z, *down = early(
+        fine_blocks, coarse_blocks, child_filter_matrices, fine_source
+    )
+    packet, nears = source([own, select] + columns, *down)
     y_packet, x_packet = far(packet, "gy"), far(packet, "gx")
-    blocks, _ = lax.optimization_barrier((tuple(blocks), packet))
+    blocks, _ = lax.optimization_barrier(((coarse_ref, child_ref), packet))
     mats = late(blocks)
     part = jax.ShapeDtypeStruct((TERMS, 4 * FINE_ROWS, 128), BF)
     parent = jax.ShapeDtypeStruct((4, PARENT_ROWS, 128), BF)
@@ -448,7 +458,7 @@
         fine_rest_kernel, "fine_rest", fine_sum, 4 * 10**9,
         x_sum, y_near, y_far, fine_vertical, fine_y, fine_z, scratch=[fine_part],
     )
-    return coarse((packet, x_parent, x_other, y_parent, y_other, coarse_vertical, *mats, fine_term))
+    return coarse((packet, y_parent, y_other, x_parent, x_other, coarse_vertical, *mats, fine_term))
 
 
 def solution(mesh):

time: 30 us -> 29.1 us (0.970); the launches traced: 29.4 us -> 29 us
  waiting for transfers between devices: 4.89 us -> 4.5 us
where the time goes in v8:
time: 29.1 us; the launch traced here: 29 us
  Pallas kernels  14.9 us (51%)
  starting transfers between devices  9.51 us (33%)
  waiting for transfers between devices  4.5 us (15%)
    pallas_call x7, Pallas kernels, small_call(): pl.pallas_call(kernel, out_shape=out_shape, name=name, scratch_shapes=scr...  10.3 us
    ppermute x2, starting transfers between devices, far(): lax.ppermute(block, axis, [(i, (i + 1 ^ 1) - 1) for i in range(1, count -...  7.28 us
    pallas_call x1, Pallas kernels, early(): pl.pallas_call(early_kernel, out_shape=out_shape, name='early', in_specs=...  3.37 us
    ppermute x2, waiting for transfers between devices, far(): lax.ppermute(block, axis, [(i, (i + 1 ^ 1) - 1) for i in range(1, count -...  2.34 us
    ppermute x4, starting transfers between devices, near(): lax.ppermute(block, axis, [(i, i ^ 1) for i in range(lax.axis_size(axis))])  1.95 us
    ppermute x4, waiting for transfers between devices, near(): lax.ppermute(block, axis, [(i, i ^ 1) for i in range(lax.axis_size(axis))])  1.67 us
    pallas_call x1, Pallas kernels, source(): pl.pallas_call(source_kernel, out_shape=out_shape, scratch_shapes=scratch...  1.24 us
  transfers between devices with their start and end apart: 7, of which 3 were waited for; matrix products, arithmetic and copies ran while one was open for 0% of the time, Pallas kernels for 36%

profile of v8, /device:TPU:130, one launch (start us, length us, event | category | flops | bytes accessed | tf_op | source)
XLA Modules:
  0.0 29.0 jit_solution(130820127593048626)
XLA Ops:
  0.0 0.0 collective-permute-start
  0.0 1.6 %collective-permute-start.1 = (bf16[1,1,4,8000]{3,2,1,0:T(4,128)(2,1)}, bf16[1,1,4,8000]{3,2,1,0:T(4,128)(2,1)S(1)}, u32[]{:S(2)}, u32[]{:S(2)}) collective-permute-start(bf16[1,1,4,8000]{3,2,1,0:T(4,128)(2,1)} %own_hbm.1), channel_id=1, source_target_pairs={{0,1},{1,0},{2,3},{3,2},{4,5},{5,4},{6,7},{7,6},{8,9},{9,8},{10,11... | collective-permute-start | bytes 192008 | tf_op jit(solution)/shard_map/ppermute | solution.py:416
  1.6 0.3 collective-permute-start.2
  1.9 3.4 %early.1 = (bf16[3,12,20,20]{3,2,1,0:T(8,128)(2,1)S(1)}, bf16[20,2,20]{2,1,0:T(2,128)(2,1)S(1)}, bf16[4,80,128]{2,1,0:T(8,128)(2,1)S(1)}, bf16[400,512]{1,0:T(8,...) custom-call(bf16[3,12,20,20]{3,2,1,0:T(8,128)(2,1)} %fine_hbm.1, ...), custom_call_target="tpu_custom_call" | custom-call | flops 2000000000 | bytes 4000000 | tf_op jit(solution)/shard_map/early/pallas_call | solution.py:229
  5.2 0.0 collective-permute-done.xnear
  5.3 0.0 collective-permute-done.1.ynear
  5.3 0.5 %collective-permute-done.2.corner = bf16[1,1,4,8000]{3,2,1,0:T(4,128)(2,1)S(1)} collective-permute-done((bf16[1,1,4,8000]{3,2,1,0:T(4,128)(2,1)}, bf16[1,1,4,8000]{3,2,1,0:T(4,128)(2,1)S(1)}, u32[]{:S(2)}, u32[]{:S(2)}) %collective-permute-start.2) | collective-permute-done | bytes 64032 | tf_op jit(solution)/shard_map/ppermute | solution.py:427
  5.8 1.2 %source.1 = (bf16[4,120,128]{2,1,0:T(8,128)(2,1)S(1)}, bf16[2,4,80,128]{3,2,1,0:T(8,128)(2,1)S(1)}) custom-call(bf16[4,80,128]{2,1,0:T(8,128)(2,1)S(1)} %get-tuple-element.31.own, bf16[400,512]{1,0:T(8,128)(2,1)S(1)} %get-tuple-element.32.select, bf16[1,1,4,8000]{3,2,1,0:T(4,128)(2,1)S(1)} %collective-permute-done.xnear, ...), custom_call_target="tpu_custom_call" | custom-call | flops 1000000000 | bytes 1000000 | tf_op jit(solution)/shard_map/source/pallas_call | solution.py:284
  7.0 3.9 %collective-permute-start.3 = (bf16[4,120,128]{2,1,0:T(8,128)(2,1)S(1)}, bf16[4,120,128]{2,1,0:T(8,128)(2,1)S(1)}, u32[]{:S(2)}, u32[]{:S(2)}) collective-permute-start(bf16[4,120,128]{2,1,0:T(8,128)(2,1)S(1)} %get-tuple-element.36.packet), channel_id=1, source_target_pairs={{1,2},{2,1},{3,4},{4,3},{5,6},{6,5},{7,8},{8,7},{9,10},{10,9},{11,... | collective-permute-start | bytes 368648 | tf_op jit(solution)/shard_map/ppermute | solution.py:421
  10.9 3.4 %collective-permute-start.4 = (bf16[4,120,128]{2,1,0:T(8,128)(2,1)S(1)}, bf16[4,120,128]{2,1,0:T(8,128)(2,1)S(1)}, u32[]{:S(2)}, u32[]{:S(2)}) collective-permute-start(bf16[4,120,128]{2,1,0:T(8,128)(2,1)S(1)} %get-tuple-element.36.packet), channel_id=1, source_target_pairs={{16,32},{32,16},{48,64},{64,48},{80,96},{96,80},{112,128},{128,112... | collective-permute-start | bytes 368648 | tf_op jit(solution)/shard_map/ppermute | solution.py:421
  14.3 2.0 %late.1 = (bf16[12,2,48,128]{3,2,1,0:T(8,128)(2,1)S(1)}, bf16[12,3,128,128]{3,2,1,0:T(8,128)(2,1)S(1)}, bf16[3,12,128,128]{3,2,1,0:T(8,128)(2,1)S(1)}, bf16[80,4...) custom-call(bf16[3,12,20,20]{3,2,1,0:T(8,128)(2,1)S(1)} %get-tuple-element.41.coarse_ref, ...), custom_call_target="tpu_custom_call" | custom-call | flops 2000000000 | bytes 4000000 | tf_op jit(solution)/shard_map/late/pallas_call | solution.py:370
  16.3 2.0 %fine_near.1 = (bf16[12,320,128]{2,1,0:T(8,128)(2,1)S(1)}, f32[320,128]{1,0:T(8,128)S(1)}) custom-call(bf16[4,120,128]{2,1,0:T(8,128)(2,1)S(1)} %get-tuple-element.36.packet, bf16[2,4,80,128]{3,2,1,0:T(8,128)(2,1)S(1)} %get-tuple-element.49.nears, bf16[12,2,80,128]{3,2,1,0:T(8,128)(2,1)S(1)} %get-tuple-element.50.row_mats, ...), custom_call_target="tpu_custom_call" | custom-call | flops 2000000000 | bytes 4000000 | tf_op jit(solution)/shard_map/fine_near/pallas_call | solution.py:370
  18.3 1.2 %coarse_near.1.vertical = f32[192,128]{1,0:T(8,128)S(1)} custom-call(bf16[4,120,128]{2,1,0:T(8,128)(2,1)S(1)} %get-tuple-element.36.packet, bf16[12,2,48,128]{3,2,1,0:T(8,128)(2,1)S(1)} %get-tuple-element.43.row_mats, bf16[12,3,128,128]{3,2,1,0:T(8,128)(2,1)S(1)} %get-tuple-element.44.y_mats, bf16[3,12,128,128]{3,2,1,0:T(8,128)(2,1)S(1)} %get-tuple-element.45.z_mats), custom_call_target="tpu_custom_call" | custom-call | flops 1000000000 | bytes 4000000 | tf_op jit(solution)/shard_map/coarse_near/pallas_call | solution.py:370
  19.5 2.3 %collective-permute-done.3.y_packet = bf16[4,120,128]{2,1,0:T(8,128)(2,1)S(1)} collective-permute-done((bf16[4,120,128]{2,1,0:T(8,128)(2,1)S(1)}, bf16[4,120,128]{2,1,0:T(8,128)(2,1)S(1)}, u32[]{:S(2)}, u32[]{:S(2)}) %collective-permute-start.3) | collective-permute-done | bytes 122912 | tf_op jit(solution)/shard_map/ppermute | solution.py:421
  21.8 0.0 collective-permute-done.4.x_packet
  21.8 0.1 collective-permute-start.5
  21.9 0.3 collective-permute-start.6
  22.2 0.7 %fine_far.1 = (bf16[12,320,128]{2,1,0:T(8,128)(2,1)S(1)}, bf16[12,320,128]{2,1,0:T(8,128)(2,1)S(1)}) custom-call(bf16[4,120,128]{2,1,0:T(8,128)(2,1)S(1)} %get-tuple-element.36.packet, bf16[2,4,80,128]{3,2,1,0:T(8,128)(2,1)S(1)} %get-tuple-element.49.nears, bf16[4,120,128]{2,1,0:T(8,128)(2,1)S(1)} %collective-permute-done.3.y_packet, ...), custom_call_target="tpu_custom_call" | custom-call | flops 1000000000 | bytes 4000000 | tf_op jit(solution)/shard_map/fine_far/pallas_call | solution.py:370
  22.9 1.4 %fine_rest.1.fine_term = f32[320,128]{1,0:T(8,128)S(1)} custom-call(bf16[12,320,128]{2,1,0:T(8,128)(2,1)S(1)} %get-tuple-element.51.x_sum, bf16[12,320,128]{2,1,0:T(8,128)(2,1)S(1)} %get-tuple-element.54.y_near, bf16[12,320,128]{2,1,0:T(8,128)(2,1)S(1)} %get-tuple-element.55.y_far, f32[320,128]{1,0:T(8,128)S(1)} %get-tuple-element.56.vertical, ...), custom_call_target="tpu_custom_call" | custom-call | flops 4000000000 | bytes 4000000 | tf_op jit(solution)/shard_map/fine_rest/pallas_call | solution.py:370
  24.3 1.7 %collective-permute-done.5.yother = bf16[4,40,128]{2,1,0:T(8,128)(2,1)S(1)} collective-permute-done((bf16[4,40,128]{2,1,0:T(8,128)(2,1)S(1)}, bf16[4,40,128]{2,1,0:T(8,128)(2,1)S(1)}, u32[]{:S(2)}, u32[]{:S(2)}) %collective-permute-start.5) | collective-permute-done | bytes 40992 | tf_op jit(solution)/shard_map/ppermute | solution.py:416
  25.9 0.0 collective-permute-done.6.xother
  25.9 3.1 %coarse.1 = f32[1,1,4,8000]{3,2,1,0:T(4,128)} custom-call(bf16[4,120,128]{2,1,0:T(8,128)(2,1)S(1)} %get-tuple-element.36.packet, bf16[4,40,128]{2,1,0:T(8,128)(2,1)S(1)} %get-tuple-element.37.yfar, bf16[4,40,128]{2,1,0:T(8,128)(2,1)S(1)} %collective-permute-done.5.yother, bf16[4,40,128]{2,1,0:T(8,128)(2,1)S(1)} %get-tuple-element.38.xfar, ...), custom_call_target="tpu_custom_call" | custom-call | flops 4000000000 | bytes 4000000 | tf_op jit(solution)/shard_map/coarse/pallas_call | solution.py:370
  (1 shorter events, 0.0 us)
Async XLA Ops:
  0.0 5.2 %collective-permute-start = (bf16[1,1,4,8000]{3,2,1,0:T(4,128)(2,1)}, bf16[1,1,4,8000]{3,2,1,0:T(4,128)(2,1)S(1)}, u32[]{:S(2)}, u32[]{:S(2)}) collective-permute-start(bf16[1,1,4,8000]{3,2,1,0:T(4,128)(2,1)} %own_hbm.1), channel_id=1, source_target_pairs={{0,16},{16,0},{32,48},{48,32},{64,80},{80,64},{96,112},{112,96},{1... | collective-permute-start | bytes 192008 | tf_op jit(solution)/shard_map/ppermute | solution.py:416
  0.0 5.3 %collective-permute-start.1 = (bf16[1,1,4,8000]{3,2,1,0:T(4,128)(2,1)}, bf16[1,1,4,8000]{3,2,1,0:T(4,128)(2,1)S(1)}, u32[]{:S(2)}, u32[]{:S(2)}) collective-permute-start(bf16[1,1,4,8000]{3,2,1,0:T(4,128)(2,1)} %own_hbm.1), channel_id=1, source_target_pairs={{0,1},{1,0},{2,3},{3,2},{4,5},{5,4},{6,7},{7,6},{8,9},{9,8},{10,11... | collective-permute-start | bytes 192008 | tf_op jit(solution)/shard_map/ppermute | solution.py:416
  1.6 4.2 %collective-permute-start.2 = (bf16[1,1,4,8000]{3,2,1,0:T(4,128)(2,1)}, bf16[1,1,4,8000]{3,2,1,0:T(4,128)(2,1)S(1)}, u32[]{:S(2)}, u32[]{:S(2)}) collective-permute-start(bf16[1,1,4,8000]{3,2,1,0:T(4,128)(2,1)} %own_hbm.1), channel_id=1, source_target_pairs={{0,17},{1,16},{2,19},{3,18},{4,21},{5,20},{6,23},{7,22},{8,25},{9,... | collective-permute-start | bytes 192008 | tf_op jit(solution)/shard_map/ppermute | solution.py:427
  7.0 14.8 %collective-permute-start.3 = (bf16[4,120,128]{2,1,0:T(8,128)(2,1)S(1)}, bf16[4,120,128]{2,1,0:T(8,128)(2,1)S(1)}, u32[]{:S(2)}, u32[]{:S(2)}) collective-permute-start(bf16[4,120,128]{2,1,0:T(8,128)(2,1)S(1)} %get-tuple-element.36.packet), channel_id=1, source_target_pairs={{1,2},{2,1},{3,4},{4,3},{5,6},{6,5},{7,8},{8,7},{9,10},{10,9},{11,... | collective-permute-start | bytes 368648 | tf_op jit(solution)/shard_map/ppermute | solution.py:421
  10.9 10.9 %collective-permute-start.4 = (bf16[4,120,128]{2,1,0:T(8,128)(2,1)S(1)}, bf16[4,120,128]{2,1,0:T(8,128)(2,1)S(1)}, u32[]{:S(2)}, u32[]{:S(2)}) collective-permute-start(bf16[4,120,128]{2,1,0:T(8,128)(2,1)S(1)} %get-tuple-element.36.packet), channel_id=1, source_target_pairs={{16,32},{32,16},{48,64},{64,48},{80,96},{96,80},{112,128},{128,112... | collective-permute-start | bytes 368648 | tf_op jit(solution)/shard_map/ppermute | solution.py:421
  21.8 4.1 %collective-permute-start.5 = (bf16[4,40,128]{2,1,0:T(8,128)(2,1)S(1)}, bf16[4,40,128]{2,1,0:T(8,128)(2,1)S(1)}, u32[]{:S(2)}, u32[]{:S(2)}) collective-permute-start(bf16[4,40,128]{2,1,0:T(8,128)(2,1)S(1)} %get-tuple-element.37.yfar), channel_id=1, source_target_pairs={{0,1},{1,0},{2,3},{3,2},{4,5},{5,4},{6,7},{7,6},{8,9},{9,8},{10,11... | collective-permute-start | bytes 122888 | tf_op jit(solution)/shard_map/ppermute | solution.py:416
  21.9 4.0 %collective-permute-start.6 = (bf16[4,40,128]{2,1,0:T(8,128)(2,1)S(1)}, bf16[4,40,128]{2,1,0:T(8,128)(2,1)S(1)}, u32[]{:S(2)}, u32[]{:S(2)}) collective-permute-start(bf16[4,40,128]{2,1,0:T(8,128)(2,1)S(1)} %get-tuple-element.38.xfar), channel_id=1, source_target_pairs={{0,16},{16,0},{32,48},{48,32},{64,80},{80,64},{96,112},{112,96},{1... | collective-permute-start | bytes 122888 | tf_op jit(solution)/shard_map/ppermute | solution.py:416

commit v9 on v8

--- a/solution.py
+++ b/solution.py
@@ -247,7 +247,7 @@
     return small_call(late_kernel, "late", out_shape, 2 * 10**9, *blocks, scratch=lane_scratch())
 
 
-def source_kernel(own, select, xnear, ynear, corner, down_rows, down_y, down_z,
+def source_kernel(own, select, ynear, corner, xnear, down_rows, down_y, down_z,
                   packet, nears, natural, mixed, turned):
     centre, diagonal = joined([own[b] for b in range(4)]), converted(corner, natural.at[0], select)
     x_near, y_near = converted(xnear, natural.at[1], select), converted(ynear, natural.at[2], select)
@@ -428,7 +428,7 @@
 
 
 def shards(fine_source, fine_blocks, coarse_blocks, child_filter_matrices):
-    columns = [near(fine_source, "gx"), near(fine_source, "gy"), corner(fine_source)]
+    columns = [near(fine_source, "gy"), corner(fine_source), near(fine_source, "gx")]
     coarse_ref, child_ref, own, select, fine_rows, fine_y, fine_z, *down = early(
         fine_blocks, coarse_blocks, child_filter_matrices, fine_source
     )

time: 29.1 us -> 28.9 us (level)
    ppermute x4, starting transfers between devices: 1.95 us -> 2.51 us  [near(): lax.ppermute(block, axis, [(i, i ^ 1) for i in range(lax.axis_size(axis))])]
    ppermute x2, starting transfers between devices: 7.28 us -> 6.91 us  [far(): lax.ppermute(block, axis, [(i, (i + 1 ^ 1) - 1) for i in range(1, count -...]
  transfers between devices with their start and end apart: 7 -> 7, of which waited for: 3 -> 3; matrix products, arithmetic and copies ran while one was open for 0% -> 0% of each run, Pallas kernels for 36% -> 37%
where the time goes in v9:
time: 28.9 us; the launch traced here: 28.8 us
  Pallas kernels  14.9 us (52%)
  starting transfers between devices  9.42 us (33%)
  waiting for transfers between devices  4.36 us (15%)
    pallas_call x7, Pallas kernels, small_call(): pl.pallas_call(kernel, out_shape=out_shape, name=name, scratch_shapes=scr...  10.3 us
    ppermute x2, starting transfers between devices, far(): lax.ppermute(block, axis, [(i, (i + 1 ^ 1) - 1) for i in range(1, count -...  6.91 us
    pallas_call x1, Pallas kernels, early(): pl.pallas_call(early_kernel, out_shape=out_shape, name='early', in_specs=...  3.37 us
    ppermute x4, starting transfers between devices, near(): lax.ppermute(block, axis, [(i, i ^ 1) for i in range(lax.axis_size(axis))])  2.51 us
    ppermute x2, waiting for transfers between devices, far(): lax.ppermute(block, axis, [(i, (i + 1 ^ 1) - 1) for i in range(1, count -...  2.33 us
    ppermute x4, waiting for transfers between devices, near(): lax.ppermute(block, axis, [(i, i ^ 1) for i in range(lax.axis_size(axis))])  1.67 us
    pallas_call x1, Pallas kernels, source(): pl.pallas_call(source_kernel, out_shape=out_shape, scratch_shapes=scratch...  1.24 us
  transfers between devices with their start and end apart: 7, of which 3 were waited for; matrix products, arithmetic and copies ran while one was open for 0% of the time, Pallas kernels for 37%

profile of v9, /device:TPU:130, one launch (start us, length us, event | category | flops | bytes accessed | tf_op | source)
XLA Modules:
  0.0 28.8 jit_solution(752546245073331900)
XLA Ops:
  0.0 1.6 %collective-permute-start = (bf16[1,1,4,8000]{3,2,1,0:T(4,128)(2,1)}, bf16[1,1,4,8000]{3,2,1,0:T(4,128)(2,1)S(1)}, u32[]{:S(2)}, u32[]{:S(2)}) collective-permute-start(bf16[1,1,4,8000]{3,2,1,0:T(4,128)(2,1)} %own_hbm.1), channel_id=1, source_target_pairs={{0,1},{1,0},{2,3},{3,2},{4,5},{5,4},{6,7},{7,6},{8,9},{9,8},{10,11... | collective-permute-start | bytes 192008 | tf_op jit(solution)/shard_map/ppermute | solution.py:416
  1.6 0.0 collective-permute-start.1
  1.6 0.6 %collective-permute-start.2 = (bf16[1,1,4,8000]{3,2,1,0:T(4,128)(2,1)}, bf16[1,1,4,8000]{3,2,1,0:T(4,128)(2,1)S(1)}, u32[]{:S(2)}, u32[]{:S(2)}) collective-permute-start(bf16[1,1,4,8000]{3,2,1,0:T(4,128)(2,1)} %own_hbm.1), channel_id=1, source_target_pairs={{0,16},{16,0},{32,48},{48,32},{64,80},{80,64},{96,112},{112,96},{1... | collective-permute-start | bytes 192008 | tf_op jit(solution)/shard_map/ppermute | solution.py:416
  2.1 3.4 %early.1 = (bf16[3,12,20,20]{3,2,1,0:T(8,128)(2,1)S(1)}, bf16[20,2,20]{2,1,0:T(2,128)(2,1)S(1)}, bf16[4,80,128]{2,1,0:T(8,128)(2,1)S(1)}, bf16[400,512]{1,0:T(8,...) custom-call(bf16[3,12,20,20]{3,2,1,0:T(8,128)(2,1)} %fine_hbm.1, ...), custom_call_target="tpu_custom_call" | custom-call | flops 2000000000 | bytes 4000000 | tf_op jit(solution)/shard_map/early/pallas_call | solution.py:229
  5.5 0.0 collective-permute-done.ynear
  5.5 0.4 %collective-permute-done.1.corner = bf16[1,1,4,8000]{3,2,1,0:T(4,128)(2,1)S(1)} collective-permute-done((bf16[1,1,4,8000]{3,2,1,0:T(4,128)(2,1)}, bf16[1,1,4,8000]{3,2,1,0:T(4,128)(2,1)S(1)}, u32[]{:S(2)}, u32[]{:S(2)}) %collective-permute-start.1) | collective-permute-done | bytes 64032 | tf_op jit(solution)/shard_map/ppermute | solution.py:427
  5.9 0.0 collective-permute-done.2.xnear
  5.9 1.2 %source.1 = (bf16[4,120,128]{2,1,0:T(8,128)(2,1)S(1)}, bf16[2,4,80,128]{3,2,1,0:T(8,128)(2,1)S(1)}) custom-call(bf16[4,80,128]{2,1,0:T(8,128)(2,1)S(1)} %get-tuple-element.31.own, bf16[400,512]{1,0:T(8,128)(2,1)S(1)} %get-tuple-element.32.select, bf16[1,1,4,8000]{3,2,1,0:T(4,128)(2,1)S(1)} %collective-permute-done.ynear, ...), custom_call_target="tpu_custom_call" | custom-call | flops 1000000000 | bytes 1000000 | tf_op jit(solution)/shard_map/source/pallas_call | solution.py:284
  7.1 3.7 %collective-permute-start.3 = (bf16[4,120,128]{2,1,0:T(8,128)(2,1)S(1)}, bf16[4,120,128]{2,1,0:T(8,128)(2,1)S(1)}, u32[]{:S(2)}, u32[]{:S(2)}) collective-permute-start(bf16[4,120,128]{2,1,0:T(8,128)(2,1)S(1)} %get-tuple-element.36.packet), channel_id=1, source_target_pairs={{1,2},{2,1},{3,4},{4,3},{5,6},{6,5},{7,8},{8,7},{9,10},{10,9},{11,... | collective-permute-start | bytes 368648 | tf_op jit(solution)/shard_map/ppermute | solution.py:421
  10.8 3.2 %collective-permute-start.4 = (bf16[4,120,128]{2,1,0:T(8,128)(2,1)S(1)}, bf16[4,120,128]{2,1,0:T(8,128)(2,1)S(1)}, u32[]{:S(2)}, u32[]{:S(2)}) collective-permute-start(bf16[4,120,128]{2,1,0:T(8,128)(2,1)S(1)} %get-tuple-element.36.packet), channel_id=1, source_target_pairs={{16,32},{32,16},{48,64},{64,48},{80,96},{96,80},{112,128},{128,112... | collective-permute-start | bytes 368648 | tf_op jit(solution)/shard_map/ppermute | solution.py:421
  14.1 2.0 %late.1 = (bf16[12,2,48,128]{3,2,1,0:T(8,128)(2,1)S(1)}, bf16[12,3,128,128]{3,2,1,0:T(8,128)(2,1)S(1)}, bf16[3,12,128,128]{3,2,1,0:T(8,128)(2,1)S(1)}, bf16[80,4...) custom-call(bf16[3,12,20,20]{3,2,1,0:T(8,128)(2,1)S(1)} %get-tuple-element.41.coarse_ref, ...), custom_call_target="tpu_custom_call" | custom-call | flops 2000000000 | bytes 4000000 | tf_op jit(solution)/shard_map/late/pallas_call | solution.py:370
  16.1 2.0 %fine_near.1 = (bf16[12,320,128]{2,1,0:T(8,128)(2,1)S(1)}, f32[320,128]{1,0:T(8,128)S(1)}) custom-call(bf16[4,120,128]{2,1,0:T(8,128)(2,1)S(1)} %get-tuple-element.36.packet, bf16[2,4,80,128]{3,2,1,0:T(8,128)(2,1)S(1)} %get-tuple-element.49.nears, bf16[12,2,80,128]{3,2,1,0:T(8,128)(2,1)S(1)} %get-tuple-element.50.row_mats, ...), custom_call_target="tpu_custom_call" | custom-call | flops 2000000000 | bytes 4000000 | tf_op jit(solution)/shard_map/fine_near/pallas_call | solution.py:370
  18.0 1.2 %coarse_near.1.vertical = f32[192,128]{1,0:T(8,128)S(1)} custom-call(bf16[4,120,128]{2,1,0:T(8,128)(2,1)S(1)} %get-tuple-element.36.packet, bf16[12,2,48,128]{3,2,1,0:T(8,128)(2,1)S(1)} %get-tuple-element.43.row_mats, bf16[12,3,128,128]{3,2,1,0:T(8,128)(2,1)S(1)} %get-tuple-element.44.y_mats, bf16[3,12,128,128]{3,2,1,0:T(8,128)(2,1)S(1)} %get-tuple-element.45.z_mats), custom_call_target="tpu_custom_call" | custom-call | flops 1000000000 | bytes 4000000 | tf_op jit(solution)/shard_map/coarse_near/pallas_call | solution.py:370
  19.2 2.3 %collective-permute-done.3.y_packet = bf16[4,120,128]{2,1,0:T(8,128)(2,1)S(1)} collective-permute-done((bf16[4,120,128]{2,1,0:T(8,128)(2,1)S(1)}, bf16[4,120,128]{2,1,0:T(8,128)(2,1)S(1)}, u32[]{:S(2)}, u32[]{:S(2)}) %collective-permute-start.3) | collective-permute-done | bytes 122912 | tf_op jit(solution)/shard_map/ppermute | solution.py:421
  21.6 0.0 collective-permute-done.4.x_packet
  21.6 0.1 collective-permute-start.5
  21.7 0.3 collective-permute-start.6
  22.0 0.7 %fine_far.1 = (bf16[12,320,128]{2,1,0:T(8,128)(2,1)S(1)}, bf16[12,320,128]{2,1,0:T(8,128)(2,1)S(1)}) custom-call(bf16[4,120,128]{2,1,0:T(8,128)(2,1)S(1)} %get-tuple-element.36.packet, bf16[2,4,80,128]{3,2,1,0:T(8,128)(2,1)S(1)} %get-tuple-element.49.nears, bf16[4,120,128]{2,1,0:T(8,128)(2,1)S(1)} %collective-permute-done.3.y_packet, ...), custom_call_target="tpu_custom_call" | custom-call | flops 1000000000 | bytes 4000000 | tf_op jit(solution)/shard_map/fine_far/pallas_call | solution.py:370
  22.7 1.4 %fine_rest.1.fine_term = f32[320,128]{1,0:T(8,128)S(1)} custom-call(bf16[12,320,128]{2,1,0:T(8,128)(2,1)S(1)} %get-tuple-element.51.x_sum, bf16[12,320,128]{2,1,0:T(8,128)(2,1)S(1)} %get-tuple-element.54.y_near, bf16[12,320,128]{2,1,0:T(8,128)(2,1)S(1)} %get-tuple-element.55.y_far, f32[320,128]{1,0:T(8,128)S(1)} %get-tuple-element.56.vertical, ...), custom_call_target="tpu_custom_call" | custom-call | flops 4000000000 | bytes 4000000 | tf_op jit(solution)/shard_map/fine_rest/pallas_call | solution.py:370
  24.0 1.7 %collective-permute-done.5.yother = bf16[4,40,128]{2,1,0:T(8,128)(2,1)S(1)} collective-permute-done((bf16[4,40,128]{2,1,0:T(8,128)(2,1)S(1)}, bf16[4,40,128]{2,1,0:T(8,128)(2,1)S(1)}, u32[]{:S(2)}, u32[]{:S(2)}) %collective-permute-start.5) | collective-permute-done | bytes 40992 | tf_op jit(solution)/shard_map/ppermute | solution.py:416
  25.7 0.0 collective-permute-done.6.xother
  25.7 3.1 %coarse.1 = f32[1,1,4,8000]{3,2,1,0:T(4,128)} custom-call(bf16[4,120,128]{2,1,0:T(8,128)(2,1)S(1)} %get-tuple-element.36.packet, bf16[4,40,128]{2,1,0:T(8,128)(2,1)S(1)} %get-tuple-element.37.yfar, bf16[4,40,128]{2,1,0:T(8,128)(2,1)S(1)} %collective-permute-done.5.yother, bf16[4,40,128]{2,1,0:T(8,128)(2,1)S(1)} %get-tuple-element.38.xfar, ...), custom_call_target="tpu_custom_call" | custom-call | flops 4000000000 | bytes 4000000 | tf_op jit(solution)/shard_map/coarse/pallas_call | solution.py:370
  (1 shorter events, 0.0 us)
Async XLA Ops:
  0.0 5.5 %collective-permute-start = (bf16[1,1,4,8000]{3,2,1,0:T(4,128)(2,1)}, bf16[1,1,4,8000]{3,2,1,0:T(4,128)(2,1)S(1)}, u32[]{:S(2)}, u32[]{:S(2)}) collective-permute-start(bf16[1,1,4,8000]{3,2,1,0:T(4,128)(2,1)} %own_hbm.1), channel_id=1, source_target_pairs={{0,1},{1,0},{2,3},{3,2},{4,5},{5,4},{6,7},{7,6},{8,9},{9,8},{10,11... | collective-permute-start | bytes 192008 | tf_op jit(solution)/shard_map/ppermute | solution.py:416
  1.6 4.3 %collective-permute-start.1 = (bf16[1,1,4,8000]{3,2,1,0:T(4,128)(2,1)}, bf16[1,1,4,8000]{3,2,1,0:T(4,128)(2,1)S(1)}, u32[]{:S(2)}, u32[]{:S(2)}) collective-permute-start(bf16[1,1,4,8000]{3,2,1,0:T(4,128)(2,1)} %own_hbm.1), channel_id=1, source_target_pairs={{0,17},{1,16},{2,19},{3,18},{4,21},{5,20},{6,23},{7,22},{8,25},{9,... | collective-permute-start | bytes 192008 | tf_op jit(solution)/shard_map/ppermute | solution.py:427
  1.6 4.3 %collective-permute-start.2 = (bf16[1,1,4,8000]{3,2,1,0:T(4,128)(2,1)}, bf16[1,1,4,8000]{3,2,1,0:T(4,128)(2,1)S(1)}, u32[]{:S(2)}, u32[]{:S(2)}) collective-permute-start(bf16[1,1,4,8000]{3,2,1,0:T(4,128)(2,1)} %own_hbm.1), channel_id=1, source_target_pairs={{0,16},{16,0},{32,48},{48,32},{64,80},{80,64},{96,112},{112,96},{1... | collective-permute-start | bytes 192008 | tf_op jit(solution)/shard_map/ppermute | solution.py:416
  7.1 14.4 %collective-permute-start.3 = (bf16[4,120,128]{2,1,0:T(8,128)(2,1)S(1)}, bf16[4,120,128]{2,1,0:T(8,128)(2,1)S(1)}, u32[]{:S(2)}, u32[]{:S(2)}) collective-permute-start(bf16[4,120,128]{2,1,0:T(8,128)(2,1)S(1)} %get-tuple-element.36.packet), channel_id=1, source_target_pairs={{1,2},{2,1},{3,4},{4,3},{5,6},{6,5},{7,8},{8,7},{9,10},{10,9},{11,... | collective-permute-start | bytes 368648 | tf_op jit(solution)/shard_map/ppermute | solution.py:421
  10.8 10.8 %collective-permute-start.4 = (bf16[4,120,128]{2,1,0:T(8,128)(2,1)S(1)}, bf16[4,120,128]{2,1,0:T(8,128)(2,1)S(1)}, u32[]{:S(2)}, u32[]{:S(2)}) collective-permute-start(bf16[4,120,128]{2,1,0:T(8,128)(2,1)S(1)} %get-tuple-element.36.packet), channel_id=1, source_target_pairs={{16,32},{32,16},{48,64},{64,48},{80,96},{96,80},{112,128},{128,112... | collective-permute-start | bytes 368648 | tf_op jit(solution)/shard_map/ppermute | solution.py:421
  21.6 4.1 %collective-permute-start.5 = (bf16[4,40,128]{2,1,0:T(8,128)(2,1)S(1)}, bf16[4,40,128]{2,1,0:T(8,128)(2,1)S(1)}, u32[]{:S(2)}, u32[]{:S(2)}) collective-permute-start(bf16[4,40,128]{2,1,0:T(8,128)(2,1)S(1)} %get-tuple-element.37.yfar), channel_id=1, source_target_pairs={{0,1},{1,0},{2,3},{3,2},{4,5},{5,4},{6,7},{7,6},{8,9},{9,8},{10,11... | collective-permute-start | bytes 122888 | tf_op jit(solution)/shard_map/ppermute | solution.py:416
  21.7 4.0 %collective-permute-start.6 = (bf16[4,40,128]{2,1,0:T(8,128)(2,1)S(1)}, bf16[4,40,128]{2,1,0:T(8,128)(2,1)S(1)}, u32[]{:S(2)}, u32[]{:S(2)}) collective-permute-start(bf16[4,40,128]{2,1,0:T(8,128)(2,1)S(1)} %get-tuple-element.38.xfar), channel_id=1, source_target_pairs={{0,16},{16,0},{32,48},{48,32},{64,80},{80,64},{96,112},{112,96},{1... | collective-permute-start | bytes 122888 | tf_op jit(solution)/shard_map/ppermute | solution.py:416
